TPU v7x, 32 devices: a 4x2x2 block of a 4x4x8 slice. The times are simulated.
32 devices in a mesh: data: 4 (over y, z), dap: 8 (over x, core).
Axes of the slice: x: 4, y: 2, z: 2, core: 2. Of those that a mesh axis runs over, the one named last changes fastest.
The devices are a block of a 4x4x8 slice.
Arguments:
- msa_act: bfloat16 [3072, 128, 64], P(('data', 'dap')), parts along dimension 0
- pair_act: bfloat16 [512, 128, 128], P(('data', 'dap')), parts along dimension 0
- msa_mask: int32 [3072, 128], P('data'), parts along dimension 0
- res_mask: int32 [512], P('data'), parts along dimension 0
- row_bias_w: bfloat16 [128, 8], replicated
- row_qkvg_w: bfloat16 [64, 4, 8, 8], replicated
- row_out_w: bfloat16 [8, 8, 64], replicated
- col_query_w: bfloat16 [64, 8, 8], replicated
- col_kv_w: bfloat16 [64, 2, 8], replicated
- col_gate_w: bfloat16 [64, 8, 8], replicated
- col_out_w: bfloat16 [8, 8, 64], replicated
- opm_proj_w: bfloat16 [64, 2, 32], replicated
- opm_out_w: bfloat16 [32, 32, 128], replicated
- start_bias_w: bfloat16 [128, 4], replicated
- start_qkvg_w: bfloat16 [128, 4, 4, 32], replicated
- start_out_w: bfloat16 [4, 32, 128], replicated
- end_bias_w: bfloat16 [128, 4], replicated
- end_qkvg_w: bfloat16 [128, 4, 4, 32], replicated
- end_out_w: bfloat16 [4, 32, 128], replicated
Outputs:
- output 1: bfloat16 [3072, 128, 64], P(('data', 'dap')), parts along dimension 0
- output 2: bfloat16 [512, 128, 128], P(('data', 'dap')), parts along dimension 0
There are 4 independent parts. A program takes and returns all parts, laid end to end along the dimension named above; an argument that names none is the same for every part.
All inputs are finite; a program needn't handle non-finite values.
Results may differ from a plain program's by a relative error of at most 0.0142.
Values are sent between devices in bfloat16 or wider.
A program may use at most 768 MiB of HBM per device.

v0:
```python
import jax
import jax.numpy as jnp
from jax import lax
from jax.sharding import PartitionSpec as P


def layer_norm(values):
    widened = values.astype(jnp.float32)
    mean_val = jnp.mean(widened, axis=-1, keepdims=True)
    centered = widened - mean_val
    variance = jnp.mean(centered * centered, axis=-1, keepdims=True)
    return (centered * lax.rsqrt(variance + 1e-5)).astype(jnp.bfloat16)


def mask_bias(mask_vals):
    return (mask_vals.astype(jnp.float32) - 1.0) * 1e4


def matmul_bf(einsum_form, left_arr, right_arr):
    return jnp.einsum(einsum_form, left_arr, right_arr, preferred_element_type=jnp.float32).astype(jnp.bfloat16)


def gated_out(einsum_form, gate_proj, attended, out_w):
    gated_vals = (jax.nn.sigmoid(gate_proj.astype(jnp.float32)) * attended).astype(jnp.bfloat16)
    return jnp.einsum(einsum_form, gated_vals, out_w, preferred_element_type=jnp.float32)


def row_attention(value_a7, bias_full, seq_mask, qkvg_w, out_w):
    projected = matmul_bf('sic,cahd->asihd', layer_norm(value_a7), qkvg_w)
    logits = jnp.einsum('sihd,sjhd->shij', projected[0], projected[1], preferred_element_type=jnp.float32) * (qkvg_w.shape[-1] ** -0.5) + bias_full[None] + mask_bias(seq_mask)[:, None, None, :]
    attn_probs = jax.nn.softmax(logits, axis=-1).astype(jnp.bfloat16)
    attended = jnp.einsum('shij,sjhd->sihd', attn_probs, projected[2], preferred_element_type=jnp.float32)
    return (value_a7 + gated_out('sihd,hdc->sic', projected[3], attended, out_w)).astype(jnp.bfloat16)


def column_attention(value_a7, col_mask, query_w, kv_w, gate_w, out_w):
    value_a6 = layer_norm(value_a7)
    mask_count = jnp.sum(col_mask, axis=0).astype(jnp.float32) + 1e-10
    mean_query = (jnp.einsum('sr,src->rc', col_mask.astype(jnp.bfloat16), value_a6, preferred_element_type=jnp.float32) / mask_count[:, None]).astype(jnp.bfloat16)
    query_proj = matmul_bf('rc,chd->rhd', mean_query, query_w)
    key_val = matmul_bf('src,cad->asrd', value_a6, kv_w)
    gate_proj = matmul_bf('src,chd->srhd', value_a6, gate_w)
    logits = jnp.einsum('rhd,srd->rhs', query_proj, key_val[0], preferred_element_type=jnp.float32) * (kv_w.shape[-1] ** -0.5) + mask_bias(col_mask).T[:, None, :]
    attn_probs = jax.nn.softmax(logits, axis=-1).astype(jnp.bfloat16)
    attended = jnp.einsum('rhs,srd->rhd', attn_probs, key_val[1], preferred_element_type=jnp.float32)
    return (value_a7 + gated_out('srhd,hdc->src', gate_proj, attended[None], out_w)).astype(jnp.bfloat16)


def outer_update(pair_act, left_proj, right_full, counts, out_w):
    outer_sum = matmul_bf('sie,sjf->ijef', left_proj, right_full)
    update = jnp.einsum('ijef,efc->ijc', outer_sum, out_w, preferred_element_type=jnp.float32) / (1e-3 + counts)[:, :, None]
    return (pair_act + update).astype(jnp.bfloat16)


def triangle_rows(pair_act, pair_ln, bias_full, res_mask, qkvg_w, out_w):
    projected = matmul_bf('ijc,cahd->aijhd', pair_ln, qkvg_w)
    logits = jnp.einsum('ijhd,ikhd->ihjk', projected[0], projected[1], preferred_element_type=jnp.float32) * (qkvg_w.shape[-1] ** -0.5) + bias_full[None] + mask_bias(res_mask)[None, None, None, :]
    attn_probs = jax.nn.softmax(logits, axis=-1).astype(jnp.bfloat16)
    attended = jnp.einsum('ihjk,ikhd->ijhd', attn_probs, projected[2], preferred_element_type=jnp.float32)
    return (pair_act + gated_out('ijhd,hdc->ijc', projected[3], attended, out_w)).astype(jnp.bfloat16)


def triangle_cols(pair_cols, pair_ln, bias_full, res_mask, qkvg_w, out_w):
    projected = matmul_bf('ijc,cahd->aijhd', pair_ln, qkvg_w)
    logits = jnp.einsum('ijhd,kjhd->jhik', projected[0], projected[1], preferred_element_type=jnp.float32) * (qkvg_w.shape[-1] ** -0.5) + bias_full[None] + mask_bias(res_mask)[None, None, None, :]
    attn_probs = jax.nn.softmax(logits, axis=-1).astype(jnp.bfloat16)
    attended = jnp.einsum('jhik,kjhd->ijhd', attn_probs, projected[2], preferred_element_type=jnp.float32)
    return (pair_cols + gated_out('ijhd,hdc->ijc', projected[3], attended, out_w)).astype(jnp.bfloat16)


def solution(mesh):
    def evoformer_block(value_a7, pair_act, array_b8, res_mask, row_bias_w, row_qkvg_w, row_out_w, col_query_w, col_kv_w, col_gate_w, col_out_w, opm_proj_w, opm_out_w, start_bias_w, start_qkvg_w, start_out_w, end_bias_w, end_qkvg_w, end_out_w):
        seq_local = value_a7.shape[0]
        res_local = pair_act.shape[0]
        dev_index = lax.axis_index('dap')
        seq_mask = lax.dynamic_slice_in_dim(array_b8, dev_index * seq_local, seq_local, axis=0)
        col_mask = lax.dynamic_slice_in_dim(array_b8, dev_index * res_local, res_local, axis=1)

        row_bias = matmul_bf('ijc,ch->hij', layer_norm(pair_act), row_bias_w)
        row_bias_full = lax.all_gather(row_bias, 'dap', axis=1, tiled=True)
        value_a7 = row_attention(value_a7, row_bias_full, seq_mask, row_qkvg_w, row_out_w)

        value_a8 = lax.all_to_all(value_a7, 'dap', 1, 0, tiled=True)
        value_a8 = column_attention(value_a8, col_mask, col_query_w, col_kv_w, col_gate_w, col_out_w)

        projected = matmul_bf('src,cae->asre', layer_norm(value_a8), opm_proj_w) * col_mask.astype(jnp.bfloat16)[None, :, :, None]
        right_full = lax.all_gather(projected[1], 'dap', axis=1, tiled=True)
        counts = jnp.einsum('si,sj->ij', col_mask.astype(jnp.bfloat16), array_b8.astype(jnp.bfloat16), preferred_element_type=jnp.float32)
        pair_act = outer_update(pair_act, projected[0], right_full, counts, opm_out_w)
        array_b7 = lax.all_to_all(value_a8, 'dap', 0, 1, tiled=True)

        pair_ln = layer_norm(pair_act)
        start_full = lax.all_gather(matmul_bf('ijc,ch->hij', pair_ln, start_bias_w), 'dap', axis=1, tiled=True)
        pair_act = triangle_rows(pair_act, pair_ln, start_full, res_mask, start_qkvg_w, start_out_w)

        pair_cols = lax.all_to_all(pair_act, 'dap', 1, 0, tiled=True)
        cols_ln = layer_norm(pair_cols)
        end_full = lax.all_gather(matmul_bf('ijc,ch->hji', cols_ln, end_bias_w), 'dap', axis=1, tiled=True)
        pair_cols = triangle_cols(pair_cols, cols_ln, end_full, res_mask, end_qkvg_w, end_out_w)
        pair_out = lax.all_to_all(pair_cols, 'dap', 0, 1, tiled=True)
        return array_b7, pair_out

    row_spec = P(('data', 'dap'), None, None)
    in_specs = (row_spec, row_spec, P('data', None), P('data')) + (P(),) * 15
    return jax.shard_map(evoformer_block, mesh=mesh, in_specs=in_specs, out_specs=(row_spec, row_spec), check_vma=False)
```

profile of v0, /device:TPU:81, one launch (start us, length us, event | category | flops | bytes accessed | tf_op | source)
XLA Modules:
  0.0 332.8 jit_solution(10926480646949895159)
XLA Ops:
  9.9 14.9 %all_gather.12 = bf16[8,128,128]{2,0,1:T(8,128)(2,1)S(1)} all-gather(bf16[8,16,128]{2,0,1:T(8,128)(2,1)S(1)} %fusion.76), channel_id=1, replica_groups=mesh['data'=4,'dap'=8] {'dap'}, dimensions={1}, use_global_device_ids=true | all-gather | bytes 294912 | tf_op jit(solution)/shard_map/all_gather | solution.py:80
  26.3 4.4 %convert_bitcast_fusion.1 = bf16[4,96,128,8,8]{2,4,3,0,1:T(8,128)(2,1)} fusion(bf16[96,128,64]{1,2,0:T(8,128)(2,1)S(1)} %copy-done.1, f32[96,128]{1,0:T(8,128)S(1)} %add_rsqrt_fusion.3, f32[96,128]{1,0:T(8,128)S(1)} %broadcast_multiply_fusion.3, bf16[64,4,8,8]{0,3,2,1:T(8,128)(2,1)S(1)} %copy-done.10), kind=kOutput, calls=%fused_computation.14 | convolution fusion | flops 408944640 | bytes 7995392 | tf_op jit(solution)/shard_map/sic,cahd->asihd/dot_general | solution.py:20
  30.7 25.3 %fusion.150 = (f32[96,8,128]{2,1,0:T(8,128)S(1)}, f32[96,8,128,128]{2,3,1,0:T(8,128)}) fusion(f32[96,128]{1,0:T(8,128)S(1)} %add_multiply_fusion, f32[8,128,128]{1,2,0:T(8,128)S(1)} %copy.133, bf16[4,96,128,8,8]{2,4,3,0,1:T(8,128)(2,1)} %convert_bitcast_fusion.1), kind=kOutput, calls=%fused_computation.211 | convolution fusion | flops 264241280 | bytes 54444032 | tf_op jit(solution)/shard_map/sub | solution.py:31
  56.0 19.7 %fusion.20 = bf16[96,128,64]{1,2,0:T(8,128)(2,1)} fusion(bf16[96,128,64]{1,2,0:T(8,128)(2,1)S(1)} %copy-done.1, f32[96,8,128,128]{2,3,1,0:T(8,128)} %get-tuple-element.15, f32[96,8,128]{2,1,0:T(8,128)S(1)} %get-tuple-element.14, bf16[4,96,128,8,8]{2,4,3,0,1:T(8,128)(2,1)} %convert_bitcast_fusion.1, bf16[8,8,64]{2,1,0:T(8,128)(2,1)S(1)} %copy-done.14), kind=kOutput, calls=%fused_computation.37 | convolution fusion | flops 334233600 | bytes 57024512 | tf_op jit(solution)/shard_map/sihd,hdc->sic/dot_general | solution.py:25
  75.7 4.3 %copy.135 = bf16[96,128,64]{0,2,1:T(8,128)(2,1)} copy(bf16[96,128,64]{1,2,0:T(8,128)(2,1)} %fusion.20) | data formatting | bytes 3145728 | tf_op jit(solution)/shard_map/convert_element_type | solution.py:33
  80.1 4.0 %all-to-all-start = ((bf16[96,128,64]{0,2,1:T(8,128)(2,1)}), bf16[96,128,64]{0,2,1:T(8,128)(2,1)S(1)}, u32[]{:S(2)}, u32[]{:S(2)}) async-start(bf16[96,128,64]{0,2,1:T(8,128)(2,1)} %copy.135), calls=%async_computation | async-start | bytes 4194304 | tf_op jit(solution)/shard_map/all_to_all | solution.py:83
  85.8 24.3 %all-to-all-done = bf16[96,128,64]{0,2,1:T(8,128)(2,1)S(1)} async-done(((bf16[96,128,64]{0,2,1:T(8,128)(2,1)}), bf16[96,128,64]{0,2,1:T(8,128)(2,1)S(1)}, u32[]{:S(2)}, u32[]{:S(2)}) %all-to-all-start) | async-done | bytes 1572896 | tf_op jit(solution)/shard_map/all_to_all | solution.py:83
  112.7 5.2 %copy.136 = f32[8,96,16,64]{1,0,3,2:T(8,128)} copy(f32[8,96,16,64]{1,3,2,0:T(8,128)S(1)} %convert_bitcast_fusion.2) | data formatting | bytes 6291456 | tf_op jit(solution)/shard_map/convert_element_type | solution.py:46
  117.9 3.8 %reshape.163 = f32[768,16,64]{0,2,1:T(8,128)S(1)} reshape(f32[8,96,16,64]{1,0,3,2:T(8,128)} %copy.136) | data formatting | bytes 6291456 | tf_op jit(solution)/shard_map/convert_element_type | solution.py:46
  126.4 2.2 fusion.113
  128.6 4.4 %convert_reduce_fusion.1 = (f32[768,16]{0,1:T(8,128)}, bf16[768,16,64]{0,2,1:T(8,128)(2,1)}) fusion(f32[768,16,64]{0,2,1:T(8,128)S(1)} %reshape.163, bf16[8,8,64]{2,1,0:T(8,128)(2,1)S(1)} %copy-done.16, f32[16,8,8]{1,2,0:T(8,128)} %fusion.113, bf16[64,8,8]{0,2,1:T(8,128)(2,1)} %param.28, f32[768,16]{0,1:T(8,128)S(1)} %rsqrt.57, f32[768,16]{0,1:T(8,128)S(1)} %div.108), kind=kOutput, calls=%fused_computation.28 | convolution fusion | flops 212324352 | bytes 4886528 | tf_op jit(solution)/shard_map/srhd,hdc->src/dot_general | solution.py:25
  135.7 2.1 multiply_bitcast_fusion
  139.0 39.6 %all-gather.3.cloned.1.call-done = bf16[1,768,128,32]{1,3,0,2:T(8,128)(2,1)} async-done(((bf16[1,768,16,32]{1,3,0,2:T(8,128)(2,1)}), bf16[1,768,128,32]{1,3,0,2:T(8,128)(2,1)}) %all-gather.3.cloned.1.call-update) | async-done | bytes 6291472 | tf_op jit(solution)/shard_map/all_gather | solution.py:87
  178.6 17.2 %convert_bitcast_fusion = bf16[16,128,32,32]{2,3,0,1:T(8,128)(2,1)} fusion(bf16[1,768,128,32]{1,3,0,2:T(8,128)(2,1)} %all-gather.3.cloned.1.call-done, bf16[2,768,16,32]{1,3,0,2:T(8,128)(2,1)S(1)} %multiply_bitcast_fusion), kind=kOutput, calls=%fused_computation.12 | convolution fusion | flops 3223322624 | bytes 11272192 | tf_op jit(solution)/shard_map/sie,sjf->ijef/dot_general | solution.py:20
  195.9 24.8 %copy.146 = bf16[16,128,32,32]{1,3,2,0:T(8,128)(2,1)} copy(bf16[16,128,32,32]{2,3,0,1:T(8,128)(2,1)} %convert_bitcast_fusion) | data formatting | bytes 8388608 | tf_op jit(solution)/shard_map/convert_element_type | solution.py:20
  220.6 3.0 convert_reduce_fusion.2
  224.1 13.3 %all_gather.14 = bf16[4,128,128]{2,0,1:T(4,128)(2,1)S(1)} all-gather(bf16[4,16,128]{2,0,1:T(4,128)(2,1)S(1)} %fusion.78), channel_id=1, replica_groups=mesh['data'=4,'dap'=8] {'dap'}, dimensions={1}, use_global_device_ids=true | all-gather | bytes 147456 | tf_op jit(solution)/shard_map/all_gather | solution.py:93
  239.1 3.3 fusion.156
  242.4 3.0 fusion.59
  246.6 4.2 %all-to-all-start.2 = ((bf16[16,128,128]{2,0,1:T(8,128)(2,1)}), bf16[16,128,128]{2,0,1:T(8,128)(2,1)}, u32[]{:S(2)}, u32[]{:S(2)}) async-start(bf16[16,128,128]{2,0,1:T(8,128)(2,1)} %copy.153), calls=%async_computation.2 | async-start | bytes 1048576 | tf_op jit(solution)/shard_map/all_to_all | solution.py:96
  250.8 4.0 %copy.144 = bf16[768,16,64]{2,1,0:T(8,128)(2,1)S(1)} copy(bf16[768,16,64]{0,2,1:T(8,128)(2,1)} %get-tuple-element.17) | data formatting | bytes 3145728 | tf_op jit(solution)/shard_map/convert_element_type | solution.py:46
  254.9 4.5 %reshape.204 = bf16[8,2,49152]{2,1,0:T(2,128)(2,1)} reshape(bf16[768,16,64]{2,1,0:T(8,128)(2,1)S(1)} %copy.144) | data formatting | bytes 3145728
  260.2 4.6 %all-to-all-start.1 = ((bf16[8,2,49152]{2,1,0:T(2,128)(2,1)}), bf16[8,2,49152]{2,1,0:T(2,128)(2,1)S(1)}, u32[]{:S(2)}, u32[]{:S(2)}) async-start(bf16[8,2,49152]{2,1,0:T(2,128)(2,1)} %reshape.204), calls=%async_computation.1 | async-start | bytes 3145728 | tf_op jit(solution)/shard_map/all_to_all | solution.py:90
  264.8 2.2 fusion.149
  272.9 2.7 fusion.100
  275.9 17.4 %all_gather.15 = bf16[4,128,128]{2,0,1:T(4,128)(2,1)S(1)} all-gather(bf16[4,16,128]{2,0,1:T(4,128)(2,1)S(1)} %fusion.79), channel_id=1, replica_groups=mesh['data'=4,'dap'=8] {'dap'}, dimensions={1}, use_global_device_ids=true | all-gather | bytes 147456 | tf_op jit(solution)/shard_map/all_gather | solution.py:98
  293.5 7.0 %fusion.157 = (f32[16,4,128]{2,1,0:T(4,128)S(1)}, f32[16,4,128,128]{2,3,1,0:T(8,128)}) fusion(f32[16,4,128,128]{2,3,1,0:T(8,128)} %fusion.100, f32[4,128,128]{1,2,0:T(8,128)S(1)} %copy.159, f32[128]{0:T(128)S(1)} %add_multiply_fusion.1), kind=kOutput, calls=%fused_computation.214 | output fusion | flops 8388735 | bytes 8684032 | tf_op jit(solution)/shard_map/sub | solution.py:66
  300.5 3.4 %fusion.60 = bf16[128,16,128]{2,0,1:T(8,128)(2,1)S(1)} fusion(f32[128,16,128]{2,0,1:T(8,128)S(1)} %bitcast.310, f32[16,4,128,128]{2,3,1,0:T(8,128)} %get-tuple-element.23, f32[16,4,128]{2,1,0:T(4,128)S(1)} %get-tuple-element.22, bf16[4,128,16,4,32]{1,4,3,0,2:T(8,128)(2,1)} %copy-done.3, bf16[4,32,128]{2,1,0:T(8,128)(2,1)S(1)} %copy-done.13), kind=kOutput, calls=%fused_computation.92 | convolution fusion | flops 138412032 | bytes 6881280 | tf_op jit(solution)/shard_map/ijhd,hdc->ijc/dot_general | solution.py:25
  306.1 4.2 %all-to-all-start.3 = ((bf16[128,16,128]{2,1,0:T(8,128)(2,1)}), bf16[128,16,128]{2,1,0:T(8,128)(2,1)}, u32[]{:S(2)}, u32[]{:S(2)}) async-start(bf16[128,16,128]{2,1,0:T(8,128)(2,1)} %copy.161), calls=%async_computation.3 | async-start | bytes 1048576 | tf_op jit(solution)/shard_map/all_to_all | solution.py:100
  310.3 5.2 %reshape.205 = bf16[768,16,64]{2,1,0:T(8,128)(2,1)S(1)} reshape(bf16[8,2,49152]{2,1,0:T(2,128)(2,1)} %copy-done.2) | data formatting | bytes 3145728
  315.6 3.6 %copy.145 = bf16[8,96,16,64]{1,3,2,0:T(8,128)(2,1)} copy(bf16[8,96,16,64]{3,2,1,0:T(8,128)(2,1)S(1)} %bitcast.306) | data formatting | bytes 3145728 | tf_op jit(solution)/shard_map/all_to_all | solution.py:90
  319.2 4.4 %copy.163 = bf16[96,128,64]{1,2,0:T(8,128)(2,1)} copy(bf16[96,128,64]{0,2,1:T(8,128)(2,1)} %bitcast.307) | data formatting | bytes 3145728
  (108 shorter events, 31.4 us)
Async XLA Ops:
  7.2 213.4 %copy-start = (bf16[32,32,128]{2,1,0:T(8,128)(2,1)S(1)}, bf16[32,32,128]{2,1,0:T(8,128)(2,1)}, u32[]{:S(2)}) copy-start(bf16[32,32,128]{2,1,0:T(8,128)(2,1)} %param.31) | copy-start | bytes 786436
  7.2 17.8 %copy-start.1 = (bf16[96,128,64]{1,2,0:T(8,128)(2,1)S(1)}, bf16[96,128,64]{1,2,0:T(8,128)(2,1)}, u32[]{:S(2)}) copy-start(bf16[96,128,64]{1,2,0:T(8,128)(2,1)} %param.19) | copy-start | bytes 4718596
  8.7 17.6 %copy-start.4 = (bf16[16,128,128]{1,2,0:T(8,128)(2,1)}, bf16[16,128,128]{1,2,0:T(8,128)(2,1)S(1)}, u32[]{:S(2)}) copy-start(bf16[16,128,128]{1,2,0:T(8,128)(2,1)S(1)} %copy.131) | copy-start | bytes 1572868
  8.8 17.5 %copy-start.6 = (s32[768,128]{1,0:T(8,128)S(1)}, s32[768,128]{1,0:T(8,128)}, u32[]{:S(2)}) copy-start(s32[768,128]{1,0:T(8,128)} %param.21) | copy-start | bytes 1179652
  25.0 1.3 copy-start.10
  30.7 25.3 %copy-start.14 = (bf16[8,8,64]{2,1,0:T(8,128)(2,1)S(1)}, bf16[8,8,64]{2,1,0:T(8,128)(2,1)}, u32[]{:S(2)}) copy-start(bf16[8,8,64]{2,1,0:T(8,128)(2,1)} %param.25) | copy-start | bytes 24580
  80.1 30.0 %all-to-all-start = ((bf16[96,128,64]{0,2,1:T(8,128)(2,1)}), bf16[96,128,64]{0,2,1:T(8,128)(2,1)S(1)}, u32[]{:S(2)}, u32[]{:S(2)}) async-start(bf16[96,128,64]{0,2,1:T(8,128)(2,1)} %copy.135), calls=%async_computation | async-start | bytes 4194304 | tf_op jit(solution)/shard_map/all_to_all | solution.py:83
  84.1 94.6 %all-gather.3.cloned.1.call-start = ((), (), s32[]{:S(2)}) async-start(), calls=%async_computation.4 | async-start | bytes 7077888 | tf_op jit(solution)/shard_map/all_gather | solution.py:87
  121.7 0.7 copy-start.15
  121.7 0.7 copy-start.19
  123.3 5.3 %copy-start.16 = (bf16[8,8,64]{2,1,0:T(8,128)(2,1)S(1)}, bf16[8,8,64]{2,1,0:T(8,128)(2,1)}, u32[]{:S(2)}) copy-start(bf16[8,8,64]{2,1,0:T(8,128)(2,1)} %param.29) | copy-start | bytes 24580
  135.7 3.1 copy-start.18
  135.7 3.1 copy-start.7
  195.9 24.8 %copy-start.5 = (bf16[16,128,128]{1,2,0:T(8,128)(2,1)S(1)}, bf16[16,128,128]{1,2,0:T(8,128)(2,1)}, u32[]{:S(2)}) copy-start(bf16[16,128,128]{1,2,0:T(8,128)(2,1)} %copy-done.4) | copy-start | bytes 1572868
  220.6 3.3 copy-start.17
  220.6 17.0 %copy-start.8 = (bf16[128,4,4,32]{0,3,2,1:T(8,128)(2,1)S(1)}, bf16[128,4,4,32]{0,3,2,1:T(8,128)(2,1)}, u32[]{:S(2)}) copy-start(bf16[128,4,4,32]{0,3,2,1:T(8,128)(2,1)} %param.33) | copy-start | bytes 393220
  239.1 3.3 copy-start.12
  246.6 13.5 %all-to-all-start.2 = ((bf16[16,128,128]{2,0,1:T(8,128)(2,1)}), bf16[16,128,128]{2,0,1:T(8,128)(2,1)}, u32[]{:S(2)}, u32[]{:S(2)}) async-start(bf16[16,128,128]{2,0,1:T(8,128)(2,1)} %copy.153), calls=%async_computation.2 | async-start | bytes 1048576 | tf_op jit(solution)/shard_map/all_to_all | solution.py:96
  260.2 44.8 %all-to-all-start.1 = ((bf16[8,2,49152]{2,1,0:T(2,128)(2,1)}), bf16[8,2,49152]{2,1,0:T(2,128)(2,1)S(1)}, u32[]{:S(2)}, u32[]{:S(2)}) async-start(bf16[8,2,49152]{2,1,0:T(2,128)(2,1)} %reshape.204), calls=%async_computation.1 | async-start | bytes 3145728 | tf_op jit(solution)/shard_map/all_to_all | solution.py:90
  267.0 3.9 %copy-start.9 = (bf16[128,4,4,32]{0,3,2,1:T(8,128)(2,1)S(1)}, bf16[128,4,4,32]{0,3,2,1:T(8,128)(2,1)}, u32[]{:S(2)}) copy-start(bf16[128,4,4,32]{0,3,2,1:T(8,128)(2,1)} %param.36) | copy-start | bytes 393220
  271.6 1.4 copy-start.3
  272.9 2.7 copy-start.11
  293.5 7.0 %copy-start.13 = (bf16[4,32,128]{2,1,0:T(8,128)(2,1)S(1)}, bf16[4,32,128]{2,1,0:T(8,128)(2,1)}, u32[]{:S(2)}) copy-start(bf16[4,32,128]{2,1,0:T(8,128)(2,1)} %param.37) | copy-start | bytes 98308
  305.0 1.1 copy-start.2
  306.1 17.4 %all-to-all-start.3 = ((bf16[128,16,128]{2,1,0:T(8,128)(2,1)}), bf16[128,16,128]{2,1,0:T(8,128)(2,1)}, u32[]{:S(2)}, u32[]{:S(2)}) async-start(bf16[128,16,128]{2,1,0:T(8,128)(2,1)} %copy.161), calls=%async_computation.3 | async-start | bytes 1048576 | tf_op jit(solution)/shard_map/all_to_all | solution.py:100
Sparse Core Ops, SparseCore 0:
  138.9 39.6 all-gather.2
where the time goes:
time: 338 us; the launch traced here: 333 us
  matrix products  95 us (28%)
  local copies, waits for them, and re-layouts  72.9 us (22%)
  waiting for transfers between devices  64.8 us (19%)
  blocking collectives  45.6 us (13%)
  other arithmetic  22.2 us (7%)
  starting transfers between devices  17.1 us (5%)
  between operations  15.1 us (4%)
    all_gather x1, waiting for transfers between devices, evoformer_block(): right_full = lax.all_gather(projected[1], 'dap', axis=1, tiled=True)  39.6 us
    dot_general x4, matrix products, gated_out(): jnp.einsum(einsum_form, gated_vals, out_w, preferred_element_type=jnp.flo...  30.5 us
    dot_general x9, matrix products, matmul_bf(): jnp.einsum(einsum_form, left_arr, right_arr, preferred_element_type=jnp.f...  28.4 us
    convert_element_type x2, local copies, waits for them, and re-layouts, matmul_bf(): jnp.einsum(einsum_form, left_arr, right_arr, preferred_element_type=jnp.f...  25.5 us
    sub x1, matrix products, row_attention(): attn_probs = jax.nn.softmax(logits, axis=-1).astype(jnp.bfloat16)  25.3 us
    all_to_all x1, waiting for transfers between devices, evoformer_block(): value_a8 = lax.all_to_all(value_a7, 'dap', 1, 0, tiled=True)  24.3 us
    unnamed x45, local copies, waits for them, and re-layouts  18.5 us
    all_gather x1, blocking collectives, evoformer_block(): lax.all_gather(matmul_bf('ijc,ch->hji', cols_ln, end_bias_w), 'dap', axis...  17.4 us
  transfers between devices with their start and end apart: 5, of which 3 were waited for; matrix products, arithmetic and copies ran while one was open for 13% of the time, Pallas kernels for 0%

commit v1 on v0

v1 whole, which is shorter than its diff:
```python
import functools
import math

import jax
import jax.numpy as jnp
import numpy as np
from jax import lax
from jax.experimental import pallas as pl
from jax.experimental.pallas import tpu as pltpu
from jax.sharding import PartitionSpec as P

BF = jnp.bfloat16
F32 = jnp.float32
MESH = pl.DeviceIdType.MESH
LOG2E = math.log2(math.e)
VM = pl.BlockSpec(memory_space=pltpu.VMEM)


def dot(a, b):
    return lax.dot_general(a, b, (((1,), (0,)), ((), ())), preferred_element_type=F32)


def dot_nt(a, b):
    return lax.dot_general(a, b, (((1,), (1,)), ((), ())), preferred_element_type=F32)


def rnd(v):
    return v.astype(BF).astype(F32)


def norm(v, axis):
    mean = jnp.mean(v, axis=axis, keepdims=True)
    cen = v - mean
    var = jnp.mean(cen * cen, axis=axis, keepdims=True)
    return (cen * lax.rsqrt(var + 1e-5)).astype(BF)


def sigmoid(v):
    return 1.0 / (1.0 + jnp.exp(-v))


def split3(value):
    hi = float(np.asarray(value).astype(BF))
    mid = float(np.asarray(value - hi).astype(BF))
    return hi, mid, float(np.asarray(value - hi - mid).astype(BF))


def peer_barrier(me, n):
    sem = pltpu.get_barrier_semaphore()
    for d in range(1, n):
        pl.semaphore_signal(sem, inc=1, device_id={"dap": lax.rem(me + d, n)}, device_id_type=MESH)
    pl.semaphore_wait(sem, n - 1)


def rcopy(src, dst, ssem, rsem, dev):
    return pltpu.make_async_remote_copy(src_ref=src, dst_ref=dst, send_sem=ssem, recv_sem=rsem, device_id={"dap": dev}, device_id_type=MESH)


def ds8(start, size, unit=8):
    return pl.ds(pl.multiple_of(start, unit), size)


def msa_kernel(n, mask_ref, m_ref, z_ref, wb_ref, wqkvg_ref, wo_ref, wq2_ref, wkv_ref,
               m1_ref, x2_ref, o2_ref,
               ball, bias, brow, kv, lg, wot, qpart, ppart, tmp,
               ssem_b, rsem_b, ssem_q, rsem_q, ssem_p, rsem_p):
    me = lax.axis_index("dap")
    nseq, chan, nres = m_ref.shape
    rows = z_ref.shape[0]
    heads = wb_ref.shape[0]
    hd = chan // heads
    scale = hd ** -0.5
    base = me * nseq
    peer_barrier(me, n)

    pitch = rows + 8

    def bias_row(i, c):
        b = dot_nt(wb_ref[...], norm(z_ref[i].astype(F32), 1))
        brow[pl.ds(i, heads, stride=pitch), :] = b
        return c
    lax.fori_loop(0, rows, bias_row, 0, unroll=4)
    mine = ds8(me * rows, rows, 16)
    for h in range(heads):
        ball[h, mine, :] = brow[h * pitch:h * pitch + rows, :].astype(BF)
    sends = []
    for d in range(1, n):
        cp = rcopy(ball.at[:, mine, :], ball.at[:, mine, :], ssem_b.at[d], rsem_b.at[d], lax.rem(me + d, n))
        cp.start()
        sends.append(cp)
    wot[...] = wo_ref[...].astype(F32).T.astype(BF)
    qpart[me] = jnp.zeros((chan, nres), F32)
    for d in range(1, n):
        src = ds8(lax.rem(me + n - d, n) * rows, rows, 16)
        rcopy(ball.at[:, src, :], ball.at[:, src, :], ssem_b.at[d], rsem_b.at[d], me).wait_recv()
    for h in range(heads):
        bias[:, h * nres:(h + 1) * nres] = ball[h].astype(F32).T * LOG2E

    hi, mid, lo = split3(1e4 / scale)
    rid = lax.broadcasted_iota(jnp.int32, (16, 2 * nres), 0)
    lid = lax.broadcasted_iota(jnp.int32, (16, 2 * nres), 1)
    aug = jnp.where(rid == 0, hi, jnp.where(rid == 1, mid, jnp.where(rid == 2, lo, 0.0))).astype(BF)
    diag = (rid < 8) == (lid < nres)

    def row_pair(t, carry):
        s0 = t * 2
        mv = jnp.concatenate([m_ref[s0].astype(F32), m_ref[s0 + 1].astype(F32)], axis=1)
        xt = norm(mv, 0)
        proj = dot(wqkvg_ref[...], xt)
        outs = []
        for s in range(2):
            sl = slice(s * nres, (s + 1) * nres)
            mk = mask_ref[pl.ds(base + s0 + s, 1), :].astype(F32) - 1.0
            kaug = jnp.concatenate([proj[chan:2 * chan, sl], jnp.broadcast_to(mk, (16, nres))], axis=0)
            lhs = kaug.T.astype(BF)
            vt = proj[2 * chan:3 * chan, sl].astype(BF)
            for p in range(heads // 2):
                q16 = proj[16 * p:16 * p + 16, sl]
                blk = jnp.where(diag, jnp.concatenate([q16, q16], axis=1), 0.0).astype(BF)
                parts = []
                if p > 0:
                    parts.append(jnp.zeros((16 * p, 2 * nres), BF))
                parts.append(blk)
                if chan - 16 * p - 16 > 0:
                    parts.append(jnp.zeros((chan - 16 * p - 16, 2 * nres), BF))
                parts.append(aug)
                l = dot(lhs, jnp.concatenate(parts, axis=0)) * (scale * LOG2E) + bias[:, 256 * p:256 * p + 256]
                e = jnp.exp2(l - jnp.max(l, axis=0, keepdims=True))
                r = 1.0 / jnp.sum(e, axis=0, keepdims=True)
                o = dot(vt[16 * p:16 * p + 16, :], e.astype(BF))
                outs.append((o[0:8, 0:nres] * r[:, 0:nres], o[8:16, nres:] * r[:, nres:]))
        half = heads // 2
        ot = jnp.concatenate(
            [jnp.concatenate([v for pr in outs[s * half:(s + 1) * half] for v in pr], axis=0) for s in range(2)], axis=1)
        y = (sigmoid(rnd(proj[3 * chan:4 * chan, :])) * ot).astype(BF)
        m1 = (mv + dot(wot[...], y)).astype(BF)
        x2 = norm(m1.astype(F32), 0)
        kvp = rnd(dot(wkv_ref[...], x2))
        acc = qpart[me]
        for s in range(2):
            sl = slice(s * nres, (s + 1) * nres)
            m1_ref[s0 + s] = m1[:, sl]
            x2_ref[s0 + s] = x2[:, sl]
            kv[s0 + s] = kvp[:, sl]
            acc = acc + mask_ref[pl.ds(base + s0 + s, 1), :].astype(F32) * x2[:, sl].astype(F32)
        qpart[me] = acc
        return carry
    lax.fori_loop(0, nseq // 2, row_pair, 0)

    for d in range(1, n):
        cp = rcopy(qpart.at[me], qpart.at[me], ssem_q.at[d], rsem_q.at[d], lax.rem(me + d, n))
        cp.start()
        sends.append(cp)
    count = jnp.sum(mask_ref[...].astype(F32), axis=0, keepdims=True) + 1e-10
    for d in range(1, n):
        src = lax.rem(me + n - d, n)
        rcopy(qpart.at[src], qpart.at[src], ssem_q.at[d], rsem_q.at[d], me).wait_recv()
    tot = qpart[0]
    for d in range(1, n):
        tot = tot + qpart[d]
    tmp[...] = rnd(dot(wq2_ref[...], (tot / count).astype(BF)))
    qd = [tmp[pl.ds(d, heads, stride=hd), :] for d in range(hd)]
    unroll = 8

    def logit(t, mx):
        for u in range(unroll):
            s = t * unroll + u
            row = kv.at[s]
            l = qd[0] * row[0:1, :]
            for d in range(1, hd):
                l = l + qd[d] * row[d:d + 1, :]
            l = l * scale + (mask_ref[pl.ds(base + s, 1), :].astype(F32) - 1.0) * 1e4
            lg[s] = l
            mx = jnp.maximum(mx, l)
        return mx
    mx = lax.fori_loop(0, nseq // unroll, logit, jnp.full((heads, nres), -jnp.inf, F32))

    def weigh(t, carry):
        ssum, acc = carry
        acc = list(acc)
        for u in range(unroll):
            s = t * unroll + u
            row = kv.at[s]
            e = jnp.exp(lg[s] - mx)
            ssum = ssum + e
            eb = rnd(e)
            for d in range(hd):
                acc[d] = acc[d] + eb * row[hd + d:hd + d + 1, :]
        return ssum, tuple(acc)
    zero = jnp.zeros((heads, nres), F32)
    ssum, acc = lax.fori_loop(0, nseq // unroll, weigh, (zero, (zero,) * hd))
    ppart[me, 0:8, :] = mx
    ppart[me, 8:16, :] = ssum
    for d in range(hd):
        ppart[me, 16 + 8 * d:24 + 8 * d, :] = acc[d]
    for d in range(1, n):
        cp = rcopy(ppart.at[me], ppart.at[me], ssem_p.at[d], rsem_p.at[d], lax.rem(me + d, n))
        cp.start()
        sends.append(cp)
    for d in range(1, n):
        src = lax.rem(me + n - d, n)
        rcopy(ppart.at[src], ppart.at[src], ssem_p.at[d], rsem_p.at[d], me).wait_recv()
    top = ppart[0, 0:8, :]
    for d in range(1, n):
        top = jnp.maximum(top, ppart[d, 0:8, :])
    fac = [jnp.exp(ppart[d, 0:8, :] - top) for d in range(n)]
    den = fac[0] * ppart[0, 8:16, :]
    for d in range(1, n):
        den = den + fac[d] * ppart[d, 8:16, :]
    inv = 1.0 / den
    for c in range(hd):
        o = fac[0] * ppart[0, 16 + 8 * c:24 + 8 * c, :]
        for d in range(1, n):
            o = o + fac[d] * ppart[d, 16 + 8 * c:24 + 8 * c, :]
        o2_ref[pl.ds(c, heads, stride=hd), :] = o * inv
    for cp in sends:
        cp.wait_send()


def msa_call(n, mask, mt, z, wb, wqkvg, wo, wq2, wkv):
    nseq, chan, nres = mt.shape
    rows = z.shape[0]
    heads = wb.shape[0]
    dma = pltpu.SemaphoreType.DMA((n,))
    return pl.pallas_call(
        functools.partial(msa_kernel, n),
        name="msa",
        out_shape=[jax.ShapeDtypeStruct((nseq, chan, nres), BF), jax.ShapeDtypeStruct((nseq, chan, nres), BF),
                   jax.ShapeDtypeStruct((chan, nres), F32)],
        in_specs=[VM] * 8,
        out_specs=[VM] * 3,
        scratch_shapes=[
            pltpu.VMEM((heads, n * rows, nres), BF),
            pltpu.VMEM((nres, heads * nres), F32),
            pltpu.VMEM((heads * (rows + 8), nres), F32),
            pltpu.VMEM((nseq, wkv.shape[0], nres), F32),
            pltpu.VMEM((nseq, heads, nres), F32),
            pltpu.VMEM((chan, chan), BF),
            pltpu.VMEM((n, chan, nres), F32),
            pltpu.VMEM((n, chan + 16, nres), F32),
            pltpu.VMEM((chan, nres), F32),
            dma, dma, dma, dma, dma, dma,
        ],
        compiler_params=pltpu.CompilerParams(collective_id=0, has_side_effects=True),
    )(mask, mt, z, wb, wqkvg, wo, wq2, wkv)


def gate_kernel(mask_ref, m1_ref, x2_ref, o2_ref, wg_ref, wo_ref, wopm_ref, m2_ref, a_ref, c_ref, ac, at, wot):
    nseq, chan, nres = m1_ref.shape
    ne = chan // 2
    pitch = chan + 8
    wot[...] = wo_ref[...].astype(F32).T.astype(BF)
    o2 = jnp.concatenate([o2_ref[...]] * 2, axis=1)

    def pair(t, carry):
        s0 = t * 2
        xv = jnp.concatenate([x2_ref[s0], x2_ref[s0 + 1]], axis=1)
        y = (sigmoid(rnd(dot(wg_ref[...], xv))) * o2).astype(BF)
        m1 = jnp.concatenate([m1_ref[s0].astype(F32), m1_ref[s0 + 1].astype(F32)], axis=1)
        m2 = (m1 + dot(wot[...], y)).astype(BF)
        pr = rnd(dot(wopm_ref[...], norm(m2.astype(F32), 0)))
        for s in range(2):
            sl = slice(s * nres, (s + 1) * nres)
            m2_ref[s0 + s] = m2[:, sl]
            ac[ds8((s0 + s) * pitch, chan), :] = pr[:, sl] * mask_ref[pl.ds(s0 + s, 1), :].astype(F32)
        return carry
    lax.fori_loop(0, nseq // 2, pair, 0, unroll=2)

    pitch2 = ne + 8
    pad = jnp.zeros((nres - nseq, nres), F32)

    def plane(e, carry):
        a = jnp.concatenate([ac[pl.ds(e, nseq, stride=pitch), :], pad], axis=0)
        at[pl.ds(e, nres, stride=pitch2), :] = a.T
        c_ref[e] = ac[pl.ds(ne + e, nseq, stride=pitch), :].astype(BF)
        return carry
    lax.fori_loop(0, ne, plane, 0, unroll=2)

    def row(i, carry):
        a_ref[ds8(i * ne, ne, 32), :] = at[ds8(i * pitch2, ne), :].astype(BF)
        return carry
    lax.fori_loop(0, nres, row, 0, unroll=4)


def gate_call(mask, m1, x2, o2, wg, wo, wopm):
    nseq, chan, nres = m1.shape
    ne = chan // 2
    return pl.pallas_call(
        gate_kernel,
        name="gate",
        out_shape=[jax.ShapeDtypeStruct((nseq, chan, nres), BF), jax.ShapeDtypeStruct((nres * ne, nres), BF),
                   jax.ShapeDtypeStruct((ne, nseq, nres), BF)],
        in_specs=[VM] * 7,
        out_specs=[VM] * 3,
        scratch_shapes=[
            pltpu.VMEM((nseq * (chan + 8), nres), F32),
            pltpu.VMEM((nres * (ne + 8), nres), F32),
            pltpu.VMEM((chan, chan), BF),
        ],
    )(mask, m1, x2, o2, wg, wo, wopm)


def tri_attend(n, me, zin, wb_ref, wqkvg_ref, wo_ref, maskcol, zln, brow, ball, bias, proj, flat, wot, tsend, zrecv,
               ssem_b, rsem_b, ssem_t, rsem_t):
    rows, nres, chan = zin.shape
    heads = wb_ref.shape[0]
    hd = chan // heads
    scale = hd ** -0.5
    pitch = rows + 8
    mine = ds8(me * rows, rows, 16)
    sends = []

    def bias_row(i, c):
        zl = norm(zin[i].astype(F32), 1)
        zln[i] = zl
        brow[pl.ds(i, heads, stride=pitch), :] = dot_nt(wb_ref[...], zl)
        return c
    lax.fori_loop(0, rows, bias_row, 0, unroll=4)
    for h in range(heads):
        ball[h, mine, :] = brow[h * pitch:h * pitch + rows, :].astype(BF)
    for d in range(1, n):
        cp = rcopy(ball.at[:, mine, :], ball.at[:, mine, :], ssem_b.at[d], rsem_b.at[d], lax.rem(me + d, n))
        cp.start()
        sends.append(cp)
    wot[...] = wo_ref[...].astype(F32).T.astype(BF)

    def project(i, c):
        zl = zln[i]
        proj[i, 0:chan, :] = dot_nt(wqkvg_ref[0:chan, :], zl).astype(BF)
        proj[i, chan:2 * chan, :] = dot_nt(zl, wqkvg_ref[chan:2 * chan, :]).astype(BF)
        proj[i, 2 * chan:4 * chan, :] = dot_nt(wqkvg_ref[2 * chan:4 * chan, :], zl).astype(BF)
        return c
    lax.fori_loop(0, rows, project, 0, unroll=2)
    for d in range(1, n):
        src = ds8(lax.rem(me + n - d, n) * rows, rows, 16)
        rcopy(ball.at[:, src, :], ball.at[:, src, :], ssem_b.at[d], rsem_b.at[d], me).wait_recv()
    for h in range(heads):
        bias[:, h * nres:(h + 1) * nres] = (ball[h].astype(F32).T + maskcol[...]) * LOG2E
    zero = jnp.zeros((hd, nres), BF)

    def attend(i, c):
        kmat = proj[i, chan:2 * chan, :]
        outs = []
        for p in range(heads // 2):
            r0 = 2 * hd * p
            qa = proj[i, r0:r0 + hd, :]
            qb = proj[i, r0 + hd:r0 + 2 * hd, :]
            blk = jnp.concatenate([jnp.concatenate([qa, zero], axis=1), jnp.concatenate([zero, qb], axis=1)], axis=0)
            parts = []
            if p > 0:
                parts.append(jnp.zeros((r0, 2 * nres), BF))
            parts.append(blk)
            if chan - r0 - 2 * hd > 0:
                parts.append(jnp.zeros((chan - r0 - 2 * hd, 2 * nres), BF))
            l = dot(kmat, jnp.concatenate(parts, axis=0)) * (scale * LOG2E) + bias[:, 256 * p:256 * p + 256]
            e = jnp.exp2(l - jnp.max(l, axis=0, keepdims=True))
            r = 1.0 / jnp.sum(e, axis=0, keepdims=True)
            o = dot(proj[i, 2 * chan + r0:2 * chan + r0 + 2 * hd, :], e.astype(BF))
            outs.append(o[0:hd, 0:nres] * r[:, 0:nres])
            outs.append(o[hd:, nres:] * r[:, nres:])
        y = (sigmoid(proj[i, 3 * chan:4 * chan, :].astype(F32)) * jnp.concatenate(outs, axis=0)).astype(BF)
        upd = dot(wot[...], y).T
        flat[pl.ds(i, nres, stride=pitch), :] = zin[i].astype(F32) + upd
        return c
    lax.fori_loop(0, rows, attend, 0, unroll=2)

    def regroup(j, c):
        tsend[j] = flat[ds8(j * pitch, rows), :].astype(BF)
        return c
    lax.fori_loop(0, nres, regroup, 0, unroll=4)
    for d in range(1, n):
        dst = lax.rem(me + d, n)
        cp = rcopy(tsend.at[pl.ds(dst * rows, rows)], zrecv.at[:, mine, :], ssem_t.at[d], rsem_t.at[d], dst)
        cp.start()
        sends.append(cp)
    zrecv[:, mine, :] = tsend[pl.ds(me * rows, rows)]
    for d in range(1, n):
        src = ds8(lax.rem(me + n - d, n) * rows, rows, 16)
        rcopy(zrecv.at[:, src, :], zrecv.at[:, src, :], ssem_t.at[d], rsem_t.at[d], me).wait_recv()
    return sends


def pair_kernel(n, nchunk, a_ref, c_ref, z_ref, cnt_ref, rm_ref, wopm_ref, wb1_ref, wqkvg1_ref, wo1_ref, wb2_ref, wqkvg2_ref, wo2_ref,
                zo_ref,
                call, aall, upd, osc, z1, zln, brow, ball1, ball2, bias, proj, flat, wot, maskcol, tsend1, tsend2, zmid, zfin,
                ssem_a, rsem_a, ssem_c, rsem_c, ssem_b1, rsem_b1, ssem_t1, rsem_t1, ssem_b2, rsem_b2, ssem_t2, rsem_t2):
    me = lax.axis_index("dap")
    nf, nseq, nres = c_ref.shape
    rows, _, chan = z_ref.shape
    ne = a_ref.shape[0] // nres
    fq = nf // nchunk
    nx = n // 2
    x, k = lax.div(me, 2), lax.rem(me, 2)
    partner = x * 2 + 1 - k
    right = lax.rem(x + 1, nx) * 2 + k
    left = lax.rem(x + nx - 1, nx) * 2 + k
    far = lax.rem(x + 2, nx) * 2 + k
    mine = me
    peer_barrier(me, n)
    arows = rows * ne
    sends = []

    def go(src, dst, ssem, rsem, dev):
        cp = rcopy(src, dst, ssem, rsem, dev)
        cp.start()
        sends.append(cp)

    def other(dev):
        return dev + 1 - 2 * k

    def blk(q, dev, lo=0, size=None):
        size = fq if size is None else size
        return call.at[pl.ds(q * fq + lo, size), dev, 0:nseq, :]

    def own(q):
        src = c_ref.at[pl.ds(q * fq, fq)]
        go(src, blk(q, me), ssem_c.at[q, 0], rsem_c.at[q, 0], right)
        go(src, blk(q, me), ssem_c.at[q, 1], rsem_c.at[q, 1], left)
        go(src, blk(q, me), ssem_c.at[q, 2], rsem_c.at[q, 2], partner)

    def got(q, kind, dev, lo=0, size=None):
        b = blk(q, dev, lo, size)
        rcopy(b, b, ssem_c.at[q, kind], rsem_c.at[q, kind], me).wait_recv()

    def relay(q, kind, dev, to, lo=0, size=None):
        b = blk(q, dev, lo, size)
        go(b, b, ssem_c.at[q, kind], rsem_c.at[q, kind], to)

    for d in range(1, n):
        dst = lax.rem(me + d, n)
        go(a_ref.at[pl.ds(dst * arows, arows), :], aall.at[me], ssem_a.at[d], rsem_a.at[d], dst)
    own(0)
    own(1)
    aall[me] = a_ref[ds8(me * arows, arows, 32), :]
    padz = jnp.zeros((call.shape[1], call.shape[2] - nseq, nres), BF)

    def fill(f, c):
        call[f, :, nseq:, :] = padz
        call[f, me, 0:nseq, :] = c_ref[f]
        return c
    lax.fori_loop(0, nf, fill, 0)
    maskcol[...] = jnp.broadcast_to((rm_ref[...].astype(F32) - 1.0) * 1e4, (nres, nres)).T
    hq = fq // 2

    for q in range(nchunk):
        if q + 2 < nchunk:
            own(q + 2)
        got(q, 0, left)
        relay(q, 3, left, right, 0, hq)
        relay(q, 5, left, partner)
        got(q, 1, right)
        relay(q, 4, right, left, hq, hq)
        relay(q, 6, right, partner)
        got(q, 3, far, 0, hq)
        relay(q, 7, far, partner, 0, hq)
        got(q, 4, far, hq, hq)
        relay(q, 8, far, partner, hq, hq)
        if q == 0:
            for d in range(1, n):
                src = lax.rem(me + n - d, n)
                rcopy(aall.at[src], aall.at[src], ssem_a.at[d], rsem_a.at[d], me).wait_recv()
        got(q, 2, partner)
        got(q, 5, other(left))
        got(q, 6, other(right))
        got(q, 7, other(far), 0, hq)
        got(q, 8, other(far), hq, hq)

        def outer(g, c):
            acc = None
            for kk in range(n // 2):
                rhs = jnp.concatenate(
                    [jnp.concatenate([call[q * fq + 2 * g + u, 2 * kk], call[q * fq + 2 * g + u, 2 * kk + 1]], axis=0) for u in range(2)],
                    axis=1)
                lhs = jnp.concatenate([aall[2 * kk], aall[2 * kk + 1]], axis=1)
                part = dot(lhs, rhs)
                acc = part if acc is None else acc + part
            ob = acc.astype(BF)
            for u in range(2):
                for i in range(rows):
                    osc[i, ds8((2 * g + u) * ne, ne, 32), :] = ob[i * ne:(i + 1) * ne, u * nres:(u + 1) * nres]
            return c
        lax.fori_loop(0, fq // 2, outer, 0)

        def contract(g, c):
            rhs = jnp.concatenate([osc[2 * g], osc[2 * g + 1]], axis=1)
            part = dot(wopm_ref[:, q * fq * ne:(q + 1) * fq * ne], rhs)
            for u in range(2):
                v = part[:, u * nres:(u + 1) * nres]
                upd[2 * g + u] = v if q == 0 else upd[2 * g + u] + v
            return c
        lax.fori_loop(0, rows // 2, contract, 0, unroll=2)

    def residual(i, c):
        u = upd[i] / (1e-3 + cnt_ref[pl.ds(i, 1), :])
        z1[i] = (z_ref[i].astype(F32) + u.T).astype(BF)
        return c
    lax.fori_loop(0, rows, residual, 0, unroll=2)

    sends += tri_attend(n, me, z1, wb1_ref, wqkvg1_ref, wo1_ref, maskcol, zln, brow, ball1, bias, proj, flat, wot, tsend1, zmid,
                        ssem_b1, rsem_b1, ssem_t1, rsem_t1)
    sends += tri_attend(n, me, zmid, wb2_ref, wqkvg2_ref, wo2_ref, maskcol, zln, brow, ball2, bias, proj, flat, wot, tsend2, zfin,
                        ssem_b2, rsem_b2, ssem_t2, rsem_t2)
    zo_ref[...] = zfin[...]
    for cp in sends:
        cp.wait_send()


def pair_call(n, a, c, z, cnt, rm, wopm, wb1, wqkvg1, wo1, wb2, wqkvg2, wo2):
    nf, nseq, nres = c.shape
    rows, _, chan = z.shape
    ne = a.shape[0] // nres
    heads = wb1.shape[0]
    nchunk = 4
    fq = nf // nchunk
    dma = pltpu.SemaphoreType.DMA((n,))
    dmac = pltpu.SemaphoreType.DMA((nchunk, 9))
    pitch = rows + 8
    vz = pltpu.VMEM((rows, nres, chan), BF)
    return pl.pallas_call(
        functools.partial(pair_kernel, n, nchunk),
        name="pair",
        out_shape=jax.ShapeDtypeStruct(z.shape, BF),
        in_specs=[VM] * 12,
        out_specs=VM,
        scratch_shapes=[
            pltpu.VMEM((nf, n, 128, nres), BF),
            pltpu.VMEM((n, rows * ne, nres), BF),
            pltpu.VMEM((rows, chan, nres), F32),
            pltpu.VMEM((rows, fq * ne, nres), BF),
            vz, vz,
            pltpu.VMEM((heads * pitch, nres), F32),
            pltpu.VMEM((heads, n * rows, nres), BF),
            pltpu.VMEM((heads, n * rows, nres), BF),
            pltpu.VMEM((nres, heads * nres), F32),
            pltpu.VMEM((rows, 4 * chan, nres), BF),
            pltpu.VMEM((nres * pitch, chan), F32),
            pltpu.VMEM((chan, chan), BF),
            pltpu.VMEM((nres, nres), F32),
            pltpu.VMEM((nres, rows, chan), BF),
            pltpu.VMEM((nres, rows, chan), BF),
            vz, vz,
            dma, dma, dmac, dmac, dma, dma, dma, dma, dma, dma, dma, dma,
        ],
        compiler_params=pltpu.CompilerParams(collective_id=1, has_side_effects=True),
    )(a, c, z, cnt, rm, wopm, wb1, wqkvg1, wo1, wb2, wqkvg2, wo2)


def flat_t(w):
    return jnp.moveaxis(w, 0, -1).reshape(-1, w.shape[0])


def solution(mesh):
    n = mesh.shape["dap"]

    def block(msa, pair, msa_mask, res_mask, row_bias_w, row_qkvg_w, row_out_w, col_query_w, col_kv_w, col_gate_w, col_out_w,
              opm_proj_w, opm_out_w, start_bias_w, start_qkvg_w, start_out_w, end_bias_w, end_qkvg_w, end_out_w):
        nseq, nres, chan = msa.shape
        rows = pair.shape[0]
        pdim = pair.shape[2]
        me = lax.axis_index("dap")
        mt = jnp.transpose(msa, (0, 2, 1))
        m1, x2, o2 = msa_call(n, msa_mask, mt, pair, row_bias_w.T, flat_t(row_qkvg_w), row_out_w.reshape(chan, chan),
                              flat_t(col_query_w), flat_t(col_kv_w))
        seq_mask = lax.dynamic_slice_in_dim(msa_mask, me * nseq, nseq, axis=0)
        m2, a, c = gate_call(seq_mask, m1, x2, o2, flat_t(col_gate_w), col_out_w.reshape(chan, chan), flat_t(opm_proj_w))
        own_mask = lax.dynamic_slice_in_dim(msa_mask, me * rows, rows, axis=1)
        cnt = jnp.einsum('si,sj->ij', own_mask.astype(BF), msa_mask.astype(BF), preferred_element_type=F32)
        wopm = jnp.transpose(opm_out_w, (2, 1, 0)).reshape(pdim, -1)
        zo = pair_call(n, a, c, pair, cnt, res_mask.reshape(1, nres), wopm,
                       start_bias_w.T, flat_t(start_qkvg_w), start_out_w.reshape(pdim, pdim),
                       end_bias_w.T, flat_t(end_qkvg_w), end_out_w.reshape(pdim, pdim))
        return jnp.transpose(m2, (0, 2, 1)), zo

    row_spec = P(('data', 'dap'), None, None)
    in_specs = (row_spec, row_spec, P('data', None), P('data')) + (P(),) * 15
    return jax.shard_map(block, mesh=mesh, in_specs=in_specs, out_specs=(row_spec, row_spec), check_vma=False)
```

time: 338 us -> 279 us (0.83); the launches traced: 333 us -> 279 us
  Pallas kernels: 0 us -> 273 us
  matrix products: 95 us -> 0.92 us
  local copies, waits for them, and re-layouts: 72.9 us -> 4.28 us
  waiting for transfers between devices: 64.8 us -> 0 us
  blocking collectives: 45.6 us -> 0 us
  other arithmetic: 22.2 us -> 0 us
  starting transfers between devices: 17.1 us -> 0 us
  between operations: 15.1 us -> 0.67 us
    pallas_call x0 -> x3, Pallas kernels: none -> 273 us  [the longest x1 137 us: msa_call(): pl.pallas_call(functools.partial(msa_kernel, n), name='msa', out_shape=[j...]
    dot_general x19 -> x1, matrix products: 68.2 us -> 0.92 us  [block(): jnp.einsum('si,sj->ij', own_mask.astype(BF), msa_mask.astype(BF), preferr...]
    convert_element_type x12 -> x0, local copies, waits for them, and re-layouts: 47.5 us -> none  [the longest x2 25.5 us: matmul_bf(): jnp.einsum(einsum_form, left_arr, right_arr, preferred_element_type=jnp.f...]
    all_gather x3 -> x0, blocking collectives: 45.6 us -> none  [the longest x1 17.4 us: evoformer_block(): lax.all_gather(matmul_bf('ijc,ch->hji', cols_ln, end_bias_w), 'dap', axis...]
    all_gather x1 -> x0, waiting for transfers between devices: 39.6 us -> none  [evoformer_block(): right_full = lax.all_gather(projected[1], 'dap', axis=1, tiled=True)]
    sub x2 -> x0, matrix products: 26.6 us -> none  [the longest x1 25.3 us: row_attention(): attn_probs = jax.nn.softmax(logits, axis=-1).astype(jnp.bfloat16)]
    all_to_all x4 -> x0, waiting for transfers between devices: 25.1 us -> none  [the longest x1 24.3 us: evoformer_block(): value_a8 = lax.all_to_all(value_a7, 'dap', 1, 0, tiled=True)]
    all_to_all x4 -> x0, starting transfers between devices: 17 us -> none  [the longest x1 4.57 us: evoformer_block(): array_b7 = lax.all_to_all(value_a8, 'dap', 0, 1, tiled=True)]
  transfers between devices with their start and end apart: 5 -> 0, of which waited for: 3 -> 0; matrix products, arithmetic and copies ran while one was open for 13% -> 0% of each run, Pallas kernels for 0% -> 0%
where the time goes in v1:
time: 279 us
  Pallas kernels  273 us (98%)
  local copies, waits for them, and re-layouts  4.28 us (2%)
    pallas_call x1, Pallas kernels, msa_call(): pl.pallas_call(functools.partial(msa_kernel, n), name='msa', out_shape=[j...  137 us
    pallas_call x1, Pallas kernels, pair_call(): pl.pallas_call(functools.partial(pair_kernel, n, nchunk), name='pair', ou...  114 us
    pallas_call x1, Pallas kernels, gate_call(): pl.pallas_call(gate_kernel, name='gate', out_shape=[jax.ShapeDtypeStruct(...  22 us

profile of v1, /device:TPU:81, one launch (start us, length us, event | category | flops | bytes accessed | tf_op | source)
XLA Modules:
  0.0 278.8 jit_solution(14780063989360963633)
XLA Ops:
  0.6 1.4 constant_dynamic-slice_fusion.mask_ref
  2.1 136.7 %msa.1 = (bf16[96,64,128]{2,1,0:T(8,128)(2,1)}, bf16[96,64,128]{2,1,0:T(8,128)(2,1)}, f32[64,128]{1,0:T(8,128)}) custom-call(s32[768,128]{1,0:T(8,128)} %mask_ref.1, bf16[96,64,128]{2,1,0:T(8,128)(2,1)} %bitcast.34, bf16[16,128,128]{2,1,0:T(8,128)(2,1)} %z_ref.3, bf16[8,128]{1,0:T(8,128)(2,1)} %bitcast.47, bf16[256,64]{1,0:T(8,128)(2,1)} %bitcast.38, ...), custom_call_target="tpu_custom_call" | custom-call | tf_op jit(solution)/shard_map/msa/pallas_call | solution.py:225
  138.8 0.0 copy-start
  138.8 0.0 copy-start.1
  138.8 22.0 %gate.1 = (bf16[96,64,128]{2,1,0:T(8,128)(2,1)}, bf16[4096,128]{1,0:T(8,128)(2,1)}, bf16[32,96,128]{2,1,0:T(8,128)(2,1)}) custom-call(s32[96,128]{1,0:T(8,128)} %constant_dynamic-slice_fusion.mask_ref, bf16[96,64,128]{2,1,0:T(8,128)(2,1)} %get-tuple-element.8.m1_ref, bf16[96,64,128]{2,1,0:T(8,128)(2,1)} %get-tuple-element.9.x2_ref, ...), custom_call_target="tpu_custom_call" | custom-call | tf_op jit(solution)/shard_map/gate/pallas_call | solution.py:288
  160.8 0.0 copy-done
  160.8 0.9 fusion.cnt_ref
  161.7 0.0 copy-done.1
  161.7 0.1 copy.22
  161.8 0.9 copy.23.wopm_ref
  162.7 114.3 %pair.1 = bf16[16,128,128]{2,1,0:T(8,128)(2,1)} custom-call(bf16[4096,128]{1,0:T(8,128)(2,1)} %get-tuple-element.12.a_ref, bf16[32,96,128]{2,1,0:T(8,128)(2,1)} %get-tuple-element.13.c_ref, bf16[16,128,128]{2,1,0:T(8,128)(2,1)} %z_ref.3, f32[16,128]{1,0:T(8,128)} %fusion.cnt_ref, s32[1,128]{1,0:T(1,128)} %bitcast.50, bf16[128,1024]{1,0:T(8,128)(2,1)} %copy.23.wopm_ref, ...), custom_call_target="tpu_custom_call" | custom-call | tf_op jit(solution)/shard_map/pair/pallas_call | solution.py:519
  276.9 1.9 copy.25
Async XLA Ops:
  138.8 22.0 %copy-start = (s32[768,128]{1,0:T(8,128)S(1)}, s32[768,128]{1,0:T(8,128)}, u32[]{:S(2)}) copy-start(s32[768,128]{1,0:T(8,128)} %mask_ref.1) | copy-start | bytes 1179652
  138.8 22.9 %copy-start.1 = (bf16[32,32,128]{2,1,0:T(8,128)(2,1)S(1)}, bf16[32,32,128]{2,1,0:T(8,128)(2,1)}, u32[]{:S(2)}) copy-start(bf16[32,32,128]{2,1,0:T(8,128)(2,1)} %param.31) | copy-start | bytes 786436

commit v2 on v1

--- a/solution.py
+++ b/solution.py
@@ -60,9 +60,9 @@
     return pl.ds(pl.multiple_of(start, unit), size)
 
 
-def msa_kernel(n, mask_ref, m_ref, z_ref, wb_ref, wqkvg_ref, wo_ref, wq2_ref, wkv_ref,
-               m1_ref, x2_ref, o2_ref,
-               ball, bias, brow, kv, lg, wot, qpart, ppart, tmp,
+def msa_kernel(n, mask_ref, m_ref, z_ref, wb_ref, wqkvg_ref, wo_ref, wq2_ref, wkv_ref, wg2_ref,
+               m1_ref, g2_ref, o2_ref,
+               ball, bias, brow, kv, lg, wot, qpart, ppart, tmp, x2_ref, xbuf, klhs, qblk, vbuf, gbuf, lbuf, mbuf, pbuf, rbuf, obuf,
                ssem_b, rsem_b, ssem_q, rsem_q, ssem_p, rsem_p):
     me = lax.axis_index("dap")
     nseq, chan, nres = m_ref.shape
@@ -89,7 +89,30 @@
         cp.start()
         sends.append(cp)
     wot[...] = wo_ref[...].astype(F32).T.astype(BF)
-    qpart[me] = jnp.zeros((chan, nres), F32)
+    rid = lax.broadcasted_iota(jnp.int32, (16, 2 * nres), 0)
+    lid = lax.broadcasted_iota(jnp.int32, (16, 2 * nres), 1)
+    diag = (rid < 8) == (lid < nres)
+
+    def lnorm(t, carry):
+        xbuf[t] = norm(jnp.concatenate([m_ref[2 * t].astype(F32), m_ref[2 * t + 1].astype(F32)], axis=1), 0)
+        return carry
+    lax.fori_loop(0, nseq // 2, lnorm, 0, unroll=2)
+
+    def project(t, carry):
+        s0 = t * 2
+        proj = dot(wqkvg_ref[...], xbuf[t])
+        gbuf[t] = proj[3 * chan:4 * chan, :].astype(BF)
+        for s in range(2):
+            sl = slice(s * nres, (s + 1) * nres)
+            mk = mask_ref[pl.ds(base + s0 + s, 1), :].astype(F32) - 1.0
+            kaug = jnp.concatenate([proj[chan:2 * chan, sl], jnp.broadcast_to(mk, (nres - chan, nres))], axis=0)
+            klhs[s0 + s] = kaug.T.astype(BF)
+            vbuf[s0 + s] = proj[2 * chan:3 * chan, sl].astype(BF)
+            for p in range(heads // 2):
+                q16 = proj[16 * p:16 * p + 16, sl]
+                qblk[s0 + s, 16 * p:16 * p + 16, :] = jnp.where(diag, jnp.concatenate([q16, q16], axis=1), 0.0).astype(BF)
+        return carry
+    lax.fori_loop(0, nseq // 2, project, 0, unroll=2)
     for d in range(1, n):
         src = ds8(lax.rem(me + n - d, n) * rows, rows, 16)
         rcopy(ball.at[:, src, :], ball.at[:, src, :], ssem_b.at[d], rsem_b.at[d], me).wait_recv()
@@ -100,57 +123,86 @@
     rid = lax.broadcasted_iota(jnp.int32, (16, 2 * nres), 0)
     lid = lax.broadcasted_iota(jnp.int32, (16, 2 * nres), 1)
     aug = jnp.where(rid == 0, hi, jnp.where(rid == 1, mid, jnp.where(rid == 2, lo, 0.0))).astype(BF)
-    diag = (rid < 8) == (lid < nres)
+
+    npair = nseq // 2
+    half = heads // 2
+    wide = 2 * nres
+
+    def qk(t, u):
+        s, p = u // half, u % half
+        parts = []
+        if p > 0:
+            parts.append(jnp.zeros((16 * p, wide), BF))
+        parts.append(qblk[t * 2 + s, 16 * p:16 * p + 16, :])
+        if chan - 16 * p - 16 > 0:
+            parts.append(jnp.zeros((chan - 16 * p - 16, wide), BF))
+        parts.append(aug)
+        l = dot(klhs[t * 2 + s, :, 0:chan + 16], jnp.concatenate(parts, axis=0)) * (scale * LOG2E) + bias[:, wide * p:wide * p + wide]
+        lbuf[u] = l
+        mbuf[u, 0:1, :] = jnp.max(l, axis=0, keepdims=True)
+
+    def ex(u):
+        e = jnp.exp2(lbuf[u] - mbuf[u, 0:1, :])
+        pbuf[u] = e.astype(BF)
+        rbuf[u, 0:1, :] = 1.0 / jnp.sum(e, axis=0, keepdims=True)
+
+    def pv(t, u):
+        s, p = u // half, u % half
+        o = dot(vbuf[t * 2 + s, 16 * p:16 * p + 16, :], pbuf[u])
+        sl = slice(s * nres, (s + 1) * nres)
+        obuf[t, 16 * p:16 * p + 8, sl] = o[0:8, 0:nres] * rbuf[u, 0:1, 0:nres]
+        obuf[t, 16 * p + 8:16 * p + 16, sl] = o[8:16, nres:] * rbuf[u, 0:1, nres:]
+
+    units = 2 * half
+    for u in range(units):
+        qk(0, u)
 
     def row_pair(t, carry):
+        tn = jnp.minimum(t + 1, npair - 1)
+        for u in range(units):
+            ex(u)
+            qk(tn, u)
+            if u > 0:
+                pv(t, u - 1)
+        pv(t, units - 1)
+        return carry
+    lax.fori_loop(0, npair, row_pair, 0)
+
+    def finish(t, carry):
         s0 = t * 2
         mv = jnp.concatenate([m_ref[s0].astype(F32), m_ref[s0 + 1].astype(F32)], axis=1)
-        xt = norm(mv, 0)
-        proj = dot(wqkvg_ref[...], xt)
-        outs = []
+        y = (sigmoid(gbuf[t].astype(F32)) * obuf[t]).astype(BF)
+        m1 = (mv + dot(wot[...], y)).astype(BF)
+        for s in range(2):
+            m1_ref[s0 + s] = m1[:, s * nres:(s + 1) * nres]
+        return carry
+    lax.fori_loop(0, npair, finish, 0, unroll=4)
+
+    def renorm(t, acc):
+        s0 = t * 2
+        m1 = jnp.concatenate([m1_ref[s0].astype(F32), m1_ref[s0 + 1].astype(F32)], axis=1)
+        x2 = norm(m1, 0)
         for s in range(2):
             sl = slice(s * nres, (s + 1) * nres)
-            mk = mask_ref[pl.ds(base + s0 + s, 1), :].astype(F32) - 1.0
-            kaug = jnp.concatenate([proj[chan:2 * chan, sl], jnp.broadcast_to(mk, (16, nres))], axis=0)
-            lhs = kaug.T.astype(BF)
-            vt = proj[2 * chan:3 * chan, sl].astype(BF)
-            for p in range(heads // 2):
-                q16 = proj[16 * p:16 * p + 16, sl]
-                blk = jnp.where(diag, jnp.concatenate([q16, q16], axis=1), 0.0).astype(BF)
-                parts = []
-                if p > 0:
-                    parts.append(jnp.zeros((16 * p, 2 * nres), BF))
-                parts.append(blk)
-                if chan - 16 * p - 16 > 0:
-                    parts.append(jnp.zeros((chan - 16 * p - 16, 2 * nres), BF))
-                parts.append(aug)
-                l = dot(lhs, jnp.concatenate(parts, axis=0)) * (scale * LOG2E) + bias[:, 256 * p:256 * p + 256]
-                e = jnp.exp2(l - jnp.max(l, axis=0, keepdims=True))
-                r = 1.0 / jnp.sum(e, axis=0, keepdims=True)
-                o = dot(vt[16 * p:16 * p + 16, :], e.astype(BF))
-                outs.append((o[0:8, 0:nres] * r[:, 0:nres], o[8:16, nres:] * r[:, nres:]))
-        half = heads // 2
-        ot = jnp.concatenate(
-            [jnp.concatenate([v for pr in outs[s * half:(s + 1) * half] for v in pr], axis=0) for s in range(2)], axis=1)
-        y = (sigmoid(rnd(proj[3 * chan:4 * chan, :])) * ot).astype(BF)
-        m1 = (mv + dot(wot[...], y)).astype(BF)
-        x2 = norm(m1.astype(F32), 0)
-        kvp = rnd(dot(wkv_ref[...], x2))
-        acc = qpart[me]
-        for s in range(2):
-            sl = slice(s * nres, (s + 1) * nres)
-            m1_ref[s0 + s] = m1[:, sl]
             x2_ref[s0 + s] = x2[:, sl]
-            kv[s0 + s] = kvp[:, sl]
             acc = acc + mask_ref[pl.ds(base + s0 + s, 1), :].astype(F32) * x2[:, sl].astype(F32)
-        qpart[me] = acc
-        return carry
-    lax.fori_loop(0, nseq // 2, row_pair, 0)
+        return acc
+    qpart[me] = lax.fori_loop(0, npair, renorm, jnp.zeros((chan, nres), F32), unroll=2)
 
     for d in range(1, n):
         cp = rcopy(qpart.at[me], qpart.at[me], ssem_q.at[d], rsem_q.at[d], lax.rem(me + d, n))
         cp.start()
         sends.append(cp)
+
+    def keyval(t, carry):
+        s0 = t * 2
+        xv = jnp.concatenate([x2_ref[s0], x2_ref[s0 + 1]], axis=1)
+        kvp = rnd(dot(wkv_ref[...], xv))
+        g2_ref[t] = dot(wg2_ref[...], xv).astype(BF)
+        for s in range(2):
+            kv[s0 + s] = kvp[:, s * nres:(s + 1) * nres]
+        return carry
+    lax.fori_loop(0, npair, keyval, 0, unroll=4)
     count = jnp.sum(mask_ref[...].astype(F32), axis=0, keepdims=True) + 1e-10
     for d in range(1, n):
         src = lax.rem(me + n - d, n)
@@ -217,7 +269,7 @@
         cp.wait_send()
 
 
-def msa_call(n, mask, mt, z, wb, wqkvg, wo, wq2, wkv):
+def msa_call(n, mask, mt, z, wb, wqkvg, wo, wq2, wkv, wg2):
     nseq, chan, nres = mt.shape
     rows = z.shape[0]
     heads = wb.shape[0]
@@ -225,9 +277,9 @@
     return pl.pallas_call(
         functools.partial(msa_kernel, n),
         name="msa",
-        out_shape=[jax.ShapeDtypeStruct((nseq, chan, nres), BF), jax.ShapeDtypeStruct((nseq, chan, nres), BF),
+        out_shape=[jax.ShapeDtypeStruct((nseq, chan, nres), BF), jax.ShapeDtypeStruct((nseq // 2, chan, 2 * nres), BF),
                    jax.ShapeDtypeStruct((chan, nres), F32)],
-        in_specs=[VM] * 8,
+        in_specs=[VM] * 9,
         out_specs=[VM] * 3,
         scratch_shapes=[
             pltpu.VMEM((heads, n * rows, nres), BF),
@@ -239,32 +291,50 @@
             pltpu.VMEM((n, chan, nres), F32),
             pltpu.VMEM((n, chan + 16, nres), F32),
             pltpu.VMEM((chan, nres), F32),
+            pltpu.VMEM((nseq, chan, nres), BF),
+            pltpu.VMEM((nseq // 2, chan, 2 * nres), BF),
+            pltpu.VMEM((nseq, nres, nres), BF),
+            pltpu.VMEM((nseq, chan, 2 * nres), BF),
+            pltpu.VMEM((nseq, chan, nres), BF),
+            pltpu.VMEM((nseq // 2, chan, 2 * nres), BF),
+            pltpu.VMEM((heads, nres, 2 * nres), F32),
+            pltpu.VMEM((heads, 8, 2 * nres), F32),
+            pltpu.VMEM((heads, nres, 2 * nres), BF),
+            pltpu.VMEM((heads, 8, 2 * nres), F32),
+            pltpu.VMEM((nseq // 2, chan, 2 * nres), F32),
             dma, dma, dma, dma, dma, dma,
         ],
         compiler_params=pltpu.CompilerParams(collective_id=0, has_side_effects=True),
-    )(mask, mt, z, wb, wqkvg, wo, wq2, wkv)
-
-
-def gate_kernel(mask_ref, m1_ref, x2_ref, o2_ref, wg_ref, wo_ref, wopm_ref, m2_ref, a_ref, c_ref, ac, at, wot):
+    )(mask, mt, z, wb, wqkvg, wo, wq2, wkv, wg2)
+
+
+def gate_kernel(mask_ref, m1_ref, g2_ref, o2_ref, wo_ref, wopm_ref, m2_ref, a_ref, c_ref, ac, at, wot, xbuf):
     nseq, chan, nres = m1_ref.shape
     ne = chan // 2
     pitch = chan + 8
     wot[...] = wo_ref[...].astype(F32).T.astype(BF)
-    o2 = jnp.concatenate([o2_ref[...]] * 2, axis=1)
-
-    def pair(t, carry):
+
+    def gate(t, carry):
         s0 = t * 2
-        xv = jnp.concatenate([x2_ref[s0], x2_ref[s0 + 1]], axis=1)
-        y = (sigmoid(rnd(dot(wg_ref[...], xv))) * o2).astype(BF)
+        y = (sigmoid(g2_ref[t].astype(F32)) * jnp.concatenate([o2_ref[...]] * 2, axis=1)).astype(BF)
         m1 = jnp.concatenate([m1_ref[s0].astype(F32), m1_ref[s0 + 1].astype(F32)], axis=1)
         m2 = (m1 + dot(wot[...], y)).astype(BF)
-        pr = rnd(dot(wopm_ref[...], norm(m2.astype(F32), 0)))
         for s in range(2):
-            sl = slice(s * nres, (s + 1) * nres)
-            m2_ref[s0 + s] = m2[:, sl]
-            ac[ds8((s0 + s) * pitch, chan), :] = pr[:, sl] * mask_ref[pl.ds(s0 + s, 1), :].astype(F32)
-        return carry
-    lax.fori_loop(0, nseq // 2, pair, 0, unroll=2)
+            m2_ref[s0 + s] = m2[:, s * nres:(s + 1) * nres]
+        return carry
+    lax.fori_loop(0, nseq // 2, gate, 0, unroll=4)
+
+    def renorm(t, carry):
+        xbuf[t] = norm(jnp.concatenate([m2_ref[2 * t].astype(F32), m2_ref[2 * t + 1].astype(F32)], axis=1), 0)
+        return carry
+    lax.fori_loop(0, nseq // 2, renorm, 0, unroll=2)
+
+    def project(t, carry):
+        pr = rnd(dot(wopm_ref[...], xbuf[t]))
+        for s in range(2):
+            ac[ds8((2 * t + s) * pitch, chan), :] = pr[:, s * nres:(s + 1) * nres] * mask_ref[pl.ds(2 * t + s, 1), :].astype(F32)
+        return carry
+    lax.fori_loop(0, nseq // 2, project, 0, unroll=4)
 
     pitch2 = ne + 8
     pad = jnp.zeros((nres - nseq, nres), F32)
@@ -274,7 +344,7 @@
         at[pl.ds(e, nres, stride=pitch2), :] = a.T
         c_ref[e] = ac[pl.ds(ne + e, nseq, stride=pitch), :].astype(BF)
         return carry
-    lax.fori_loop(0, ne, plane, 0, unroll=2)
+    lax.fori_loop(0, ne, plane, 0, unroll=4)
 
     def row(i, carry):
         a_ref[ds8(i * ne, ne, 32), :] = at[ds8(i * pitch2, ne), :].astype(BF)
@@ -282,7 +352,7 @@
     lax.fori_loop(0, nres, row, 0, unroll=4)
 
 
-def gate_call(mask, m1, x2, o2, wg, wo, wopm):
+def gate_call(mask, m1, g2, o2, wo, wopm):
     nseq, chan, nres = m1.shape
     ne = chan // 2
     return pl.pallas_call(
@@ -290,17 +360,18 @@
         name="gate",
         out_shape=[jax.ShapeDtypeStruct((nseq, chan, nres), BF), jax.ShapeDtypeStruct((nres * ne, nres), BF),
                    jax.ShapeDtypeStruct((ne, nseq, nres), BF)],
-        in_specs=[VM] * 7,
+        in_specs=[VM] * 6,
         out_specs=[VM] * 3,
         scratch_shapes=[
             pltpu.VMEM((nseq * (chan + 8), nres), F32),
             pltpu.VMEM((nres * (ne + 8), nres), F32),
             pltpu.VMEM((chan, chan), BF),
+            pltpu.VMEM((nseq // 2, chan, 2 * nres), BF),
         ],
-    )(mask, m1, x2, o2, wg, wo, wopm)
-
-
-def tri_attend(n, me, zin, wb_ref, wqkvg_ref, wo_ref, maskcol, zln, brow, ball, bias, proj, flat, wot, tsend, zrecv,
+    )(mask, m1, g2, o2, wo, wopm)
+
+
+def tri_attend(n, me, zin, wb_ref, wqkvg_ref, wo_ref, maskcol, zln, brow, ball, bias, proj, flat, wot, lbuf, mbuf, pbuf, rbuf, obuf, tsend, zrecv,
                ssem_b, rsem_b, ssem_t, rsem_t):
     rows, nres, chan = zin.shape
     heads = wb_ref.shape[0]
@@ -338,31 +409,54 @@
         bias[:, h * nres:(h + 1) * nres] = (ball[h].astype(F32).T + maskcol[...]) * LOG2E
     zero = jnp.zeros((hd, nres), BF)
 
-    def attend(i, c):
-        kmat = proj[i, chan:2 * chan, :]
-        outs = []
-        for p in range(heads // 2):
-            r0 = 2 * hd * p
-            qa = proj[i, r0:r0 + hd, :]
-            qb = proj[i, r0 + hd:r0 + 2 * hd, :]
-            blk = jnp.concatenate([jnp.concatenate([qa, zero], axis=1), jnp.concatenate([zero, qb], axis=1)], axis=0)
-            parts = []
-            if p > 0:
-                parts.append(jnp.zeros((r0, 2 * nres), BF))
-            parts.append(blk)
-            if chan - r0 - 2 * hd > 0:
-                parts.append(jnp.zeros((chan - r0 - 2 * hd, 2 * nres), BF))
-            l = dot(kmat, jnp.concatenate(parts, axis=0)) * (scale * LOG2E) + bias[:, 256 * p:256 * p + 256]
-            e = jnp.exp2(l - jnp.max(l, axis=0, keepdims=True))
-            r = 1.0 / jnp.sum(e, axis=0, keepdims=True)
-            o = dot(proj[i, 2 * chan + r0:2 * chan + r0 + 2 * hd, :], e.astype(BF))
-            outs.append(o[0:hd, 0:nres] * r[:, 0:nres])
-            outs.append(o[hd:, nres:] * r[:, nres:])
-        y = (sigmoid(proj[i, 3 * chan:4 * chan, :].astype(F32)) * jnp.concatenate(outs, axis=0)).astype(BF)
+    half = heads // 2
+    wide = 2 * nres
+
+    def qk(i, p, u):
+        r0 = 2 * hd * p
+        qa = proj[i, r0:r0 + hd, :]
+        qb = proj[i, r0 + hd:r0 + 2 * hd, :]
+        parts = [jnp.zeros((r0, wide), BF)] if p > 0 else []
+        parts.append(jnp.concatenate([qa, zero], axis=1))
+        parts.append(jnp.concatenate([zero, qb], axis=1))
+        if chan - r0 - 2 * hd > 0:
+            parts.append(jnp.zeros((chan - r0 - 2 * hd, wide), BF))
+        l = dot(proj[i, chan:2 * chan, :], jnp.concatenate(parts, axis=0)) * (scale * LOG2E) + bias[:, wide * p:wide * p + wide]
+        lbuf[u] = l
+        mbuf[u, 0:1, :] = jnp.max(l, axis=0, keepdims=True)
+
+    def ex(u):
+        e = jnp.exp2(lbuf[u] - mbuf[u, 0:1, :])
+        pbuf[u] = e.astype(BF)
+        rbuf[u, 0:1, :] = 1.0 / jnp.sum(e, axis=0, keepdims=True)
+
+    def pv(i, p, u):
+        r0 = 2 * hd * p
+        o = dot(proj[i, 2 * chan + r0:2 * chan + r0 + 2 * hd, :], pbuf[u])
+        obuf[i, r0:r0 + hd, :] = o[0:hd, 0:nres] * rbuf[u, 0:1, 0:nres]
+        obuf[i, r0 + hd:r0 + 2 * hd, :] = o[hd:, nres:] * rbuf[u, 0:1, nres:]
+
+    units = [(i, p) for i in range(2) for p in range(half)]
+    for u, (i, p) in enumerate(units):
+        qk(i, p, u)
+
+    def attend(t, c):
+        nxt = jnp.minimum(2 * t + 2, rows - 2)
+        for u, (i, p) in enumerate(units):
+            ex(u)
+            qk(nxt + i, p, u)
+            if u > 0:
+                pv(2 * t + units[u - 1][0], units[u - 1][1], u - 1)
+        pv(2 * t + units[-1][0], units[-1][1], len(units) - 1)
+        return c
+    lax.fori_loop(0, rows // 2, attend, 0)
+
+    def finish(i, c):
+        y = (sigmoid(proj[i, 3 * chan:4 * chan, :].astype(F32)) * obuf[i]).astype(BF)
         upd = dot(wot[...], y).T
         flat[pl.ds(i, nres, stride=pitch), :] = zin[i].astype(F32) + upd
         return c
-    lax.fori_loop(0, rows, attend, 0, unroll=2)
+    lax.fori_loop(0, rows, finish, 0, unroll=4)
 
     def regroup(j, c):
         tsend[j] = flat[ds8(j * pitch, rows), :].astype(BF)
@@ -382,8 +476,8 @@
 
 def pair_kernel(n, nchunk, a_ref, c_ref, z_ref, cnt_ref, rm_ref, wopm_ref, wb1_ref, wqkvg1_ref, wo1_ref, wb2_ref, wqkvg2_ref, wo2_ref,
                 zo_ref,
-                call, aall, upd, osc, z1, zln, brow, ball1, ball2, bias, proj, flat, wot, maskcol, tsend1, tsend2, zmid, zfin,
-                ssem_a, rsem_a, ssem_c, rsem_c, ssem_b1, rsem_b1, ssem_t1, rsem_t1, ssem_b2, rsem_b2, ssem_t2, rsem_t2):
+                call, aall, upd, osc, z1, zln, brow, ball1, ball2, bias, proj, flat, wot, lbuf, mbuf, pbuf, rbuf, obuf, arel, maskcol, tsend1, tsend2, zmid, zfin,
+                ssem_a, rsem_a, ssem_r, rsem_r, ssem_c, rsem_c, ssem_b1, rsem_b1, ssem_t1, rsem_t1, ssem_b2, rsem_b2, ssem_t2, rsem_t2):
     me = lax.axis_index("dap")
     nf, nseq, nres = c_ref.shape
     rows, _, chan = z_ref.shape
@@ -426,9 +520,17 @@
         b = blk(q, dev, lo, size)
         go(b, b, ssem_c.at[q, kind], rsem_c.at[q, kind], to)
 
-    for d in range(1, n):
-        dst = lax.rem(me + d, n)
-        go(a_ref.at[pl.ds(dst * arows, arows), :], aall.at[me], ssem_a.at[d], rsem_a.at[d], dst)
+    rightc, leftc, farc = lax.rem(x + 1, nx) * 2, lax.rem(x + nx - 1, nx) * 2, lax.rem(x + 2, nx) * 2
+
+    def ablk(dst):
+        return a_ref.at[pl.ds(dst * arows, arows), :]
+
+    go(ablk(farc), arel.at[0], ssem_a.at[0], rsem_a.at[0], right)
+    go(ablk(farc + 1), arel.at[1], ssem_a.at[1], rsem_a.at[1], left)
+    for j in range(2):
+        go(ablk(rightc + j), aall.at[me], ssem_a.at[2 + j], rsem_a.at[2 + k], rightc + j)
+        go(ablk(leftc + j), aall.at[me], ssem_a.at[4 + j], rsem_a.at[4 + k], leftc + j)
+    go(ablk(partner), aall.at[me], ssem_a.at[6], rsem_a.at[6], partner)
     own(0)
     own(1)
     aall[me] = a_ref[ds8(me * arows, arows, 32), :]
@@ -442,23 +544,36 @@
     maskcol[...] = jnp.broadcast_to((rm_ref[...].astype(F32) - 1.0) * 1e4, (nres, nres)).T
     hq = fq // 2
 
-    for q in range(nchunk):
-        if q + 2 < nchunk:
-            own(q + 2)
+    def neighbours(q):
         got(q, 0, left)
         relay(q, 3, left, right, 0, hq)
         relay(q, 5, left, partner)
         got(q, 1, right)
         relay(q, 4, right, left, hq, hq)
         relay(q, 6, right, partner)
+        if q + 2 < nchunk:
+            own(q + 2)
+
+    def gota(slot, sem):
+        rcopy(aall.at[slot], aall.at[slot], ssem_a.at[0], sem, me).wait_recv()
+
+    rcopy(arel.at[0], arel.at[0], ssem_a.at[0], rsem_a.at[0], me).wait_recv()
+    go(arel.at[0], aall.at[left], ssem_r.at[0], rsem_r.at[k], rightc)
+    rcopy(arel.at[1], arel.at[1], ssem_a.at[1], rsem_a.at[1], me).wait_recv()
+    go(arel.at[1], aall.at[right], ssem_r.at[1], rsem_r.at[k], leftc + 1)
+    neighbours(0)
+    neighbours(1)
+    for j in range(2):
+        gota(leftc + j, rsem_a.at[2 + j])
+        gota(rightc + j, rsem_a.at[4 + j])
+        gota(farc + j, rsem_r.at[j])
+    gota(partner, rsem_a.at[6])
+
+    for q in range(nchunk):
         got(q, 3, far, 0, hq)
         relay(q, 7, far, partner, 0, hq)
         got(q, 4, far, hq, hq)
         relay(q, 8, far, partner, hq, hq)
-        if q == 0:
-            for d in range(1, n):
-                src = lax.rem(me + n - d, n)
-                rcopy(aall.at[src], aall.at[src], ssem_a.at[d], rsem_a.at[d], me).wait_recv()
         got(q, 2, partner)
         got(q, 5, other(left))
         got(q, 6, other(right))
@@ -489,6 +604,8 @@
                 upd[2 * g + u] = v if q == 0 else upd[2 * g + u] + v
             return c
         lax.fori_loop(0, rows // 2, contract, 0, unroll=2)
+        if q + 2 < nchunk:
+            neighbours(q + 2)
 
     def residual(i, c):
         u = upd[i] / (1e-3 + cnt_ref[pl.ds(i, 1), :])
@@ -496,9 +613,9 @@
         return c
     lax.fori_loop(0, rows, residual, 0, unroll=2)
 
-    sends += tri_attend(n, me, z1, wb1_ref, wqkvg1_ref, wo1_ref, maskcol, zln, brow, ball1, bias, proj, flat, wot, tsend1, zmid,
+    sends += tri_attend(n, me, z1, wb1_ref, wqkvg1_ref, wo1_ref, maskcol, zln, brow, ball1, bias, proj, flat, wot, lbuf, mbuf, pbuf, rbuf, obuf, tsend1, zmid,
                         ssem_b1, rsem_b1, ssem_t1, rsem_t1)
-    sends += tri_attend(n, me, zmid, wb2_ref, wqkvg2_ref, wo2_ref, maskcol, zln, brow, ball2, bias, proj, flat, wot, tsend2, zfin,
+    sends += tri_attend(n, me, zmid, wb2_ref, wqkvg2_ref, wo2_ref, maskcol, zln, brow, ball2, bias, proj, flat, wot, lbuf, mbuf, pbuf, rbuf, obuf, tsend2, zfin,
                         ssem_b2, rsem_b2, ssem_t2, rsem_t2)
     zo_ref[...] = zfin[...]
     for cp in sends:
@@ -535,11 +652,17 @@
             pltpu.VMEM((rows, 4 * chan, nres), BF),
             pltpu.VMEM((nres * pitch, chan), F32),
             pltpu.VMEM((chan, chan), BF),
+            pltpu.VMEM((heads, nres, 2 * nres), F32),
+            pltpu.VMEM((heads, 8, 2 * nres), F32),
+            pltpu.VMEM((heads, nres, 2 * nres), BF),
+            pltpu.VMEM((heads, 8, 2 * nres), F32),
+            pltpu.VMEM((rows, chan, nres), F32),
+            pltpu.VMEM((2, rows * ne, nres), BF),
             pltpu.VMEM((nres, nres), F32),
             pltpu.VMEM((nres, rows, chan), BF),
             pltpu.VMEM((nres, rows, chan), BF),
             vz, vz,
-            dma, dma, dmac, dmac, dma, dma, dma, dma, dma, dma, dma, dma,
+            dma, dma, dma, dma, dmac, dmac, dma, dma, dma, dma, dma, dma, dma, dma,
         ],
         compiler_params=pltpu.CompilerParams(collective_id=1, has_side_effects=True),
     )(a, c, z, cnt, rm, wopm, wb1, wqkvg1, wo1, wb2, wqkvg2, wo2)
@@ -559,10 +682,10 @@
         pdim = pair.shape[2]
         me = lax.axis_index("dap")
         mt = jnp.transpose(msa, (0, 2, 1))
-        m1, x2, o2 = msa_call(n, msa_mask, mt, pair, row_bias_w.T, flat_t(row_qkvg_w), row_out_w.reshape(chan, chan),
-                              flat_t(col_query_w), flat_t(col_kv_w))
+        m1, g2, o2 = msa_call(n, msa_mask, mt, pair, row_bias_w.T, flat_t(row_qkvg_w), row_out_w.reshape(chan, chan),
+                              flat_t(col_query_w), flat_t(col_kv_w), flat_t(col_gate_w))
         seq_mask = lax.dynamic_slice_in_dim(msa_mask, me * nseq, nseq, axis=0)
-        m2, a, c = gate_call(seq_mask, m1, x2, o2, flat_t(col_gate_w), col_out_w.reshape(chan, chan), flat_t(opm_proj_w))
+        m2, a, c = gate_call(seq_mask, m1, g2, o2, col_out_w.reshape(chan, chan), flat_t(opm_proj_w))
         own_mask = lax.dynamic_slice_in_dim(msa_mask, me * rows, rows, axis=1)
         cnt = jnp.einsum('si,sj->ij', own_mask.astype(BF), msa_mask.astype(BF), preferred_element_type=F32)
         wopm = jnp.transpose(opm_out_w, (2, 1, 0)).reshape(pdim, -1)

time: 279 us -> 155 us (0.56)
  Pallas kernels: 273 us -> 149 us
    pallas_call x1, Pallas kernels: 137 us -> 51.3 us  [msa_call(): pl.pallas_call(functools.partial(msa_kernel, n), name='msa', out_shape=[j...]
    pallas_call x1, Pallas kernels: 114 us -> 86 us  [pair_call(): pl.pallas_call(functools.partial(pair_kernel, n, nchunk), name='pair', ou...]
    pallas_call x1, Pallas kernels: 22 us -> 11.6 us  [gate_call(): pl.pallas_call(gate_kernel, name='gate', out_shape=[jax.ShapeDtypeStruct(...]
where the time goes in v2:
time: 155 us
  Pallas kernels  149 us (96%)
  local copies, waits for them, and re-layouts  4.28 us (3%)
    pallas_call x1, Pallas kernels, pair_call(): pl.pallas_call(functools.partial(pair_kernel, n, nchunk), name='pair', ou...  86 us
    pallas_call x1, Pallas kernels, msa_call(): pl.pallas_call(functools.partial(msa_kernel, n), name='msa', out_shape=[j...  51.3 us
    pallas_call x1, Pallas kernels, gate_call(): pl.pallas_call(gate_kernel, name='gate', out_shape=[jax.ShapeDtypeStruct(...  11.6 us

profile of v2, /device:TPU:81, one launch (start us, length us, event | category | flops | bytes accessed | tf_op | source)
XLA Modules:
  0.0 154.7 jit_solution(2732417972095623758)
XLA Ops:
  0.6 1.4 constant_dynamic-slice_fusion.mask_ref
  2.1 51.3 %msa.1 = (bf16[96,64,128]{2,1,0:T(8,128)(2,1)}, bf16[48,64,256]{2,1,0:T(8,128)(2,1)}, f32[64,128]{1,0:T(8,128)}) custom-call(s32[768,128]{1,0:T(8,128)} %mask_ref.1, bf16[96,64,128]{2,1,0:T(8,128)(2,1)} %bitcast.34, bf16[16,128,128]{2,1,0:T(8,128)(2,1)} %z_ref.3, bf16[8,128]{1,0:T(8,128)(2,1)} %bitcast.47, bf16[256,64]{1,0:T(8,128)(2,1)} %bitcast.38, ...), custom_call_target="tpu_custom_call" | custom-call | tf_op jit(solution)/shard_map/msa/pallas_call | solution.py:277
  53.4 0.0 copy-start
  53.4 0.0 copy-start.1
  53.4 11.6 %gate.1 = (bf16[96,64,128]{2,1,0:T(8,128)(2,1)}, bf16[4096,128]{1,0:T(8,128)(2,1)}, bf16[32,96,128]{2,1,0:T(8,128)(2,1)}) custom-call(s32[96,128]{1,0:T(8,128)} %constant_dynamic-slice_fusion.mask_ref, bf16[96,64,128]{2,1,0:T(8,128)(2,1)} %get-tuple-element.8.m1_ref, bf16[48,64,256]{2,1,0:T(8,128)(2,1)} %get-tuple-element.9.g2_ref, ...), custom_call_target="tpu_custom_call" | custom-call | tf_op jit(solution)/shard_map/gate/pallas_call | solution.py:358
  64.9 0.0 copy-done
  64.9 0.9 fusion.cnt_ref
  65.9 0.0 copy-done.1
  65.9 0.1 copy.22
  66.0 0.9 copy.23.wopm_ref
  66.8 86.0 %pair.1 = bf16[16,128,128]{2,1,0:T(8,128)(2,1)} custom-call(bf16[4096,128]{1,0:T(8,128)(2,1)} %get-tuple-element.12.a_ref, bf16[32,96,128]{2,1,0:T(8,128)(2,1)} %get-tuple-element.13.c_ref, bf16[16,128,128]{2,1,0:T(8,128)(2,1)} %z_ref.3, f32[16,128]{1,0:T(8,128)} %fusion.cnt_ref, s32[1,128]{1,0:T(1,128)} %bitcast.50, bf16[128,1024]{1,0:T(8,128)(2,1)} %copy.23.wopm_ref, ...), custom_call_target="tpu_custom_call" | custom-call | tf_op jit(solution)/shard_map/pair/pallas_call | solution.py:636
  152.8 1.9 %copy.25 = bf16[16,128,128]{2,1,0:T(8,128)(2,1)} copy(bf16[16,128,128]{2,1,0:T(8,128)(2,1)} %pair.1) | data formatting | bytes 1048576
Async XLA Ops:
  53.4 11.6 %copy-start = (s32[768,128]{1,0:T(8,128)S(1)}, s32[768,128]{1,0:T(8,128)}, u32[]{:S(2)}) copy-start(s32[768,128]{1,0:T(8,128)} %mask_ref.1) | copy-start | bytes 1179652
  53.4 12.5 %copy-start.1 = (bf16[32,32,128]{2,1,0:T(8,128)(2,1)S(1)}, bf16[32,32,128]{2,1,0:T(8,128)(2,1)}, u32[]{:S(2)}) copy-start(bf16[32,32,128]{2,1,0:T(8,128)(2,1)} %param.31) | copy-start | bytes 786436

commit v3 on v2

v3 whole, which is shorter than its diff:
```python
import functools
import math

import jax
import jax.numpy as jnp
import numpy as np
from jax import lax
from jax.experimental import pallas as pl
from jax.experimental.pallas import tpu as pltpu
from jax.sharding import PartitionSpec as P

BF = jnp.bfloat16
F32 = jnp.float32
MESH = pl.DeviceIdType.MESH
LOG2E = math.log2(math.e)
VM = pl.BlockSpec(memory_space=pltpu.VMEM)


def dot(a, b):
    return lax.dot_general(a, b, (((1,), (0,)), ((), ())), preferred_element_type=F32)


def dot_nt(a, b):
    return lax.dot_general(a, b, (((1,), (1,)), ((), ())), preferred_element_type=F32)


def rnd(v):
    return v.astype(BF).astype(F32)


def norm(v, axis):
    mean = jnp.mean(v, axis=axis, keepdims=True)
    cen = v - mean
    var = jnp.mean(cen * cen, axis=axis, keepdims=True)
    return (cen * lax.rsqrt(var + 1e-5)).astype(BF)


def sigmoid(v):
    return 1.0 / (1.0 + jnp.exp(-v))


def split3(value):
    hi = float(np.asarray(value).astype(BF))
    mid = float(np.asarray(value - hi).astype(BF))
    return hi, mid, float(np.asarray(value - hi - mid).astype(BF))


def rcopy(src, dst, ssem, rsem, dev):
    return pltpu.make_async_remote_copy(src_ref=src, dst_ref=dst, send_sem=ssem, recv_sem=rsem, device_id={"dap": dev}, device_id_type=MESH)


def loop(count, body, unroll=1):
    lax.fori_loop(0, count, lambda t, c: (body(t), c)[-1], 0, unroll=unroll)


def cat(*v):
    return jnp.concatenate(v, axis=-1)


def stack(*v):
    return jnp.concatenate(v, axis=0)


def part(s, width):
    return slice(s * width, s * width + width)


class Place:
    def __init__(self, n):
        nx = n // 2
        self.n, self.me = n, lax.axis_index("dap")
        x, self.k = lax.div(self.me, 2), lax.rem(self.me, 2)
        self.rightc, self.leftc, self.farc = (lax.rem(x + d, nx) * 2 for d in (1, nx - 1, 2))
        self.right, self.left, self.far = (c + self.k for c in (self.rightc, self.leftc, self.farc))
        self.partner = self.other(self.me)
        self.sends = []

    def other(self, dev):
        return dev + 1 - 2 * self.k

    def signal(self):
        sem = pltpu.get_barrier_semaphore()
        for d in range(1, self.n):
            pl.semaphore_signal(sem, inc=1, device_id={"dap": lax.rem(self.me + d, self.n)}, device_id_type=MESH)

    def meet(self):
        pl.semaphore_wait(pltpu.get_barrier_semaphore(), self.n - 1)

    def go(self, src, dst, ssem, rsem, dev):
        cp = rcopy(src, dst, ssem, rsem, dev)
        cp.start()
        self.sends.append(cp)

    def got(self, dst, rsem):
        rcopy(dst, dst, rsem, rsem, self.me).wait_recv()

    def drain(self):
        for cp in self.sends:
            cp.wait_send()

    def to_all(self, src, slot, ssem, rsem):
        for d in range(1, self.n):
            self.go(src, slot(self.me), ssem.at[d], rsem.at[d], lax.rem(self.me + d, self.n))

    def from_all(self, slot, rsem):
        for d in range(1, self.n):
            self.got(slot(lax.rem(self.me + self.n - d, self.n)), rsem.at[d])

    def scatter(self, blk, slot, rel, ssem, rsem):
        k, me = self.k, self.me
        self.go(blk(self.farc), rel.at[0], ssem.at[0], rsem.at[0], self.right)
        self.go(blk(self.farc + 1), rel.at[1], ssem.at[1], rsem.at[1], self.left)
        for j in range(2):
            self.go(blk(self.rightc + j), slot(me), ssem.at[2 + j], rsem.at[2 + k], self.rightc + j)
            self.go(blk(self.leftc + j), slot(me), ssem.at[4 + j], rsem.at[4 + k], self.leftc + j)
        self.go(blk(self.partner), slot(me), ssem.at[6], rsem.at[6], self.partner)

    def scatter_relay(self, slot, rel, ssem, rsem):
        self.got(rel.at[0], rsem.at[0])
        self.go(rel.at[0], slot(self.left), ssem.at[7], rsem.at[7 + self.k], self.rightc)
        self.got(rel.at[1], rsem.at[1])
        self.go(rel.at[1], slot(self.right), ssem.at[8], rsem.at[7 + self.k], self.leftc + 1)

    def scatter_wait(self, slot, rsem):
        for j in range(2):
            self.got(slot(self.leftc + j), rsem.at[2 + j])
            self.got(slot(self.rightc + j), rsem.at[4 + j])
            self.got(slot(self.farc + j), rsem.at[7 + j])
        self.got(slot(self.partner), rsem.at[6])

    def spread(self, src, slot, ssem, rsem):
        for i, dev in enumerate((self.right, self.left, self.partner)):
            self.go(src, slot(self.me), ssem.at[i], rsem.at[i], dev)

    def spread_relay(self, slot, lower, upper, ssem, rsem):
        left, right = self.left, self.right
        self.got(slot(left), rsem.at[0])
        self.go(lower(left), lower(left), ssem.at[3], rsem.at[3], right)
        self.go(slot(left), slot(left), ssem.at[5], rsem.at[5], self.partner)
        self.got(slot(right), rsem.at[1])
        self.go(upper(right), upper(right), ssem.at[4], rsem.at[4], left)
        self.go(slot(right), slot(right), ssem.at[6], rsem.at[6], self.partner)

    def spread_wait(self, slot, lower, upper, ssem, rsem):
        for i, half in enumerate((lower, upper)):
            self.got(half(self.far), rsem.at[3 + i])
            self.go(half(self.far), half(self.far), ssem.at[7 + i], rsem.at[7 + i], self.partner)
        self.got(slot(self.partner), rsem.at[2])
        self.got(slot(self.other(self.left)), rsem.at[5])
        self.got(slot(self.other(self.right)), rsem.at[6])
        for i, half in enumerate((lower, upper)):
            self.got(half(self.other(self.far)), rsem.at[7 + i])


def ds8(start, size, unit=8):
    return pl.ds(pl.multiple_of(start, unit), size)


def msa_kernel(n, nin, *refs):
    inputs, outputs, held = refs[:nin], refs[nin:nin + 3], refs[nin + 3:2 * nin + 3]
    msa_body(n, inputs, held, *outputs, *refs[2 * nin + 3:])


def msa_body(n, inputs, held,
               m1_ref, g2_ref, o2_ref, isem,
               ball, bias, brow, kv, lg, wot, qpart, ppart, tmp, x2_ref, xbuf, klhs, qblk, vbuf, gbuf, lbuf, mbuf, pbuf, rbuf, obuf,
               ssem_b, rsem_b, ssem_q, rsem_q, ssem_p, rsem_p):
    pc = Place(n)
    me = pc.me
    pc.signal()
    loads = [pltpu.make_async_copy(a, b, isem.at[i]) for i, (a, b) in enumerate(zip(inputs, held))]
    for cp in loads:
        cp.start()
    z_ref, wb_ref, mask_ref, m_ref, wqkvg_ref, wo_ref, wq2_ref, wkv_ref, wg2_ref = held
    loads[0].wait()
    loads[1].wait()
    nseq, chan, nres = m_ref.shape
    rows = z_ref.shape[0]
    heads = wb_ref.shape[0]
    hd = chan // heads
    scale = hd ** -0.5
    base = me * nseq

    pitch = rows + 8

    def bias_row(i):
        b = dot_nt(wb_ref[:], norm(z_ref[i].astype(F32), 1))
        brow[pl.ds(i, heads, stride=pitch), :] = b
    loop(rows, bias_row, 4)
    mine = ds8(me * rows, rows, 16)
    for h in range(heads):
        ball[h, mine, :] = brow[h * pitch:h * pitch + rows, :].astype(BF)
    def bslot(dev):
        return ball.at[:, ds8(dev * rows, rows, 16), :]

    pc.meet()
    pc.to_all(bslot(me), bslot, ssem_b, rsem_b)
    for cp in loads[2:]:
        cp.wait()
    wot[:] = wo_ref[:].astype(F32).T.astype(BF)
    rid = lax.broadcasted_iota(jnp.int32, (16, 2 * nres), 0)
    lid = lax.broadcasted_iota(jnp.int32, (16, 2 * nres), 1)
    diag = (rid < 8) == (lid < nres)

    def lnorm(t):
        xbuf[t] = norm(jnp.concatenate([m_ref[2 * t].astype(F32), m_ref[2 * t + 1].astype(F32)], axis=1), 0)
    loop(nseq // 2, lnorm, 2)

    def project(t):
        s0 = t * 2
        proj = dot(wqkvg_ref[:], xbuf[t])
        gbuf[t] = proj[3 * chan:4 * chan, :].astype(BF)
        for s in range(2):
            sl = slice(s * nres, (s + 1) * nres)
            mk = mask_ref[pl.ds(base + s0 + s, 1), :].astype(F32) - 1.0
            kaug = jnp.concatenate([proj[chan:2 * chan, sl], jnp.broadcast_to(mk, (nres - chan, nres))], axis=0)
            klhs[s0 + s] = kaug.T.astype(BF)
            vbuf[s0 + s] = proj[2 * chan:3 * chan, sl].astype(BF)
            for p in range(heads // 2):
                q16 = proj[16 * p:16 * p + 16, sl]
                qblk[s0 + s, 16 * p:16 * p + 16, :] = jnp.where(diag, jnp.concatenate([q16, q16], axis=1), 0.0).astype(BF)
    loop(nseq // 2, project, 2)
    pc.from_all(bslot, rsem_b)
    for h in range(heads):
        bias[:, h * nres:(h + 1) * nres] = ball[h].astype(F32).T * LOG2E

    hi, mid, lo = split3(1e4 / scale)
    rid = lax.broadcasted_iota(jnp.int32, (16, 2 * nres), 0)
    lid = lax.broadcasted_iota(jnp.int32, (16, 2 * nres), 1)
    aug = jnp.where(rid == 0, hi, jnp.where(rid == 1, mid, jnp.where(rid == 2, lo, 0.0))).astype(BF)

    npair = nseq // 2
    half = heads // 2
    wide = 2 * nres

    def qk(t, u):
        s, p = u // half, u % half
        parts = []
        if p > 0:
            parts.append(jnp.zeros((16 * p, wide), BF))
        parts.append(qblk[t * 2 + s, 16 * p:16 * p + 16, :])
        if chan - 16 * p - 16 > 0:
            parts.append(jnp.zeros((chan - 16 * p - 16, wide), BF))
        parts.append(aug)
        l = dot(klhs[t * 2 + s, :, :chan + 16], jnp.concatenate(parts, axis=0)) * (scale * LOG2E) + bias[:, wide * p:wide * p + wide]
        lbuf[u] = l
        mbuf[u, 0:1, :] = jnp.max(l, axis=0, keepdims=True)

    def ex(u):
        e = jnp.exp2(lbuf[u] - mbuf[u, 0:1, :])
        pbuf[u] = e.astype(BF)
        rbuf[u, 0:1, :] = 1.0 / jnp.sum(e, axis=0, keepdims=True)

    def pv(t, u):
        s, p = u // half, u % half
        o = dot(vbuf[t * 2 + s, 16 * p:16 * p + 16, :], pbuf[u])
        sl = slice(s * nres, (s + 1) * nres)
        obuf[t, 16 * p:16 * p + 8, sl] = o[:8, :nres] * rbuf[u, 0:1, :nres]
        obuf[t, 16 * p + 8:16 * p + 16, sl] = o[8:16, nres:] * rbuf[u, 0:1, nres:]

    units = 2 * half
    for u in range(units):
        qk(0, u)

    def row_pair(t):
        tn = jnp.minimum(t + 1, npair - 1)
        for u in range(units):
            ex(u)
            qk(tn, u)
            if u > 0:
                pv(t, u - 1)
        pv(t, units - 1)
    loop(npair, row_pair)

    def finish(t):
        s0 = t * 2
        mv = jnp.concatenate([m_ref[s0].astype(F32), m_ref[s0 + 1].astype(F32)], axis=1)
        y = (sigmoid(gbuf[t].astype(F32)) * obuf[t]).astype(BF)
        m1 = (mv + dot(wot[:], y)).astype(BF)
        for s in range(2):
            m1_ref[s0 + s] = m1[:, s * nres:(s + 1) * nres]
    loop(npair, finish, 4)

    def renorm(t, acc):
        s0 = t * 2
        m1 = jnp.concatenate([m1_ref[s0].astype(F32), m1_ref[s0 + 1].astype(F32)], axis=1)
        x2 = norm(m1, 0)
        for s in range(2):
            sl = slice(s * nres, (s + 1) * nres)
            x2_ref[s0 + s] = x2[:, sl]
            acc = acc + mask_ref[pl.ds(base + s0 + s, 1), :].astype(F32) * x2[:, sl].astype(F32)
        return acc
    qpart[me] = lax.fori_loop(0, npair, renorm, jnp.zeros((chan, nres), F32), unroll=2)

    halfq = chan // 2
    qslots = (lambda dev: qpart.at[dev]), (lambda dev: qpart.at[dev, :halfq]), (lambda dev: qpart.at[dev, halfq:])
    pc.spread(qpart.at[me], qslots[0], ssem_q, rsem_q)

    def keyval(t):
        s0 = t * 2
        xv = jnp.concatenate([x2_ref[s0], x2_ref[s0 + 1]], axis=1)
        kvp = rnd(dot(wkv_ref[:], xv))
        g2_ref[t] = dot(wg2_ref[:], xv).astype(BF)
        for s in range(2):
            kv[s0 + s] = kvp[:, s * nres:(s + 1) * nres]
    loop(npair, keyval, 4)
    count = jnp.sum(mask_ref[:].astype(F32), axis=0, keepdims=True) + 1e-10
    pc.spread_relay(*qslots, ssem_q, rsem_q)
    pc.spread_wait(*qslots, ssem_q, rsem_q)
    tot = qpart[0]
    for d in range(1, n):
        tot = tot + qpart[d]
    tmp[:] = rnd(dot(wq2_ref[:], (tot / count).astype(BF)))
    qd = [tmp[pl.ds(d, heads, stride=hd), :] for d in range(hd)]
    unroll = 8

    def logit(t, mx):
        for u in range(unroll):
            s = t * unroll + u
            row = kv.at[s]
            l = qd[0] * row[0:1, :]
            for d in range(1, hd):
                l = l + qd[d] * row[d:d + 1, :]
            l = l * scale + (mask_ref[pl.ds(base + s, 1), :].astype(F32) - 1.0) * 1e4
            lg[s] = l
            mx = jnp.maximum(mx, l)
        return mx
    mx = lax.fori_loop(0, nseq // unroll, logit, jnp.full((heads, nres), -jnp.inf, F32))

    def weigh(t, carry):
        ssum, acc = carry
        acc = list(acc)
        for u in range(unroll):
            s = t * unroll + u
            row = kv.at[s]
            e = jnp.exp(lg[s] - mx)
            ssum = ssum + e
            eb = rnd(e)
            for d in range(hd):
                acc[d] = acc[d] + eb * row[hd + d:hd + d + 1, :]
        return ssum, tuple(acc)
    zero = jnp.zeros((heads, nres), F32)
    ssum, acc = lax.fori_loop(0, nseq // unroll, weigh, (zero, (zero,) * hd))
    ppart[me, :8, :] = mx
    ppart[me, 8:16, :] = ssum
    for d in range(hd):
        ppart[me, 16 + 8 * d:24 + 8 * d, :] = acc[d]
    halfp = 8 + chan // 2
    pslots = (lambda dev: ppart.at[dev]), (lambda dev: ppart.at[dev, :halfp]), (lambda dev: ppart.at[dev, halfp:])
    pc.spread(ppart.at[me], pslots[0], ssem_p, rsem_p)
    pc.spread_relay(*pslots, ssem_p, rsem_p)
    pc.spread_wait(*pslots, ssem_p, rsem_p)
    top = ppart[0, :8, :]
    for d in range(1, n):
        top = jnp.maximum(top, ppart[d, :8, :])
    fac = [jnp.exp(ppart[d, :8, :] - top) for d in range(n)]
    den = fac[0] * ppart[0, 8:16, :]
    for d in range(1, n):
        den = den + fac[d] * ppart[d, 8:16, :]
    inv = 1.0 / den
    for c in range(hd):
        o = fac[0] * ppart[0, 16 + 8 * c:24 + 8 * c, :]
        for d in range(1, n):
            o = o + fac[d] * ppart[d, 16 + 8 * c:24 + 8 * c, :]
        o2_ref[pl.ds(c, heads, stride=hd), :] = o * inv
    pc.drain()


def msa_call(n, mask, mt, z, wb, wqkvg, wo, wq2, wkv, wg2):
    nseq, chan, nres = mt.shape
    rows = z.shape[0]
    heads = wb.shape[0]
    dma = pltpu.SemaphoreType.DMA((n,))
    dma9 = pltpu.SemaphoreType.DMA((9,))
    args = [pltpu.with_memory_space_constraint(v, pltpu.HBM) for v in (z, wb, mask, mt, wqkvg, wo, wq2, wkv, wg2)]
    return pl.pallas_call(
        functools.partial(msa_kernel, n, len(args)),
        name="msa",
        out_shape=[jax.ShapeDtypeStruct((nseq, chan, nres), BF), jax.ShapeDtypeStruct((nseq // 2, chan, 2 * nres), BF),
                   jax.ShapeDtypeStruct((chan, nres), F32)],
        in_specs=[pl.BlockSpec(memory_space=pltpu.HBM)] * len(args),
        out_specs=[VM] * 3,
        scratch_shapes=[pltpu.VMEM(v.shape, v.dtype) for v in args] + [
            dma9,
            pltpu.VMEM((heads, n * rows, nres), BF),
            pltpu.VMEM((nres, heads * nres), F32),
            pltpu.VMEM((heads * (rows + 8), nres), F32),
            pltpu.VMEM((nseq, wkv.shape[0], nres), F32),
            pltpu.VMEM((nseq, heads, nres), F32),
            pltpu.VMEM((chan, chan), BF),
            pltpu.VMEM((n, chan, nres), F32),
            pltpu.VMEM((n, chan + 16, nres), F32),
            pltpu.VMEM((chan, nres), F32),
            pltpu.VMEM((nseq, chan, nres), BF),
            pltpu.VMEM((nseq // 2, chan, 2 * nres), BF),
            pltpu.VMEM((nseq, nres, nres), BF),
            pltpu.VMEM((nseq, chan, 2 * nres), BF),
            pltpu.VMEM((nseq, chan, nres), BF),
            pltpu.VMEM((nseq // 2, chan, 2 * nres), BF),
            pltpu.VMEM((heads, nres, 2 * nres), F32),
            pltpu.VMEM((heads, 8, 2 * nres), F32),
            pltpu.VMEM((heads, nres, 2 * nres), BF),
            pltpu.VMEM((heads, 8, 2 * nres), F32),
            pltpu.VMEM((nseq // 2, chan, 2 * nres), F32),
            dma, dma, dma9, dma9, dma9, dma9,
        ],
        compiler_params=pltpu.CompilerParams(vmem_limit_bytes=36 * 2 ** 20, collective_id=0, has_side_effects=True),
    )(*args)


def gate_kernel(m1_ref, g2_ref, o2_ref, wo_ref, m2_ref, x_ref, wot):
    nseq, chan, nres = m1_ref.shape
    wot[:] = wo_ref[:].astype(F32).T.astype(BF)

    def gate(t):
        y = (sigmoid(g2_ref[t].astype(F32)) * cat(o2_ref[:], o2_ref[:])).astype(BF)
        m2 = (cat(m1_ref[2 * t].astype(F32), m1_ref[2 * t + 1].astype(F32)) + dot(wot[:], y)).astype(BF)
        for s in range(2):
            m2_ref[2 * t + s] = m2[:, part(s, nres)]
    loop(nseq // 2, gate, 4)

    def renorm(t):
        x_ref[t] = norm(cat(m2_ref[2 * t].astype(F32), m2_ref[2 * t + 1].astype(F32)), 0)
    loop(nseq // 2, renorm, 2)


def gate_call(m1, g2, o2, wo):
    nseq, chan, nres = m1.shape
    return pl.pallas_call(
        gate_kernel,
        name="gate",
        out_shape=[jax.ShapeDtypeStruct(m1.shape, BF), jax.ShapeDtypeStruct(g2.shape, BF)],
        in_specs=[VM] * 4,
        out_specs=[VM] * 2,
        scratch_shapes=[pltpu.VMEM((chan, chan), BF)],
        compiler_params=pltpu.CompilerParams(vmem_limit_bytes=16 * 2 ** 20),
    )(m1, g2, o2, wo)


def tri_attend(pc, zin, wb_ref, wqkvg_ref, wo_ref, maskcol, zln, brow, ball, bias, proj, flat, wot, lbuf, mbuf, pbuf, rbuf, obuf, zrel, tsend, zrecv,
               ssem_b, rsem_b, ssem_t, rsem_t):
    me = pc.me
    rows, nres, chan = zin.shape
    heads = wb_ref.shape[0]
    hd = chan // heads
    scale = hd ** -0.5
    pitch = rows + 8
    mine = ds8(me * rows, rows, 16)

    def bias_row(i):
        zl = norm(zin[i].astype(F32), 1)
        zln[i] = zl
        brow[pl.ds(i, heads, stride=pitch), :] = dot_nt(wb_ref[:], zl)
    loop(rows, bias_row, 4)
    for h in range(heads):
        ball[h, mine, :] = brow[h * pitch:h * pitch + rows, :].astype(BF)

    def bslot(dev):
        return ball.at[:, ds8(dev * rows, rows, 16), :]

    pc.to_all(bslot(me), bslot, ssem_b, rsem_b)
    wot[:] = wo_ref[:].astype(F32).T.astype(BF)

    def project(i):
        zl = zln[i]
        proj[i, :chan, :] = dot_nt(wqkvg_ref[:chan, :], zl).astype(BF)
        proj[i, chan:2 * chan, :] = dot_nt(zl, wqkvg_ref[chan:2 * chan, :]).astype(BF)
        proj[i, 2 * chan:4 * chan, :] = dot_nt(wqkvg_ref[2 * chan:4 * chan, :], zl).astype(BF)
    loop(rows, project, 2)
    pc.from_all(bslot, rsem_b)
    for h in range(heads):
        bias[:, h * nres:(h + 1) * nres] = (ball[h].astype(F32).T + maskcol[:]) * LOG2E
    zero = jnp.zeros((hd, nres), BF)

    half = heads // 2
    wide = 2 * nres

    def qk(i, p, u):
        r0 = 2 * hd * p
        qa = proj[i, r0:r0 + hd, :]
        qb = proj[i, r0 + hd:r0 + 2 * hd, :]
        parts = [jnp.zeros((r0, wide), BF)] if p > 0 else []
        parts.append(jnp.concatenate([qa, zero], axis=1))
        parts.append(jnp.concatenate([zero, qb], axis=1))
        if chan - r0 - 2 * hd > 0:
            parts.append(jnp.zeros((chan - r0 - 2 * hd, wide), BF))
        l = dot(proj[i, chan:2 * chan, :], jnp.concatenate(parts, axis=0)) * (scale * LOG2E) + bias[:, wide * p:wide * p + wide]
        lbuf[u] = l
        mbuf[u, 0:1, :] = jnp.max(l, axis=0, keepdims=True)

    def ex(u):
        e = jnp.exp2(lbuf[u] - mbuf[u, 0:1, :])
        pbuf[u] = e.astype(BF)
        rbuf[u, 0:1, :] = 1.0 / jnp.sum(e, axis=0, keepdims=True)

    def pv(i, p, u):
        r0 = 2 * hd * p
        o = dot(proj[i, 2 * chan + r0:2 * chan + r0 + 2 * hd, :], pbuf[u])
        obuf[i, r0:r0 + hd, :] = o[:hd, :nres] * rbuf[u, 0:1, :nres]
        obuf[i, r0 + hd:r0 + 2 * hd, :] = o[hd:, nres:] * rbuf[u, 0:1, nres:]

    units = [(i, p) for i in range(2) for p in range(half)]
    for u, (i, p) in enumerate(units):
        qk(i, p, u)

    def attend(t):
        nxt = jnp.minimum(2 * t + 2, rows - 2)
        for u, (i, p) in enumerate(units):
            ex(u)
            qk(nxt + i, p, u)
            if u > 0:
                pv(2 * t + units[u - 1][0], units[u - 1][1], u - 1)
        pv(2 * t + units[-1][0], units[-1][1], len(units) - 1)
    loop(rows // 2, attend)

    def finish(i):
        y = (sigmoid(proj[i, 3 * chan:4 * chan, :].astype(F32)) * obuf[i]).astype(BF)
        upd = dot(wot[:], y).T
        flat[pl.ds(i, nres, stride=pitch), :] = zin[i].astype(F32) + upd
    loop(rows, finish, 4)

    def regroup(j):
        tsend[j] = flat[ds8(j * pitch, rows), :].astype(BF)
    loop(nres, regroup, 4)

    def tblk(dev):
        return tsend.at[pl.ds(dev * rows, rows)]

    def tslot(dev):
        return zrecv.at[:, ds8(dev * rows, rows, 16), :]

    pc.scatter(tblk, tslot, zrel, ssem_t, rsem_t)
    zrecv[:, mine, :] = tsend[pl.ds(me * rows, rows)]
    pc.scatter_relay(tslot, zrel, ssem_t, rsem_t)
    pc.scatter_wait(tslot, rsem_t)


def pair_kernel(n, nchunk, mask_ref, x_ref, z_ref, rm_ref, wproj_ref, wopm_ref, wb1_ref, wqkvg1_ref, wo1_ref, wb2_ref, wqkvg2_ref, wo2_ref,
                zo_ref,
                ac, at, w32, wt, cbuf, asend, csend, call, apack, arel, aall, upd, osc, z1, zln, brow, ball1, ball2, bias, proj, flat, wot,
                lbuf, mbuf, pbuf, rbuf, obuf, maskcol, tsend1, tsend2, zrel1, zrel2, zmid, zfin,
                ssem_a, rsem_a, ssem_c, rsem_c, ssem_b1, rsem_b1, ssem_t1, rsem_t1, ssem_b2, rsem_b2, ssem_t2, rsem_t2):
    pc = Place(n)
    me = pc.me
    pc.signal()
    rows, nres, chan = z_ref.shape
    nf, nseq = csend.shape[0:2]
    ne = nf
    fq = nf // nchunk
    hq = fq // 2
    lane = lax.broadcasted_iota(jnp.int32, (nres, nres), 1)
    pitch = ac.shape[0] // nseq
    pitch2 = at.shape[0] // nres

    def project(t):
        pr = rnd(dot(wproj_ref[:], x_ref[t]))
        for s in range(2):
            mk = mask_ref[pl.ds(me * nseq + 2 * t + s, 1), :].astype(F32)
            ac[ds8((2 * t + s) * pitch, 2 * ne), :] = pr[:, part(s, nres)] * mk
    loop(nseq // 2, project, 4)
    pad = jnp.zeros((nres - nseq, nres), F32)

    def plane(e):
        at[pl.ds(e, nres, stride=pitch2), :] = stack(ac[pl.ds(e, nseq, stride=pitch), :], pad).T
    loop(ne, plane, 4)
    blocks = rows * ne // nres
    per = nres // ne

    def pack(d):
        v = [stack(*[at[ds8((d * rows + b * per + u) * pitch2, ne), :] for u in range(per)]) for b in range(blocks)]
        for r in range(blocks - 1):
            asend[d, part(r, nres), :] = jnp.where(lane >= nseq, pltpu.roll(v[-1], nseq - r * (nres - nseq), 1), v[r]).astype(BF)
    loop(n, pack)
    pc.meet()

    def aslot(dev):
        return apack.at[dev]

    pc.scatter(lambda dev: asend.at[dev], aslot, arel, ssem_a, rsem_a)

    def cslots(q):
        def slot(lo, size):
            return lambda dev: call.at[pl.ds(q * fq + lo, size), dev, :nseq, :]
        return slot(0, fq), slot(0, hq), slot(hq, hq)

    def own(q):
        for f in range(q * fq, q * fq + fq):
            v = ac[pl.ds(ne + f, nseq, stride=pitch), :].astype(BF)
            csend[f] = v
            call[f, me, :nseq, :] = v
        pc.spread(csend.at[pl.ds(q * fq, fq)], cslots(q)[0], ssem_c.at[q], rsem_c.at[q])

    def neighbours(q):
        pc.spread_relay(*cslots(q), ssem_c.at[q], rsem_c.at[q])
        if q + 2 < nchunk:
            own(q + 2)

    own(0)
    own(1)
    apack[me] = asend[me]
    pc.scatter_relay(aslot, arel, ssem_a, rsem_a)
    neighbours(0)
    padz = jnp.zeros((call.shape[1], call.shape[2] - nseq, nres), BF)

    def fill(f):
        call[f, :, nseq:, :] = padz
    loop(nf, fill)
    maskcol[:] = jnp.broadcast_to((rm_ref[:].astype(F32) - 1.0) * 1e4, (nres, nres)).T
    mbf = mask_ref[:].astype(F32).astype(BF)
    cbuf[:] = lax.dot_general(mbf, mbf, (((0,), (0,)), ((), ())), preferred_element_type=F32)
    w32[:] = wopm_ref[:].astype(F32)
    for g in range(nf // per):
        wt[:, part(g, nres)] = stack(*[w32[pl.ds(g * per + u, ne, stride=nf), :] for u in range(per)]).T.astype(BF)
    neighbours(1)
    pc.scatter_wait(aslot, rsem_a)

    def unpack(d):
        last = jnp.zeros((nres, nres), F32)
        for r in range(blocks - 1):
            v = apack[d, part(r, nres), :].astype(F32)
            aall[d, part(r, nres), :] = jnp.where(lane < nseq, v, 0.0).astype(BF)
            moved = pltpu.roll(v, (r + 1) * (nres - nseq), 1)
            last = last + jnp.where((lane >= r * (nres - nseq)) & (lane < (r + 1) * (nres - nseq)), moved, 0.0)
        aall[d, part(blocks - 1, nres), :] = last.astype(BF)
    loop(n, unpack)

    for q in range(nchunk):
        pc.spread_wait(*cslots(q), ssem_c.at[q], rsem_c.at[q])

        def outer(g):
            acc = None
            for kk in range(n // 2):
                rhs = jnp.concatenate(
                    [jnp.concatenate([call[q * fq + 2 * g + u, 2 * kk], call[q * fq + 2 * g + u, 2 * kk + 1]], axis=0) for u in range(2)],
                    axis=1)
                lhs = jnp.concatenate([aall[2 * kk], aall[2 * kk + 1]], axis=1)
                step = dot(lhs, rhs)
                acc = step if acc is None else acc + step
            ob = acc.astype(BF)
            for u in range(2):
                for i in range(rows):
                    osc[i, ds8((2 * g + u) * ne, ne, 32), :] = ob[i * ne:(i + 1) * ne, u * nres:(u + 1) * nres]
        loop(fq // 2, outer)

        def contract(g):
            rhs = jnp.concatenate([osc[2 * g], osc[2 * g + 1]], axis=1)
            step = dot(wt[:, part(q, fq * ne)], rhs)
            for u in range(2):
                v = step[:, part(u, nres)]
                upd[2 * g + u] = v if q == 0 else upd[2 * g + u] + v
        loop(rows // 2, contract, 2)
        if q + 2 < nchunk:
            neighbours(q + 2)

    def residual(i):
        u = upd[i] / (1e-3 + cbuf[pl.ds(me * rows + i, 1), :])
        z1[i] = (z_ref[i].astype(F32) + u.T).astype(BF)
    loop(rows, residual, 2)

    for zin, wb, wq, wo, ball, ts, zrel, zout, sems in (
            (z1, wb1_ref, wqkvg1_ref, wo1_ref, ball1, tsend1, zrel1, zmid, (ssem_b1, rsem_b1, ssem_t1, rsem_t1)),
            (zmid, wb2_ref, wqkvg2_ref, wo2_ref, ball2, tsend2, zrel2, zfin, (ssem_b2, rsem_b2, ssem_t2, rsem_t2))):
        tri_attend(pc, zin, wb, wq, wo, maskcol, zln, brow, ball, bias, proj, flat, wot, lbuf, mbuf, pbuf, rbuf, obuf, zrel, ts, zout, *sems)
    zo_ref[:] = zfin[:]
    pc.drain()


def pair_call(n, mask, x, z, rm, wproj, wopm, wb1, wqkvg1, wo1, wb2, wqkvg2, wo2):
    rows, nres, chan = z.shape
    nseq = 2 * x.shape[0]
    ne = wproj.shape[0] // 2
    heads = wb1.shape[0]
    nchunk = 4
    fq = ne // nchunk
    dma = pltpu.SemaphoreType.DMA((n,))
    dma9 = pltpu.SemaphoreType.DMA((9,))
    dmac = pltpu.SemaphoreType.DMA((nchunk, 9))
    pitch = rows + 8
    vz = pltpu.VMEM((rows, nres, chan), BF)
    fz = pltpu.VMEM((rows, chan, nres), F32)
    sq = pltpu.VMEM((nres, nres), F32)
    vb = pltpu.VMEM((heads, n * rows, nres), BF)
    vt = pltpu.VMEM((nres, rows, chan), BF)
    vr = pltpu.VMEM((2, rows, rows, chan), BF)
    apk = rows * ne * nseq // nres
    row8 = pltpu.VMEM((heads, 8, 2 * nres), F32)
    args = (mask, x, z, rm, wproj, wopm, wb1, wqkvg1, wo1, wb2, wqkvg2, wo2)
    return pl.pallas_call(
        functools.partial(pair_kernel, n, nchunk),
        name="pair",
        out_shape=jax.ShapeDtypeStruct(z.shape, BF),
        in_specs=[VM] * len(args),
        out_specs=VM,
        scratch_shapes=[
            pltpu.VMEM((nseq * (2 * ne + 8), nres), F32),
            pltpu.VMEM((nres * (ne + 8), nres), F32),
            pltpu.VMEM(wopm.shape, F32),
            pltpu.VMEM(wopm.shape[::-1], BF),
            sq,
            pltpu.VMEM((n, apk, nres), BF),
            pltpu.VMEM((ne, nseq, nres), BF),
            pltpu.VMEM((ne, n, nres, nres), BF),
            pltpu.VMEM((n, apk, nres), BF),
            pltpu.VMEM((2, apk, nres), BF),
            pltpu.VMEM((n, rows * ne, nres), BF),
            fz,
            pltpu.VMEM((rows, fq * ne, nres), BF),
            vz, vz,
            pltpu.VMEM((heads * pitch, nres), F32),
            vb, vb,
            pltpu.VMEM((nres, heads * nres), F32),
            pltpu.VMEM((rows, 4 * chan, nres), BF),
            pltpu.VMEM((nres * pitch, chan), F32),
            pltpu.VMEM((chan, chan), BF),
            pltpu.VMEM((heads, nres, 2 * nres), F32), row8, pltpu.VMEM((heads, nres, 2 * nres), BF), row8,
            fz, sq, vt, vt, vr, vr, vz, vz,
            dma9, dma9, dmac, dmac, dma, dma, dma9, dma9, dma, dma, dma9, dma9,
        ],
        compiler_params=pltpu.CompilerParams(vmem_limit_bytes=40 * 2 ** 20, collective_id=1, has_side_effects=True),
    )(*args)


def flat_t(w):
    return jnp.moveaxis(w, 0, -1).reshape(-1, w.shape[0])


def solution(mesh):
    n = mesh.shape["dap"]

    def block(msa, pair, msa_mask, res_mask, row_bias_w, row_qkvg_w, row_out_w, col_query_w, col_kv_w, col_gate_w, col_out_w,
              opm_proj_w, opm_out_w, start_bias_w, start_qkvg_w, start_out_w, end_bias_w, end_qkvg_w, end_out_w):
        nseq, nres, chan = msa.shape
        pdim = pair.shape[2]
        mt = jnp.transpose(msa, (0, 2, 1))
        m1, g2, o2 = msa_call(n, msa_mask, mt, pair, row_bias_w.T, flat_t(row_qkvg_w), row_out_w.reshape(chan, chan),
                              flat_t(col_query_w), flat_t(col_kv_w), flat_t(col_gate_w))
        m2, x3 = gate_call(m1, g2, o2, col_out_w.reshape(chan, chan))
        zo = pair_call(n, msa_mask, x3, pair, res_mask.reshape(1, nres), flat_t(opm_proj_w), opm_out_w.reshape(-1, pdim),
                       start_bias_w.T, flat_t(start_qkvg_w), start_out_w.reshape(pdim, pdim),
                       end_bias_w.T, flat_t(end_qkvg_w), end_out_w.reshape(pdim, pdim))
        return jnp.transpose(m2, (0, 2, 1)), zo

    row_spec = P(('data', 'dap'), None, None)
    in_specs = (row_spec, row_spec, P('data', None), P('data')) + (P(),) * 15
    return jax.shard_map(block, mesh=mesh, in_specs=in_specs, out_specs=(row_spec, row_spec), check_vma=False)
```

time: 155 us -> 140 us (0.903)
  Pallas kernels: 149 us -> 139 us
  local copies, waits for them, and re-layouts: 4.28 us -> 0.87 us
    pallas_call x1, Pallas kernels: 11.6 us -> 5.22 us  [gate_call(): pl.pallas_call(gate_kernel, name='gate', out_shape=[jax.ShapeDtypeStruct(...]
    pallas_call x1, Pallas kernels: 51.3 us -> 49.2 us  [msa_call(): pl.pallas_call(functools.partial(msa_kernel, n, len(args)), name='msa', o...]
    pallas_call x1, Pallas kernels: 86 us -> 84.3 us  [pair_call(): pl.pallas_call(functools.partial(pair_kernel, n, nchunk), name='pair', ou...]
where the time goes in v3:
time: 140 us
  Pallas kernels  139 us (99%)
    pallas_call x1, Pallas kernels, pair_call(): pl.pallas_call(functools.partial(pair_kernel, n, nchunk), name='pair', ou...  84.3 us
    pallas_call x1, Pallas kernels, msa_call(): pl.pallas_call(functools.partial(msa_kernel, n, len(args)), name='msa', o...  49.2 us
    pallas_call x1, Pallas kernels, gate_call(): pl.pallas_call(gate_kernel, name='gate', out_shape=[jax.ShapeDtypeStruct(...  5.22 us

profile of v3, /device:TPU:81, one launch (start us, length us, event | category | flops | bytes accessed | tf_op | source)
XLA Modules:
  0.0 140.4 jit_solution(13655521774074040647)
XLA Ops:
  0.6 0.0 copy-start.7
  0.6 49.2 %msa.1 = (bf16[96,64,128]{2,1,0:T(8,128)(2,1)S(1)}, bf16[48,64,256]{2,1,0:T(8,128)(2,1)S(1)}, f32[64,128]{1,0:T(8,128)S(1)}) custom-call(bf16[16,128,128]{2,1,0:T(8,128)(2,1)} %z_ref.1, bf16[8,128]{1,0:T(8,128)(2,1)} %bitcast.48, s32[768,128]{1,0:T(8,128)} %mask_ref.1, bf16[96,64,128]{2,1,0:T(8,128)(2,1)} %bitcast.42, bf16[256,64]{1,0:T(8,128)(2,1)} %bitcast.43, ...), custom_call_target="tpu_custom_call" | custom-call | tf_op jit(solution)/shard_map/msa/pallas_call | solution.py:376
  49.8 0.0 copy-done.7
  49.8 0.0 copy-start
  49.9 0.0 copy-start.1
  49.9 0.0 copy-start.2
  49.9 0.0 copy-start.3
  49.9 0.0 copy-start.4
  49.9 0.0 copy-start.5
  49.9 0.0 copy-start.6
  49.9 0.0 copy-start.8
  49.9 0.0 copy-start.9
  50.0 0.0 copy-start.10
  50.0 0.0 copy-start.11
  50.0 5.2 %gate.1 = (bf16[96,64,128]{2,1,0:T(8,128)(2,1)}, bf16[48,64,256]{2,1,0:T(8,128)(2,1)S(1)}) custom-call(bf16[96,64,128]{2,1,0:T(8,128)(2,1)S(1)} %get-tuple-element.7.m1_ref, bf16[48,64,256]{2,1,0:T(8,128)(2,1)S(1)} %get-tuple-element.8.g2_ref, f32[64,128]{1,0:T(8,128)S(1)} %get-tuple-element.9.o2_ref, bf16[64,64]{1,0:T(8,128)(2,1)S(1)} %bitcast.37), custom_call_target="tpu_custom_call" | custom-call | tf_op jit(solution)/shard_map/gate/pallas_call | solution.py:429
  55.2 0.0 copy-done
  55.2 0.0 copy-done.1
  55.2 0.0 copy-done.2
  55.2 0.0 copy-done.3
  55.2 0.0 copy-done.4
  55.2 0.0 copy-done.5
  55.2 0.0 copy-done.6
  55.2 0.0 copy-done.8
  55.3 0.0 copy-done.9
  55.3 0.0 copy-done.10
  55.3 0.0 copy-done.11
  55.3 84.3 %pair.1 = bf16[16,128,128]{2,1,0:T(8,128)(2,1)S(1)} custom-call(s32[768,128]{1,0:T(8,128)S(1)} %copy-done.1, bf16[48,64,256]{2,1,0:T(8,128)(2,1)S(1)} %get-tuple-element.11.x_ref, bf16[16,128,128]{2,1,0:T(8,128)(2,1)S(1)} %copy-done, s32[1,128]{1,0:T(1,128)S(1)} %bitcast.41, bf16[64,64]{1,0:T(8,128)(2,1)S(1)} %bitcast.38, bf16[1024,128]{1,0:T(8,128)(2,1)S(1)} %bitcast.32, ...), custom_call_target="tpu_custom_call" | custom-call | tf_op jit(solution)/shard_map/pair/pallas_call | solution.py:688
  139.6 0.8 copy.22
Async XLA Ops:
  0.6 49.2 %copy-start.7 = (bf16[8,8,64]{2,1,0:T(8,128)(2,1)S(1)}, bf16[8,8,64]{2,1,0:T(8,128)(2,1)}, u32[]{:S(2)}) copy-start(bf16[8,8,64]{2,1,0:T(8,128)(2,1)} %param.29) | copy-start | bytes 24580
  49.8 5.4 %copy-start = (bf16[16,128,128]{2,1,0:T(8,128)(2,1)S(1)}, bf16[16,128,128]{2,1,0:T(8,128)(2,1)}, u32[]{:S(2)}) copy-start(bf16[16,128,128]{2,1,0:T(8,128)(2,1)} %z_ref.1) | copy-start | bytes 1572868
  49.9 5.3 %copy-start.1 = (s32[768,128]{1,0:T(8,128)S(1)}, s32[768,128]{1,0:T(8,128)}, u32[]{:S(2)}) copy-start(s32[768,128]{1,0:T(8,128)} %mask_ref.1) | copy-start | bytes 1179652
  49.9 5.3 %copy-start.2 = (bf16[32,32,128]{2,1,0:T(8,128)(2,1)S(1)}, bf16[32,32,128]{2,1,0:T(8,128)(2,1)}, u32[]{:S(2)}) copy-start(bf16[32,32,128]{2,1,0:T(8,128)(2,1)} %param.31) | copy-start | bytes 786436
  49.9 5.3 %copy-start.3 = (bf16[128,4,4,32]{0,3,2,1:T(8,128)(2,1)S(1)}, bf16[128,4,4,32]{0,3,2,1:T(8,128)(2,1)}, u32[]{:S(2)}) copy-start(bf16[128,4,4,32]{0,3,2,1:T(8,128)(2,1)} %param.33) | copy-start | bytes 393220
  49.9 5.3 %copy-start.4 = (bf16[128,4,4,32]{0,3,2,1:T(8,128)(2,1)S(1)}, bf16[128,4,4,32]{0,3,2,1:T(8,128)(2,1)}, u32[]{:S(2)}) copy-start(bf16[128,4,4,32]{0,3,2,1:T(8,128)(2,1)} %param.36) | copy-start | bytes 393220
  49.9 5.3 %copy-start.5 = (bf16[4,32,128]{2,1,0:T(8,128)(2,1)S(1)}, bf16[4,32,128]{2,1,0:T(8,128)(2,1)}, u32[]{:S(2)}) copy-start(bf16[4,32,128]{2,1,0:T(8,128)(2,1)} %param.34) | copy-start | bytes 98308
  49.9 5.3 %copy-start.6 = (bf16[4,32,128]{2,1,0:T(8,128)(2,1)S(1)}, bf16[4,32,128]{2,1,0:T(8,128)(2,1)}, u32[]{:S(2)}) copy-start(bf16[4,32,128]{2,1,0:T(8,128)(2,1)} %param.37) | copy-start | bytes 98308
  49.9 5.3 %copy-start.8 = (bf16[64,2,32]{0,2,1:T(8,128)(2,1)S(1)}, bf16[64,2,32]{0,2,1:T(8,128)(2,1)}, u32[]{:S(2)}) copy-start(bf16[64,2,32]{0,2,1:T(8,128)(2,1)} %param.30) | copy-start | bytes 24580
  49.9 5.3 %copy-start.9 = (bf16[128,4]{0,1:T(4,128)(2,1)S(1)}, bf16[128,4]{0,1:T(4,128)(2,1)}, u32[]{:S(2)}) copy-start(bf16[128,4]{0,1:T(4,128)(2,1)} %param.32) | copy-start | bytes 3076
  50.0 5.3 %copy-start.10 = (bf16[128,4]{0,1:T(4,128)(2,1)S(1)}, bf16[128,4]{0,1:T(4,128)(2,1)}, u32[]{:S(2)}) copy-start(bf16[128,4]{0,1:T(4,128)(2,1)} %param.35) | copy-start | bytes 3076
  50.0 5.3 %copy-start.11 = (s32[128]{0:T(128)S(1)}, s32[128]{0:T(128)}, u32[]{:S(2)}) copy-start(s32[128]{0:T(128)} %param.22) | copy-start | bytes 1540

commit v4 on v3

--- a/solution.py
+++ b/solution.py
@@ -33,6 +33,14 @@
     cen = v - mean
     var = jnp.mean(cen * cen, axis=axis, keepdims=True)
     return (cen * lax.rsqrt(var + 1e-5)).astype(BF)
+
+
+def peak(v):
+    return jnp.max(v, axis=0, keepdims=True)
+
+
+def total(v):
+    return jnp.sum(v, axis=0, keepdims=True)
 
 
 def sigmoid(v):
@@ -99,7 +107,7 @@
             cp.wait_send()
 
     def to_all(self, src, slot, ssem, rsem):
-        for d in range(1, self.n):
+        for d in sorted(range(1, self.n), key=lambda d: -min(d, self.n - d)):
             self.go(src, slot(self.me), ssem.at[d], rsem.at[d], lax.rem(self.me + d, self.n))
 
     def from_all(self, slot, rsem):
@@ -186,7 +194,7 @@
     def bias_row(i):
         b = dot_nt(wb_ref[:], norm(z_ref[i].astype(F32), 1))
         brow[pl.ds(i, heads, stride=pitch), :] = b
-    loop(rows, bias_row, 4)
+    loop(rows, bias_row, rows)
     mine = ds8(me * rows, rows, 16)
     for h in range(heads):
         ball[h, mine, :] = brow[h * pitch:h * pitch + rows, :].astype(BF)
@@ -204,14 +212,14 @@
 
     def lnorm(t):
         xbuf[t] = norm(jnp.concatenate([m_ref[2 * t].astype(F32), m_ref[2 * t + 1].astype(F32)], axis=1), 0)
-    loop(nseq // 2, lnorm, 2)
+    loop(nseq // 2, lnorm, 4)
 
     def project(t):
         s0 = t * 2
         proj = dot(wqkvg_ref[:], xbuf[t])
         gbuf[t] = proj[3 * chan:4 * chan, :].astype(BF)
         for s in range(2):
-            sl = slice(s * nres, (s + 1) * nres)
+            sl = part(s, nres)
             mk = mask_ref[pl.ds(base + s0 + s, 1), :].astype(F32) - 1.0
             kaug = jnp.concatenate([proj[chan:2 * chan, sl], jnp.broadcast_to(mk, (nres - chan, nres))], axis=0)
             klhs[s0 + s] = kaug.T.astype(BF)
@@ -219,10 +227,10 @@
             for p in range(heads // 2):
                 q16 = proj[16 * p:16 * p + 16, sl]
                 qblk[s0 + s, 16 * p:16 * p + 16, :] = jnp.where(diag, jnp.concatenate([q16, q16], axis=1), 0.0).astype(BF)
-    loop(nseq // 2, project, 2)
+    loop(nseq // 2, project, 8)
     pc.from_all(bslot, rsem_b)
     for h in range(heads):
-        bias[:, h * nres:(h + 1) * nres] = ball[h].astype(F32).T * LOG2E
+        bias[:, part(h, nres)] = ball[h].astype(F32).T * LOG2E
 
     hi, mid, lo = split3(1e4 / scale)
     rid = lax.broadcasted_iota(jnp.int32, (16, 2 * nres), 0)
@@ -242,19 +250,19 @@
         if chan - 16 * p - 16 > 0:
             parts.append(jnp.zeros((chan - 16 * p - 16, wide), BF))
         parts.append(aug)
-        l = dot(klhs[t * 2 + s, :, :chan + 16], jnp.concatenate(parts, axis=0)) * (scale * LOG2E) + bias[:, wide * p:wide * p + wide]
+        l = dot(klhs[t * 2 + s, :, :chan + 16], jnp.concatenate(parts, axis=0)) * (scale * LOG2E) + bias[:, part(p, wide)]
         lbuf[u] = l
-        mbuf[u, 0:1, :] = jnp.max(l, axis=0, keepdims=True)
+        mbuf[u, 0:1, :] = peak(l)
 
     def ex(u):
         e = jnp.exp2(lbuf[u] - mbuf[u, 0:1, :])
         pbuf[u] = e.astype(BF)
-        rbuf[u, 0:1, :] = 1.0 / jnp.sum(e, axis=0, keepdims=True)
+        rbuf[u, 0:1, :] = 1.0 / total(e)
 
     def pv(t, u):
         s, p = u // half, u % half
         o = dot(vbuf[t * 2 + s, 16 * p:16 * p + 16, :], pbuf[u])
-        sl = slice(s * nres, (s + 1) * nres)
+        sl = part(s, nres)
         obuf[t, 16 * p:16 * p + 8, sl] = o[:8, :nres] * rbuf[u, 0:1, :nres]
         obuf[t, 16 * p + 8:16 * p + 16, sl] = o[8:16, nres:] * rbuf[u, 0:1, nres:]
 
@@ -270,7 +278,7 @@
             if u > 0:
                 pv(t, u - 1)
         pv(t, units - 1)
-    loop(npair, row_pair)
+    loop(npair, row_pair, 2)
 
     def finish(t):
         s0 = t * 2
@@ -278,15 +286,15 @@
         y = (sigmoid(gbuf[t].astype(F32)) * obuf[t]).astype(BF)
         m1 = (mv + dot(wot[:], y)).astype(BF)
         for s in range(2):
-            m1_ref[s0 + s] = m1[:, s * nres:(s + 1) * nres]
-    loop(npair, finish, 4)
+            m1_ref[s0 + s] = m1[:, part(s, nres)]
+    loop(npair, finish, 16)
 
     def renorm(t, acc):
         s0 = t * 2
         m1 = jnp.concatenate([m1_ref[s0].astype(F32), m1_ref[s0 + 1].astype(F32)], axis=1)
         x2 = norm(m1, 0)
         for s in range(2):
-            sl = slice(s * nres, (s + 1) * nres)
+            sl = part(s, nres)
             x2_ref[s0 + s] = x2[:, sl]
             acc = acc + mask_ref[pl.ds(base + s0 + s, 1), :].astype(F32) * x2[:, sl].astype(F32)
         return acc
@@ -302,9 +310,9 @@
         kvp = rnd(dot(wkv_ref[:], xv))
         g2_ref[t] = dot(wg2_ref[:], xv).astype(BF)
         for s in range(2):
-            kv[s0 + s] = kvp[:, s * nres:(s + 1) * nres]
-    loop(npair, keyval, 4)
-    count = jnp.sum(mask_ref[:].astype(F32), axis=0, keepdims=True) + 1e-10
+            kv[s0 + s] = kvp[:, part(s, nres)]
+    loop(npair, keyval, 8)
+    count = total(mask_ref[:].astype(F32)) + 1e-10
     pc.spread_relay(*qslots, ssem_q, rsem_q)
     pc.spread_wait(*qslots, ssem_q, rsem_q)
     tot = qpart[0]
@@ -417,7 +425,7 @@
         m2 = (cat(m1_ref[2 * t].astype(F32), m1_ref[2 * t + 1].astype(F32)) + dot(wot[:], y)).astype(BF)
         for s in range(2):
             m2_ref[2 * t + s] = m2[:, part(s, nres)]
-    loop(nseq // 2, gate, 4)
+    loop(nseq // 2, gate, 16)
 
     def renorm(t):
         x_ref[t] = norm(cat(m2_ref[2 * t].astype(F32), m2_ref[2 * t + 1].astype(F32)), 0)
@@ -451,7 +459,7 @@
         zl = norm(zin[i].astype(F32), 1)
         zln[i] = zl
         brow[pl.ds(i, heads, stride=pitch), :] = dot_nt(wb_ref[:], zl)
-    loop(rows, bias_row, 4)
+    loop(rows, bias_row, rows)
     for h in range(heads):
         ball[h, mine, :] = brow[h * pitch:h * pitch + rows, :].astype(BF)
 
@@ -466,10 +474,10 @@
         proj[i, :chan, :] = dot_nt(wqkvg_ref[:chan, :], zl).astype(BF)
         proj[i, chan:2 * chan, :] = dot_nt(zl, wqkvg_ref[chan:2 * chan, :]).astype(BF)
         proj[i, 2 * chan:4 * chan, :] = dot_nt(wqkvg_ref[2 * chan:4 * chan, :], zl).astype(BF)
-    loop(rows, project, 2)
+    loop(rows, project, 8)
     pc.from_all(bslot, rsem_b)
     for h in range(heads):
-        bias[:, h * nres:(h + 1) * nres] = (ball[h].astype(F32).T + maskcol[:]) * LOG2E
+        bias[:, part(h, nres)] = (ball[h].astype(F32).T + maskcol[:]) * LOG2E
     zero = jnp.zeros((hd, nres), BF)
 
     half = heads // 2
@@ -484,14 +492,14 @@
         parts.append(jnp.concatenate([zero, qb], axis=1))
         if chan - r0 - 2 * hd > 0:
             parts.append(jnp.zeros((chan - r0 - 2 * hd, wide), BF))
-        l = dot(proj[i, chan:2 * chan, :], jnp.concatenate(parts, axis=0)) * (scale * LOG2E) + bias[:, wide * p:wide * p + wide]
+        l = dot(proj[i, chan:2 * chan, :], jnp.concatenate(parts, axis=0)) * (scale * LOG2E) + bias[:, part(p, wide)]
         lbuf[u] = l
-        mbuf[u, 0:1, :] = jnp.max(l, axis=0, keepdims=True)
+        mbuf[u, 0:1, :] = peak(l)
 
     def ex(u):
         e = jnp.exp2(lbuf[u] - mbuf[u, 0:1, :])
         pbuf[u] = e.astype(BF)
-        rbuf[u, 0:1, :] = 1.0 / jnp.sum(e, axis=0, keepdims=True)
+        rbuf[u, 0:1, :] = 1.0 / total(e)
 
     def pv(i, p, u):
         r0 = 2 * hd * p
@@ -511,31 +519,34 @@
             if u > 0:
                 pv(2 * t + units[u - 1][0], units[u - 1][1], u - 1)
         pv(2 * t + units[-1][0], units[-1][1], len(units) - 1)
-    loop(rows // 2, attend)
-
     def finish(i):
         y = (sigmoid(proj[i, 3 * chan:4 * chan, :].astype(F32)) * obuf[i]).astype(BF)
         upd = dot(wot[:], y).T
         flat[pl.ds(i, nres, stride=pitch), :] = zin[i].astype(F32) + upd
-    loop(rows, finish, 4)
-
-    def regroup(j):
-        tsend[j] = flat[ds8(j * pitch, rows), :].astype(BF)
-    loop(nres, regroup, 4)
-
-    def tblk(dev):
-        return tsend.at[pl.ds(dev * rows, rows)]
-
-    def tslot(dev):
-        return zrecv.at[:, ds8(dev * rows, rows, 16), :]
-
-    pc.scatter(tblk, tslot, zrel, ssem_t, rsem_t)
-    zrecv[:, mine, :] = tsend[pl.ds(me * rows, rows)]
-    pc.scatter_relay(tslot, zrel, ssem_t, rsem_t)
-    pc.scatter_wait(tslot, rsem_t)
-
-
-def pair_kernel(n, nchunk, mask_ref, x_ref, z_ref, rm_ref, wproj_ref, wopm_ref, wb1_ref, wqkvg1_ref, wo1_ref, wb2_ref, wqkvg2_ref, wo2_ref,
+    hrow = rows // 2
+
+    def tblk(h):
+        return lambda dev: tsend.at[h, pl.ds(dev * rows, rows)]
+
+    def tslot(h):
+        return lambda dev: zrecv.at[:, ds8(dev * rows + h * hrow, hrow), :]
+
+    for h in range(2):
+        loop(rows // 4, lambda t: attend(t + h * (rows // 4)), 4)
+        loop(hrow, lambda i: finish(i + h * hrow), 8)
+
+        def regroup(j):
+            tsend[h, j] = flat[ds8(j * pitch + h * hrow, hrow), :].astype(BF)
+        loop(nres, regroup, 8)
+        pc.scatter(tblk(h), tslot(h), zrel.at[h], ssem_t.at[h], rsem_t.at[h])
+    for h in range(2):
+        zrecv[:, ds8(me * rows + h * hrow, hrow), :] = tsend[h, pl.ds(me * rows, rows)]
+        pc.scatter_relay(tslot(h), zrel.at[h], ssem_t.at[h], rsem_t.at[h])
+    for h in range(2):
+        pc.scatter_wait(tslot(h), rsem_t.at[h])
+
+
+def pair_kernel(n, sizes, mask_ref, x_ref, z_ref, rm_ref, wproj_ref, wopm_ref, wb1_ref, wqkvg1_ref, wo1_ref, wb2_ref, wqkvg2_ref, wo2_ref,
                 zo_ref,
                 ac, at, w32, wt, cbuf, asend, csend, call, apack, arel, aall, upd, osc, z1, zln, brow, ball1, ball2, bias, proj, flat, wot,
                 lbuf, mbuf, pbuf, rbuf, obuf, maskcol, tsend1, tsend2, zrel1, zrel2, zmid, zfin,
@@ -546,8 +557,8 @@
     rows, nres, chan = z_ref.shape
     nf, nseq = csend.shape[0:2]
     ne = nf
-    fq = nf // nchunk
-    hq = fq // 2
+    nchunk = len(sizes)
+    first = [sum(sizes[:q]) for q in range(nchunk)]
     lane = lax.broadcasted_iota(jnp.int32, (nres, nres), 1)
     pitch = ac.shape[0] // nseq
     pitch2 = at.shape[0] // nres
@@ -557,12 +568,33 @@
         for s in range(2):
             mk = mask_ref[pl.ds(me * nseq + 2 * t + s, 1), :].astype(F32)
             ac[ds8((2 * t + s) * pitch, 2 * ne), :] = pr[:, part(s, nres)] * mk
-    loop(nseq // 2, project, 4)
+    loop(nseq // 2, project, 16)
+
+    def cslots(q):
+        def slot(lo, size):
+            return lambda dev: call.at[pl.ds(first[q] + lo, size), dev, :nseq, :]
+        hq = sizes[q] // 2
+        return slot(0, sizes[q]), slot(0, hq), slot(hq, hq)
+
+    def own(q):
+        for f in range(first[q], first[q] + sizes[q]):
+            v = ac[pl.ds(ne + f, nseq, stride=pitch), :].astype(BF)
+            csend[f] = v
+            call[f, me, :nseq, :] = v
+        pc.spread(csend.at[pl.ds(first[q], sizes[q])], cslots(q)[0], ssem_c.at[q], rsem_c.at[q])
+
+    def neighbours(q):
+        pc.spread_relay(*cslots(q), ssem_c.at[q], rsem_c.at[q])
+        if q + 2 < nchunk:
+            own(q + 2)
+
+    pc.meet()
+    own(0)
     pad = jnp.zeros((nres - nseq, nres), F32)
 
     def plane(e):
         at[pl.ds(e, nres, stride=pitch2), :] = stack(ac[pl.ds(e, nseq, stride=pitch), :], pad).T
-    loop(ne, plane, 4)
+    loop(ne, plane, 8)
     blocks = rows * ne // nres
     per = nres // ne
 
@@ -570,32 +602,13 @@
         v = [stack(*[at[ds8((d * rows + b * per + u) * pitch2, ne), :] for u in range(per)]) for b in range(blocks)]
         for r in range(blocks - 1):
             asend[d, part(r, nres), :] = jnp.where(lane >= nseq, pltpu.roll(v[-1], nseq - r * (nres - nseq), 1), v[r]).astype(BF)
-    loop(n, pack)
-    pc.meet()
+    loop(n, pack, 4)
 
     def aslot(dev):
         return apack.at[dev]
 
     pc.scatter(lambda dev: asend.at[dev], aslot, arel, ssem_a, rsem_a)
 
-    def cslots(q):
-        def slot(lo, size):
-            return lambda dev: call.at[pl.ds(q * fq + lo, size), dev, :nseq, :]
-        return slot(0, fq), slot(0, hq), slot(hq, hq)
-
-    def own(q):
-        for f in range(q * fq, q * fq + fq):
-            v = ac[pl.ds(ne + f, nseq, stride=pitch), :].astype(BF)
-            csend[f] = v
-            call[f, me, :nseq, :] = v
-        pc.spread(csend.at[pl.ds(q * fq, fq)], cslots(q)[0], ssem_c.at[q], rsem_c.at[q])
-
-    def neighbours(q):
-        pc.spread_relay(*cslots(q), ssem_c.at[q], rsem_c.at[q])
-        if q + 2 < nchunk:
-            own(q + 2)
-
-    own(0)
     own(1)
     apack[me] = asend[me]
     pc.scatter_relay(aslot, arel, ssem_a, rsem_a)
@@ -622,40 +635,38 @@
             moved = pltpu.roll(v, (r + 1) * (nres - nseq), 1)
             last = last + jnp.where((lane >= r * (nres - nseq)) & (lane < (r + 1) * (nres - nseq)), moved, 0.0)
         aall[d, part(blocks - 1, nres), :] = last.astype(BF)
-    loop(n, unpack)
+    loop(n, unpack, 2)
 
     for q in range(nchunk):
         pc.spread_wait(*cslots(q), ssem_c.at[q], rsem_c.at[q])
 
         def outer(g):
             acc = None
+            f = first[q] + 2 * g
             for kk in range(n // 2):
-                rhs = jnp.concatenate(
-                    [jnp.concatenate([call[q * fq + 2 * g + u, 2 * kk], call[q * fq + 2 * g + u, 2 * kk + 1]], axis=0) for u in range(2)],
-                    axis=1)
-                lhs = jnp.concatenate([aall[2 * kk], aall[2 * kk + 1]], axis=1)
-                step = dot(lhs, rhs)
+                rhs = cat(*[stack(call[f + u, 2 * kk], call[f + u, 2 * kk + 1]) for u in range(2)])
+                step = dot(cat(aall[2 * kk], aall[2 * kk + 1]), rhs)
                 acc = step if acc is None else acc + step
             ob = acc.astype(BF)
             for u in range(2):
                 for i in range(rows):
-                    osc[i, ds8((2 * g + u) * ne, ne, 32), :] = ob[i * ne:(i + 1) * ne, u * nres:(u + 1) * nres]
-        loop(fq // 2, outer)
+                    osc[i, ds8((2 * g + u) * ne, ne, 32), :] = ob[part(i, ne), part(u, nres)]
+        loop(sizes[q] // 2, outer, 2)
+        depth = sizes[q] * ne
 
         def contract(g):
-            rhs = jnp.concatenate([osc[2 * g], osc[2 * g + 1]], axis=1)
-            step = dot(wt[:, part(q, fq * ne)], rhs)
+            step = dot(wt[:, first[q] * ne:first[q] * ne + depth], cat(osc[2 * g, :depth, :], osc[2 * g + 1, :depth, :]))
             for u in range(2):
                 v = step[:, part(u, nres)]
                 upd[2 * g + u] = v if q == 0 else upd[2 * g + u] + v
-        loop(rows // 2, contract, 2)
-        if q + 2 < nchunk:
+        loop(rows // 2, contract, 8)
+        if 0 < q + 2 < nchunk:
             neighbours(q + 2)
 
     def residual(i):
         u = upd[i] / (1e-3 + cbuf[pl.ds(me * rows + i, 1), :])
         z1[i] = (z_ref[i].astype(F32) + u.T).astype(BF)
-    loop(rows, residual, 2)
+    loop(rows, residual, 8)
 
     for zin, wb, wq, wo, ball, ts, zrel, zout, sems in (
             (z1, wb1_ref, wqkvg1_ref, wo1_ref, ball1, tsend1, zrel1, zmid, (ssem_b1, rsem_b1, ssem_t1, rsem_t1)),
@@ -670,23 +681,23 @@
     nseq = 2 * x.shape[0]
     ne = wproj.shape[0] // 2
     heads = wb1.shape[0]
-    nchunk = 4
-    fq = ne // nchunk
+    sizes = (8, 8, 8, 4, 4)
     dma = pltpu.SemaphoreType.DMA((n,))
     dma9 = pltpu.SemaphoreType.DMA((9,))
-    dmac = pltpu.SemaphoreType.DMA((nchunk, 9))
+    dmac = pltpu.SemaphoreType.DMA((len(sizes), 9))
     pitch = rows + 8
     vz = pltpu.VMEM((rows, nres, chan), BF)
     fz = pltpu.VMEM((rows, chan, nres), F32)
     sq = pltpu.VMEM((nres, nres), F32)
     vb = pltpu.VMEM((heads, n * rows, nres), BF)
-    vt = pltpu.VMEM((nres, rows, chan), BF)
-    vr = pltpu.VMEM((2, rows, rows, chan), BF)
+    vt = pltpu.VMEM((2, nres, rows // 2, chan), BF)
+    vr = pltpu.VMEM((2, 2, rows, rows // 2, chan), BF)
+    dma29 = pltpu.SemaphoreType.DMA((2, 9))
     apk = rows * ne * nseq // nres
     row8 = pltpu.VMEM((heads, 8, 2 * nres), F32)
     args = (mask, x, z, rm, wproj, wopm, wb1, wqkvg1, wo1, wb2, wqkvg2, wo2)
     return pl.pallas_call(
-        functools.partial(pair_kernel, n, nchunk),
+        functools.partial(pair_kernel, n, sizes),
         name="pair",
         out_shape=jax.ShapeDtypeStruct(z.shape, BF),
         in_specs=[VM] * len(args),
@@ -704,7 +715,7 @@
             pltpu.VMEM((2, apk, nres), BF),
             pltpu.VMEM((n, rows * ne, nres), BF),
             fz,
-            pltpu.VMEM((rows, fq * ne, nres), BF),
+            pltpu.VMEM((rows, sizes[0] * ne, nres), BF),
             vz, vz,
             pltpu.VMEM((heads * pitch, nres), F32),
             vb, vb,
@@ -714,7 +725,7 @@
             pltpu.VMEM((chan, chan), BF),
             pltpu.VMEM((heads, nres, 2 * nres), F32), row8, pltpu.VMEM((heads, nres, 2 * nres), BF), row8,
             fz, sq, vt, vt, vr, vr, vz, vz,
-            dma9, dma9, dmac, dmac, dma, dma, dma9, dma9, dma, dma, dma9, dma9,
+            dma9, dma9, dmac, dmac, dma, dma, dma29, dma29, dma, dma, dma29, dma29,
         ],
         compiler_params=pltpu.CompilerParams(vmem_limit_bytes=40 * 2 ** 20, collective_id=1, has_side_effects=True),
     )(*args)

time: 140 us -> 125 us (0.89)
  Pallas kernels: 139 us -> 123 us
    pallas_call x1, Pallas kernels: 84.3 us -> 74.1 us  [pair_call(): pl.pallas_call(functools.partial(pair_kernel, n, sizes), name='pair', out...]
    pallas_call x1, Pallas kernels: 49.2 us -> 44.6 us  [msa_call(): pl.pallas_call(functools.partial(msa_kernel, n, len(args)), name='msa', o...]
where the time goes in v4:
time: 125 us; the launch traced here: 124 us
  Pallas kernels  123 us (98%)
    pallas_call x1, Pallas kernels, pair_call(): pl.pallas_call(functools.partial(pair_kernel, n, sizes), name='pair', out...  74.1 us
    pallas_call x1, Pallas kernels, msa_call(): pl.pallas_call(functools.partial(msa_kernel, n, len(args)), name='msa', o...  44.6 us
    pallas_call x1, Pallas kernels, gate_call(): pl.pallas_call(gate_kernel, name='gate', out_shape=[jax.ShapeDtypeStruct(...  4.05 us

profile of v4, /device:TPU:81, one launch (start us, length us, event | category | flops | bytes accessed | tf_op | source)
XLA Modules:
  0.0 124.4 jit_solution(2853068633737303953)
XLA Ops:
  0.6 0.0 copy-start.7
  0.6 44.6 %msa.1 = (bf16[96,64,128]{2,1,0:T(8,128)(2,1)S(1)}, bf16[48,64,256]{2,1,0:T(8,128)(2,1)S(1)}, f32[64,128]{1,0:T(8,128)S(1)}) custom-call(bf16[16,128,128]{2,1,0:T(8,128)(2,1)} %z_ref.1, bf16[8,128]{1,0:T(8,128)(2,1)} %bitcast.48, s32[768,128]{1,0:T(8,128)} %mask_ref.1, bf16[96,64,128]{2,1,0:T(8,128)(2,1)} %bitcast.42, bf16[256,64]{1,0:T(8,128)(2,1)} %bitcast.43, ...), custom_call_target="tpu_custom_call" | custom-call | tf_op jit(solution)/shard_map/msa/pallas_call | solution.py:384
  45.3 0.0 copy-done.7
  45.3 0.0 copy-start
  45.3 0.0 copy-start.1
  45.3 0.0 copy-start.2
  45.3 0.0 copy-start.3
  45.3 0.0 copy-start.4
  45.3 0.0 copy-start.5
  45.3 0.0 copy-start.6
  45.4 0.0 copy-start.8
  45.4 0.0 copy-start.9
  45.4 0.0 copy-start.10
  45.4 0.0 copy-start.11
  45.4 4.1 %gate.1 = (bf16[96,64,128]{2,1,0:T(8,128)(2,1)}, bf16[48,64,256]{2,1,0:T(8,128)(2,1)S(1)}) custom-call(bf16[96,64,128]{2,1,0:T(8,128)(2,1)S(1)} %get-tuple-element.7.m1_ref, bf16[48,64,256]{2,1,0:T(8,128)(2,1)S(1)} %get-tuple-element.8.g2_ref, f32[64,128]{1,0:T(8,128)S(1)} %get-tuple-element.9.o2_ref, bf16[64,64]{1,0:T(8,128)(2,1)S(1)} %bitcast.37), custom_call_target="tpu_custom_call" | custom-call | tf_op jit(solution)/shard_map/gate/pallas_call | solution.py:437
  49.5 0.0 copy-done
  49.5 0.0 copy-done.1
  49.5 0.0 copy-done.2
  49.5 0.0 copy-done.3
  49.5 0.0 copy-done.4
  49.5 0.0 copy-done.5
  49.5 0.0 copy-done.6
  49.5 0.0 copy-done.8
  49.5 0.0 copy-done.9
  49.5 0.0 copy-done.10
  49.5 0.0 copy-done.11
  49.5 74.1 %pair.1 = bf16[16,128,128]{2,1,0:T(8,128)(2,1)S(1)} custom-call(s32[768,128]{1,0:T(8,128)S(1)} %copy-done.1, bf16[48,64,256]{2,1,0:T(8,128)(2,1)S(1)} %get-tuple-element.11.x_ref, bf16[16,128,128]{2,1,0:T(8,128)(2,1)S(1)} %copy-done, s32[1,128]{1,0:T(1,128)S(1)} %bitcast.41, bf16[64,64]{1,0:T(8,128)(2,1)S(1)} %bitcast.38, bf16[1024,128]{1,0:T(8,128)(2,1)S(1)} %bitcast.32, ...), custom_call_target="tpu_custom_call" | custom-call | tf_op jit(solution)/shard_map/pair/pallas_call | solution.py:699
  123.6 0.8 copy.22
Async XLA Ops:
  0.6 44.6 %copy-start.7 = (bf16[8,8,64]{2,1,0:T(8,128)(2,1)S(1)}, bf16[8,8,64]{2,1,0:T(8,128)(2,1)}, u32[]{:S(2)}) copy-start(bf16[8,8,64]{2,1,0:T(8,128)(2,1)} %param.29) | copy-start | bytes 24580
  45.3 4.2 %copy-start = (bf16[16,128,128]{2,1,0:T(8,128)(2,1)S(1)}, bf16[16,128,128]{2,1,0:T(8,128)(2,1)}, u32[]{:S(2)}) copy-start(bf16[16,128,128]{2,1,0:T(8,128)(2,1)} %z_ref.1) | copy-start | bytes 1572868
  45.3 4.2 %copy-start.1 = (s32[768,128]{1,0:T(8,128)S(1)}, s32[768,128]{1,0:T(8,128)}, u32[]{:S(2)}) copy-start(s32[768,128]{1,0:T(8,128)} %mask_ref.1) | copy-start | bytes 1179652
  45.3 4.2 %copy-start.2 = (bf16[32,32,128]{2,1,0:T(8,128)(2,1)S(1)}, bf16[32,32,128]{2,1,0:T(8,128)(2,1)}, u32[]{:S(2)}) copy-start(bf16[32,32,128]{2,1,0:T(8,128)(2,1)} %param.31) | copy-start | bytes 786436
  45.3 4.2 %copy-start.3 = (bf16[128,4,4,32]{0,3,2,1:T(8,128)(2,1)S(1)}, bf16[128,4,4,32]{0,3,2,1:T(8,128)(2,1)}, u32[]{:S(2)}) copy-start(bf16[128,4,4,32]{0,3,2,1:T(8,128)(2,1)} %param.33) | copy-start | bytes 393220
  45.3 4.2 %copy-start.4 = (bf16[128,4,4,32]{0,3,2,1:T(8,128)(2,1)S(1)}, bf16[128,4,4,32]{0,3,2,1:T(8,128)(2,1)}, u32[]{:S(2)}) copy-start(bf16[128,4,4,32]{0,3,2,1:T(8,128)(2,1)} %param.36) | copy-start | bytes 393220
  45.3 4.2 %copy-start.5 = (bf16[4,32,128]{2,1,0:T(8,128)(2,1)S(1)}, bf16[4,32,128]{2,1,0:T(8,128)(2,1)}, u32[]{:S(2)}) copy-start(bf16[4,32,128]{2,1,0:T(8,128)(2,1)} %param.34) | copy-start | bytes 98308
  45.3 4.1 %copy-start.6 = (bf16[4,32,128]{2,1,0:T(8,128)(2,1)S(1)}, bf16[4,32,128]{2,1,0:T(8,128)(2,1)}, u32[]{:S(2)}) copy-start(bf16[4,32,128]{2,1,0:T(8,128)(2,1)} %param.37) | copy-start | bytes 98308
  45.4 4.1 %copy-start.8 = (bf16[64,2,32]{0,2,1:T(8,128)(2,1)S(1)}, bf16[64,2,32]{0,2,1:T(8,128)(2,1)}, u32[]{:S(2)}) copy-start(bf16[64,2,32]{0,2,1:T(8,128)(2,1)} %param.30) | copy-start | bytes 24580
  45.4 4.1 %copy-start.9 = (bf16[128,4]{0,1:T(4,128)(2,1)S(1)}, bf16[128,4]{0,1:T(4,128)(2,1)}, u32[]{:S(2)}) copy-start(bf16[128,4]{0,1:T(4,128)(2,1)} %param.32) | copy-start | bytes 3076
  45.4 4.1 %copy-start.10 = (bf16[128,4]{0,1:T(4,128)(2,1)S(1)}, bf16[128,4]{0,1:T(4,128)(2,1)}, u32[]{:S(2)}) copy-start(bf16[128,4]{0,1:T(4,128)(2,1)} %param.35) | copy-start | bytes 3076
  45.4 4.1 %copy-start.11 = (s32[128]{0:T(128)S(1)}, s32[128]{0:T(128)}, u32[]{:S(2)}) copy-start(s32[128]{0:T(128)} %param.22) | copy-start | bytes 1540

commit v5 on v4

--- a/solution.py
+++ b/solution.py
@@ -140,19 +140,20 @@
         for i, dev in enumerate((self.right, self.left, self.partner)):
             self.go(src, slot(self.me), ssem.at[i], rsem.at[i], dev)
 
-    def spread_relay(self, slot, lower, upper, ssem, rsem):
+    def spread_relay(self, slot, lower, upper, ssem, rsem, both=False):
         left, right = self.left, self.right
-        self.got(slot(left), rsem.at[0])
-        self.go(lower(left), lower(left), ssem.at[3], rsem.at[3], right)
-        self.go(slot(left), slot(left), ssem.at[5], rsem.at[5], self.partner)
-        self.got(slot(right), rsem.at[1])
-        self.go(upper(right), upper(right), ssem.at[4], rsem.at[4], left)
-        self.go(slot(right), slot(right), ssem.at[6], rsem.at[6], self.partner)
-
-    def spread_wait(self, slot, lower, upper, ssem, rsem):
+        for i, (dev, half, onward) in enumerate(((left, lower, right), (right, upper, left))):
+            self.got(slot(dev), rsem.at[i])
+            self.go(half(dev), half(dev), ssem.at[3 + i], rsem.at[3 + i], onward)
+            if both:
+                self.go(half(dev), half(dev), ssem.at[7 + i], rsem.at[7 + i], self.other(onward))
+            self.go(slot(dev), slot(dev), ssem.at[5 + i], rsem.at[5 + i], self.partner)
+
+    def spread_wait(self, slot, lower, upper, ssem, rsem, both=False):
         for i, half in enumerate((lower, upper)):
             self.got(half(self.far), rsem.at[3 + i])
-            self.go(half(self.far), half(self.far), ssem.at[7 + i], rsem.at[7 + i], self.partner)
+            if not both:
+                self.go(half(self.far), half(self.far), ssem.at[7 + i], rsem.at[7 + i], self.partner)
         self.got(slot(self.partner), rsem.at[2])
         self.got(slot(self.other(self.left)), rsem.at[5])
         self.got(slot(self.other(self.right)), rsem.at[6])
@@ -217,7 +218,7 @@
     def project(t):
         s0 = t * 2
         proj = dot(wqkvg_ref[:], xbuf[t])
-        gbuf[t] = proj[3 * chan:4 * chan, :].astype(BF)
+        gbuf[t] = sigmoid(rnd(proj[3 * chan:, :]))
         for s in range(2):
             sl = part(s, nres)
             mk = mask_ref[pl.ds(base + s0 + s, 1), :].astype(F32) - 1.0
@@ -283,7 +284,7 @@
     def finish(t):
         s0 = t * 2
         mv = jnp.concatenate([m_ref[s0].astype(F32), m_ref[s0 + 1].astype(F32)], axis=1)
-        y = (sigmoid(gbuf[t].astype(F32)) * obuf[t]).astype(BF)
+        y = (gbuf[t] * obuf[t]).astype(BF)
         m1 = (mv + dot(wot[:], y)).astype(BF)
         for s in range(2):
             m1_ref[s0 + s] = m1[:, part(s, nres)]
@@ -308,13 +309,13 @@
         s0 = t * 2
         xv = jnp.concatenate([x2_ref[s0], x2_ref[s0 + 1]], axis=1)
         kvp = rnd(dot(wkv_ref[:], xv))
-        g2_ref[t] = dot(wg2_ref[:], xv).astype(BF)
+        g2_ref[t] = sigmoid(rnd(dot(wg2_ref[:], xv)))
         for s in range(2):
             kv[s0 + s] = kvp[:, part(s, nres)]
     loop(npair, keyval, 8)
     count = total(mask_ref[:].astype(F32)) + 1e-10
-    pc.spread_relay(*qslots, ssem_q, rsem_q)
-    pc.spread_wait(*qslots, ssem_q, rsem_q)
+    pc.spread_relay(*qslots, ssem_q, rsem_q, True)
+    pc.spread_wait(*qslots, ssem_q, rsem_q, True)
     tot = qpart[0]
     for d in range(1, n):
         tot = tot + qpart[d]
@@ -356,8 +357,8 @@
     halfp = 8 + chan // 2
     pslots = (lambda dev: ppart.at[dev]), (lambda dev: ppart.at[dev, :halfp]), (lambda dev: ppart.at[dev, halfp:])
     pc.spread(ppart.at[me], pslots[0], ssem_p, rsem_p)
-    pc.spread_relay(*pslots, ssem_p, rsem_p)
-    pc.spread_wait(*pslots, ssem_p, rsem_p)
+    pc.spread_relay(*pslots, ssem_p, rsem_p, True)
+    pc.spread_wait(*pslots, ssem_p, rsem_p, True)
     top = ppart[0, :8, :]
     for d in range(1, n):
         top = jnp.maximum(top, ppart[d, :8, :])
@@ -384,7 +385,7 @@
     return pl.pallas_call(
         functools.partial(msa_kernel, n, len(args)),
         name="msa",
-        out_shape=[jax.ShapeDtypeStruct((nseq, chan, nres), BF), jax.ShapeDtypeStruct((nseq // 2, chan, 2 * nres), BF),
+        out_shape=[jax.ShapeDtypeStruct((nseq, chan, nres), BF), jax.ShapeDtypeStruct((nseq // 2, chan, 2 * nres), F32),
                    jax.ShapeDtypeStruct((chan, nres), F32)],
         in_specs=[pl.BlockSpec(memory_space=pltpu.HBM)] * len(args),
         out_specs=[VM] * 3,
@@ -404,7 +405,7 @@
             pltpu.VMEM((nseq, nres, nres), BF),
             pltpu.VMEM((nseq, chan, 2 * nres), BF),
             pltpu.VMEM((nseq, chan, nres), BF),
-            pltpu.VMEM((nseq // 2, chan, 2 * nres), BF),
+            pltpu.VMEM((nseq // 2, chan, 2 * nres), F32),
             pltpu.VMEM((heads, nres, 2 * nres), F32),
             pltpu.VMEM((heads, 8, 2 * nres), F32),
             pltpu.VMEM((heads, nres, 2 * nres), BF),
@@ -412,24 +413,33 @@
             pltpu.VMEM((nseq // 2, chan, 2 * nres), F32),
             dma, dma, dma9, dma9, dma9, dma9,
         ],
-        compiler_params=pltpu.CompilerParams(vmem_limit_bytes=36 * 2 ** 20, collective_id=0, has_side_effects=True),
+        compiler_params=pltpu.CompilerParams(vmem_limit_bytes=38 * 2 ** 20, collective_id=0, has_side_effects=True),
     )(*args)
 
 
-def gate_kernel(m1_ref, g2_ref, o2_ref, wo_ref, m2_ref, x_ref, wot):
+def gate_kernel(m1_ref, g2_ref, o2_ref, wo_ref, m2_ref, x_ref, wot, m2, sem):
     nseq, chan, nres = m1_ref.shape
     wot[:] = wo_ref[:].astype(F32).T.astype(BF)
+    pieces = sem.shape[0]
+    size = nseq // pieces
 
     def gate(t):
-        y = (sigmoid(g2_ref[t].astype(F32)) * cat(o2_ref[:], o2_ref[:])).astype(BF)
-        m2 = (cat(m1_ref[2 * t].astype(F32), m1_ref[2 * t + 1].astype(F32)) + dot(wot[:], y)).astype(BF)
+        y = (g2_ref[t] * cat(o2_ref[:], o2_ref[:])).astype(BF)
+        m = (cat(m1_ref[2 * t].astype(F32), m1_ref[2 * t + 1].astype(F32)) + dot(wot[:], y)).astype(BF)
         for s in range(2):
-            m2_ref[2 * t + s] = m2[:, part(s, nres)]
-    loop(nseq // 2, gate, 16)
+            m2[2 * t + s] = m[:, part(s, nres)]
 
     def renorm(t):
-        x_ref[t] = norm(cat(m2_ref[2 * t].astype(F32), m2_ref[2 * t + 1].astype(F32)), 0)
+        x_ref[t] = norm(cat(m2[2 * t].astype(F32), m2[2 * t + 1].astype(F32)), 0)
+    copies = []
+    for p in range(pieces):
+        loop(size // 2, lambda t: gate(t + p * (size // 2)), size // 2)
+        piece = pl.ds(p * size, size)
+        copies.append(pltpu.make_async_copy(m2.at[piece], m2_ref.at[piece], sem.at[p]))
+        copies[-1].start()
     loop(nseq // 2, renorm, 2)
+    for cp in copies:
+        cp.wait()
 
 
 def gate_call(m1, g2, o2, wo):
@@ -439,13 +449,13 @@
         name="gate",
         out_shape=[jax.ShapeDtypeStruct(m1.shape, BF), jax.ShapeDtypeStruct(g2.shape, BF)],
         in_specs=[VM] * 4,
-        out_specs=[VM] * 2,
-        scratch_shapes=[pltpu.VMEM((chan, chan), BF)],
+        out_specs=[pl.BlockSpec(memory_space=pltpu.HBM), VM],
+        scratch_shapes=[pltpu.VMEM((chan, chan), BF), pltpu.VMEM(m1.shape, BF), pltpu.SemaphoreType.DMA((3,))],
         compiler_params=pltpu.CompilerParams(vmem_limit_bytes=16 * 2 ** 20),
     )(m1, g2, o2, wo)
 
 
-def tri_attend(pc, zin, wb_ref, wqkvg_ref, wo_ref, maskcol, zln, brow, ball, bias, proj, flat, wot, lbuf, mbuf, pbuf, rbuf, obuf, zrel, tsend, zrecv,
+def tri_attend(pc, early, zin, wb_ref, wqkvg_ref, wo_ref, maskcol, zln, brow, ball, bias, proj, gate, flat, wot, lbuf, mbuf, pbuf, rbuf, obuf, zrel, tsend, zrecv,
                ssem_b, rsem_b, ssem_t, rsem_t):
     me = pc.me
     rows, nres, chan = zin.shape
@@ -455,29 +465,38 @@
     pitch = rows + 8
     mine = ds8(me * rows, rows, 16)
 
-    def bias_row(i):
-        zl = norm(zin[i].astype(F32), 1)
-        zln[i] = zl
-        brow[pl.ds(i, heads, stride=pitch), :] = dot_nt(wb_ref[:], zl)
-    loop(rows, bias_row, rows)
-    for h in range(heads):
-        ball[h, mine, :] = brow[h * pitch:h * pitch + rows, :].astype(BF)
-
-    def bslot(dev):
-        return ball.at[:, ds8(dev * rows, rows, 16), :]
-
-    pc.to_all(bslot(me), bslot, ssem_b, rsem_b)
+    def bslot(buf):
+        return lambda dev: buf.at[:, ds8(dev * rows, rows, 16), :]
+
+    def make_bias(src, w_ref, buf, ssem, rsem):
+        def bias_row(i):
+            zl = norm(src[i].astype(F32), 1)
+            zln[i] = zl
+            brow[pl.ds(i, heads, stride=pitch), :] = dot_nt(w_ref[:], zl)
+        loop(rows, bias_row, rows)
+        for h in range(heads):
+            buf[h, mine, :] = brow[h * pitch:h * pitch + rows, :].astype(BF)
+        pc.to_all(bslot(buf)(me), bslot(buf), ssem, rsem)
+
+    if early:
+        make_bias(zin, wb_ref, ball, ssem_b, rsem_b)
+    else:
+        def renorm(i):
+            zln[i] = norm(zin[i].astype(F32), 1)
+        loop(rows, renorm, 8)
     wot[:] = wo_ref[:].astype(F32).T.astype(BF)
 
     def project(i):
         zl = zln[i]
         proj[i, :chan, :] = dot_nt(wqkvg_ref[:chan, :], zl).astype(BF)
         proj[i, chan:2 * chan, :] = dot_nt(zl, wqkvg_ref[chan:2 * chan, :]).astype(BF)
-        proj[i, 2 * chan:4 * chan, :] = dot_nt(wqkvg_ref[2 * chan:4 * chan, :], zl).astype(BF)
+        proj[i, 2 * chan:, :] = dot_nt(wqkvg_ref[2 * chan:3 * chan, :], zl).astype(BF)
+        gate[i] = sigmoid(rnd(dot_nt(wqkvg_ref[3 * chan:, :], zl)))
     loop(rows, project, 8)
-    pc.from_all(bslot, rsem_b)
+    pc.from_all(bslot(ball), rsem_b)
     for h in range(heads):
-        bias[:, part(h, nres)] = (ball[h].astype(F32).T + maskcol[:]) * LOG2E
+        b = ball[h].astype(F32)
+        bias[:, part(h, nres)] = ((b.T if early else b) + maskcol[:]) * LOG2E
     zero = jnp.zeros((hd, nres), BF)
 
     half = heads // 2
@@ -520,9 +539,12 @@
                 pv(2 * t + units[u - 1][0], units[u - 1][1], u - 1)
         pv(2 * t + units[-1][0], units[-1][1], len(units) - 1)
     def finish(i):
-        y = (sigmoid(proj[i, 3 * chan:4 * chan, :].astype(F32)) * obuf[i]).astype(BF)
+        y = (gate[i] * obuf[i]).astype(BF)
         upd = dot(wot[:], y).T
-        flat[pl.ds(i, nres, stride=pitch), :] = zin[i].astype(F32) + upd
+        zn = zin[i].astype(F32) + upd
+        flat[pl.ds(i, nres, stride=pitch), :] = zn
+        if early:
+            zin[i] = zn.astype(BF)
     hrow = rows // 2
 
     def tblk(h):
@@ -540,15 +562,17 @@
         loop(nres, regroup, 8)
         pc.scatter(tblk(h), tslot(h), zrel.at[h], ssem_t.at[h], rsem_t.at[h])
     for h in range(2):
+        pc.scatter_relay(tslot(h), zrel.at[h], ssem_t.at[h], rsem_t.at[h])
+        if early and h == 0:
+            make_bias(zin, *early)
         zrecv[:, ds8(me * rows + h * hrow, hrow), :] = tsend[h, pl.ds(me * rows, rows)]
-        pc.scatter_relay(tslot(h), zrel.at[h], ssem_t.at[h], rsem_t.at[h])
     for h in range(2):
         pc.scatter_wait(tslot(h), rsem_t.at[h])
 
 
 def pair_kernel(n, sizes, mask_ref, x_ref, z_ref, rm_ref, wproj_ref, wopm_ref, wb1_ref, wqkvg1_ref, wo1_ref, wb2_ref, wqkvg2_ref, wo2_ref,
                 zo_ref,
-                ac, at, w32, wt, cbuf, asend, csend, call, apack, arel, aall, upd, osc, z1, zln, brow, ball1, ball2, bias, proj, flat, wot,
+                ac, at, w32, wt, cbuf, asend, csend, call, apack, arel, aall, upd, osc, z1, zln, brow, ball1, ball2, bias, proj, gate, flat, wot,
                 lbuf, mbuf, pbuf, rbuf, obuf, maskcol, tsend1, tsend2, zrel1, zrel2, zmid, zfin,
                 ssem_a, rsem_a, ssem_c, rsem_c, ssem_b1, rsem_b1, ssem_t1, rsem_t1, ssem_b2, rsem_b2, ssem_t2, rsem_t2):
     pc = Place(n)
@@ -640,6 +664,9 @@
     for q in range(nchunk):
         pc.spread_wait(*cslots(q), ssem_c.at[q], rsem_c.at[q])
 
+        if q == nchunk - 3:
+            neighbours(q + 2)
+
         def outer(g):
             acc = None
             f = first[q] + 2 * g
@@ -660,7 +687,7 @@
                 v = step[:, part(u, nres)]
                 upd[2 * g + u] = v if q == 0 else upd[2 * g + u] + v
         loop(rows // 2, contract, 8)
-        if 0 < q + 2 < nchunk:
+        if q + 3 < nchunk:
             neighbours(q + 2)
 
     def residual(i):
@@ -668,10 +695,10 @@
         z1[i] = (z_ref[i].astype(F32) + u.T).astype(BF)
     loop(rows, residual, 8)
 
-    for zin, wb, wq, wo, ball, ts, zrel, zout, sems in (
-            (z1, wb1_ref, wqkvg1_ref, wo1_ref, ball1, tsend1, zrel1, zmid, (ssem_b1, rsem_b1, ssem_t1, rsem_t1)),
-            (zmid, wb2_ref, wqkvg2_ref, wo2_ref, ball2, tsend2, zrel2, zfin, (ssem_b2, rsem_b2, ssem_t2, rsem_t2))):
-        tri_attend(pc, zin, wb, wq, wo, maskcol, zln, brow, ball, bias, proj, flat, wot, lbuf, mbuf, pbuf, rbuf, obuf, zrel, ts, zout, *sems)
+    for early, zin, wb, wq, wo, ball, ts, zrel, zout, sems in (
+            ((wb2_ref, ball2, ssem_b2, rsem_b2), z1, wb1_ref, wqkvg1_ref, wo1_ref, ball1, tsend1, zrel1, zmid, (ssem_b1, rsem_b1, ssem_t1, rsem_t1)),
+            (None, zmid, wb2_ref, wqkvg2_ref, wo2_ref, ball2, tsend2, zrel2, zfin, (ssem_b2, rsem_b2, ssem_t2, rsem_t2))):
+        tri_attend(pc, early, zin, wb, wq, wo, maskcol, zln, brow, ball, bias, proj, gate, flat, wot, lbuf, mbuf, pbuf, rbuf, obuf, zrel, ts, zout, *sems)
     zo_ref[:] = zfin[:]
     pc.drain()
 
@@ -720,7 +747,7 @@
             pltpu.VMEM((heads * pitch, nres), F32),
             vb, vb,
             pltpu.VMEM((nres, heads * nres), F32),
-            pltpu.VMEM((rows, 4 * chan, nres), BF),
+            pltpu.VMEM((rows, 3 * chan, nres), BF), fz,
             pltpu.VMEM((nres * pitch, chan), F32),
             pltpu.VMEM((chan, chan), BF),
             pltpu.VMEM((heads, nres, 2 * nres), F32), row8, pltpu.VMEM((heads, nres, 2 * nres), BF), row8,

time: 125 us -> 119 us (0.952)
  Pallas kernels: 123 us -> 117 us
    pallas_call x1, Pallas kernels: 4.05 us -> 2.03 us  [gate_call(): pl.pallas_call(gate_kernel, name='gate', out_shape=[jax.ShapeDtypeStruct(...]
    pallas_call x1, Pallas kernels: 44.6 us -> 42.9 us  [msa_call(): pl.pallas_call(functools.partial(msa_kernel, n, len(args)), name='msa', o...]
    pallas_call x1, Pallas kernels: 74.1 us -> 72.5 us  [pair_call(): pl.pallas_call(functools.partial(pair_kernel, n, sizes), name='pair', out...]
where the time goes in v5:
time: 119 us
  Pallas kernels  117 us (98%)
    pallas_call x1, Pallas kernels, pair_call(): pl.pallas_call(functools.partial(pair_kernel, n, sizes), name='pair', out...  72.5 us
    pallas_call x1, Pallas kernels, msa_call(): pl.pallas_call(functools.partial(msa_kernel, n, len(args)), name='msa', o...  42.9 us

profile of v5, /device:TPU:81, one launch (start us, length us, event | category | flops | bytes accessed | tf_op | source)
XLA Modules:
  0.0 119.2 jit_solution(5065644939916112375)
XLA Ops:
  0.6 0.0 copy-start.7
  0.6 42.9 %msa.1 = (bf16[96,64,128]{2,1,0:T(8,128)(2,1)S(1)}, f32[48,64,256]{2,1,0:T(8,128)S(1)}, f32[64,128]{1,0:T(8,128)S(1)}) custom-call(bf16[16,128,128]{2,1,0:T(8,128)(2,1)} %z_ref.1, bf16[8,128]{1,0:T(8,128)(2,1)} %bitcast.48, s32[768,128]{1,0:T(8,128)} %mask_ref.1, bf16[96,64,128]{2,1,0:T(8,128)(2,1)} %bitcast.42, bf16[256,64]{1,0:T(8,128)(2,1)} %bitcast.43, ...), custom_call_target="tpu_custom_call" | custom-call | tf_op jit(solution)/shard_map/msa/pallas_call | solution.py:385
  43.6 0.0 copy-done.7
  43.6 0.0 copy-start
  43.6 0.0 copy-start.1
  43.6 0.0 copy-start.2
  43.6 0.0 copy-start.3
  43.6 0.0 copy-start.4
  43.6 0.0 copy-start.5
  43.7 0.0 copy-start.6
  43.7 0.0 copy-start.8
  43.7 0.0 copy-start.9
  43.7 0.0 copy-start.10
  43.7 0.0 copy-start.11
  43.7 2.0 %gate.1 = (bf16[96,64,128]{2,1,0:T(8,128)(2,1)}, bf16[48,64,256]{2,1,0:T(8,128)(2,1)S(1)}) custom-call(bf16[96,64,128]{2,1,0:T(8,128)(2,1)S(1)} %get-tuple-element.7.m1_ref, f32[48,64,256]{2,1,0:T(8,128)S(1)} %get-tuple-element.8.g2_ref, f32[64,128]{1,0:T(8,128)S(1)} %get-tuple-element.9.o2_ref, bf16[64,64]{1,0:T(8,128)(2,1)S(1)} %bitcast.37), custom_call_target="tpu_custom_call" | custom-call | tf_op jit(solution)/shard_map/gate/pallas_call | solution.py:447
  45.8 0.0 copy-done
  45.8 0.0 copy-done.1
  45.8 0.0 copy-done.2
  45.8 0.0 copy-done.3
  45.8 0.0 copy-done.4
  45.8 0.0 copy-done.5
  45.8 0.0 copy-done.6
  45.8 0.0 copy-done.8
  45.8 0.0 copy-done.9
  45.8 0.0 copy-done.10
  45.9 0.0 copy-done.11
  45.9 72.5 %pair.1 = bf16[16,128,128]{2,1,0:T(8,128)(2,1)S(1)} custom-call(s32[768,128]{1,0:T(8,128)S(1)} %copy-done.1, bf16[48,64,256]{2,1,0:T(8,128)(2,1)S(1)} %get-tuple-element.11.x_ref, bf16[16,128,128]{2,1,0:T(8,128)(2,1)S(1)} %copy-done, s32[1,128]{1,0:T(1,128)S(1)} %bitcast.41, bf16[64,64]{1,0:T(8,128)(2,1)S(1)} %bitcast.38, bf16[1024,128]{1,0:T(8,128)(2,1)S(1)} %bitcast.32, ...), custom_call_target="tpu_custom_call" | custom-call | tf_op jit(solution)/shard_map/pair/pallas_call | solution.py:726
  118.4 0.8 copy.22
Async XLA Ops:
  0.6 42.9 %copy-start.7 = (bf16[8,8,64]{2,1,0:T(8,128)(2,1)S(1)}, bf16[8,8,64]{2,1,0:T(8,128)(2,1)}, u32[]{:S(2)}) copy-start(bf16[8,8,64]{2,1,0:T(8,128)(2,1)} %param.29) | copy-start | bytes 24580
  43.6 2.2 %copy-start = (bf16[16,128,128]{2,1,0:T(8,128)(2,1)S(1)}, bf16[16,128,128]{2,1,0:T(8,128)(2,1)}, u32[]{:S(2)}) copy-start(bf16[16,128,128]{2,1,0:T(8,128)(2,1)} %z_ref.1) | copy-start | bytes 1572868
  43.6 2.2 %copy-start.1 = (s32[768,128]{1,0:T(8,128)S(1)}, s32[768,128]{1,0:T(8,128)}, u32[]{:S(2)}) copy-start(s32[768,128]{1,0:T(8,128)} %mask_ref.1) | copy-start | bytes 1179652
  43.6 2.2 %copy-start.2 = (bf16[32,32,128]{2,1,0:T(8,128)(2,1)S(1)}, bf16[32,32,128]{2,1,0:T(8,128)(2,1)}, u32[]{:S(2)}) copy-start(bf16[32,32,128]{2,1,0:T(8,128)(2,1)} %param.31) | copy-start | bytes 786436
  43.6 2.2 %copy-start.3 = (bf16[128,4,4,32]{0,3,2,1:T(8,128)(2,1)S(1)}, bf16[128,4,4,32]{0,3,2,1:T(8,128)(2,1)}, u32[]{:S(2)}) copy-start(bf16[128,4,4,32]{0,3,2,1:T(8,128)(2,1)} %param.33) | copy-start | bytes 393220
  43.6 2.2 %copy-start.4 = (bf16[128,4,4,32]{0,3,2,1:T(8,128)(2,1)S(1)}, bf16[128,4,4,32]{0,3,2,1:T(8,128)(2,1)}, u32[]{:S(2)}) copy-start(bf16[128,4,4,32]{0,3,2,1:T(8,128)(2,1)} %param.36) | copy-start | bytes 393220
  43.6 2.2 %copy-start.5 = (bf16[4,32,128]{2,1,0:T(8,128)(2,1)S(1)}, bf16[4,32,128]{2,1,0:T(8,128)(2,1)}, u32[]{:S(2)}) copy-start(bf16[4,32,128]{2,1,0:T(8,128)(2,1)} %param.34) | copy-start | bytes 98308
  43.7 2.2 %copy-start.6 = (bf16[4,32,128]{2,1,0:T(8,128)(2,1)S(1)}, bf16[4,32,128]{2,1,0:T(8,128)(2,1)}, u32[]{:S(2)}) copy-start(bf16[4,32,128]{2,1,0:T(8,128)(2,1)} %param.37) | copy-start | bytes 98308
  43.7 2.2 %copy-start.8 = (bf16[64,2,32]{0,2,1:T(8,128)(2,1)S(1)}, bf16[64,2,32]{0,2,1:T(8,128)(2,1)}, u32[]{:S(2)}) copy-start(bf16[64,2,32]{0,2,1:T(8,128)(2,1)} %param.30) | copy-start | bytes 24580
  43.7 2.2 %copy-start.9 = (bf16[128,4]{0,1:T(4,128)(2,1)S(1)}, bf16[128,4]{0,1:T(4,128)(2,1)}, u32[]{:S(2)}) copy-start(bf16[128,4]{0,1:T(4,128)(2,1)} %param.32) | copy-start | bytes 3076
  43.7 2.2 %copy-start.10 = (bf16[128,4]{0,1:T(4,128)(2,1)S(1)}, bf16[128,4]{0,1:T(4,128)(2,1)}, u32[]{:S(2)}) copy-start(bf16[128,4]{0,1:T(4,128)(2,1)} %param.35) | copy-start | bytes 3076
  43.7 2.2 %copy-start.11 = (s32[128]{0:T(128)S(1)}, s32[128]{0:T(128)}, u32[]{:S(2)}) copy-start(s32[128]{0:T(128)} %param.22) | copy-start | bytes 1540

commit v6 on v5

--- a/solution.py
+++ b/solution.py
@@ -114,20 +114,22 @@
         for d in range(1, self.n):
             self.got(slot(lax.rem(self.me + self.n - d, self.n)), rsem.at[d])
 
-    def scatter(self, blk, slot, rel, ssem, rsem):
+    def scatter(self, blk, slot, ssem, rsem, rel=None):
         k, me = self.k, self.me
-        self.go(blk(self.farc), rel.at[0], ssem.at[0], rsem.at[0], self.right)
-        self.go(blk(self.farc + 1), rel.at[1], ssem.at[1], rsem.at[1], self.left)
+        for j, onward in enumerate((self.right, self.left)):
+            if rel is None:
+                self.go(blk(self.farc + j), slot(me), ssem.at[j], rsem.at[7 + k], self.farc + j)
+            else:
+                self.go(blk(self.farc + j), rel.at[j], ssem.at[j], rsem.at[j], onward)
         for j in range(2):
             self.go(blk(self.rightc + j), slot(me), ssem.at[2 + j], rsem.at[2 + k], self.rightc + j)
             self.go(blk(self.leftc + j), slot(me), ssem.at[4 + j], rsem.at[4 + k], self.leftc + j)
         self.go(blk(self.partner), slot(me), ssem.at[6], rsem.at[6], self.partner)
 
     def scatter_relay(self, slot, rel, ssem, rsem):
-        self.got(rel.at[0], rsem.at[0])
-        self.go(rel.at[0], slot(self.left), ssem.at[7], rsem.at[7 + self.k], self.rightc)
-        self.got(rel.at[1], rsem.at[1])
-        self.go(rel.at[1], slot(self.right), ssem.at[8], rsem.at[7 + self.k], self.leftc + 1)
+        for j, (dev, onward) in enumerate(((self.left, self.rightc), (self.right, self.leftc + 1))):
+            self.got(rel.at[j], rsem.at[j])
+            self.go(rel.at[j], slot(dev), ssem.at[7 + j], rsem.at[7 + self.k], onward)
 
     def scatter_wait(self, slot, rsem):
         for j in range(2):
@@ -301,9 +303,11 @@
         return acc
     qpart[me] = lax.fori_loop(0, npair, renorm, jnp.zeros((chan, nres), F32), unroll=2)
 
-    halfq = chan // 2
-    qslots = (lambda dev: qpart.at[dev]), (lambda dev: qpart.at[dev, :halfq]), (lambda dev: qpart.at[dev, halfq:])
-    pc.spread(qpart.at[me], qslots[0], ssem_q, rsem_q)
+
+    def qslots(dev):
+        return qpart.at[dev]
+
+    pc.to_all(qpart.at[me], qslots, ssem_q, rsem_q)
 
     def keyval(t):
         s0 = t * 2
@@ -314,8 +318,7 @@
             kv[s0 + s] = kvp[:, part(s, nres)]
     loop(npair, keyval, 8)
     count = total(mask_ref[:].astype(F32)) + 1e-10
-    pc.spread_relay(*qslots, ssem_q, rsem_q, True)
-    pc.spread_wait(*qslots, ssem_q, rsem_q, True)
+    pc.from_all(qslots, rsem_q)
     tot = qpart[0]
     for d in range(1, n):
         tot = tot + qpart[d]
@@ -354,11 +357,12 @@
     ppart[me, 8:16, :] = ssum
     for d in range(hd):
         ppart[me, 16 + 8 * d:24 + 8 * d, :] = acc[d]
-    halfp = 8 + chan // 2
-    pslots = (lambda dev: ppart.at[dev]), (lambda dev: ppart.at[dev, :halfp]), (lambda dev: ppart.at[dev, halfp:])
-    pc.spread(ppart.at[me], pslots[0], ssem_p, rsem_p)
-    pc.spread_relay(*pslots, ssem_p, rsem_p, True)
-    pc.spread_wait(*pslots, ssem_p, rsem_p, True)
+
+    def pslots(dev):
+        return ppart.at[dev]
+
+    pc.to_all(ppart.at[me], pslots, ssem_p, rsem_p)
+    pc.from_all(pslots, rsem_p)
     top = ppart[0, :8, :]
     for d in range(1, n):
         top = jnp.maximum(top, ppart[d, :8, :])
@@ -411,7 +415,7 @@
             pltpu.VMEM((heads, nres, 2 * nres), BF),
             pltpu.VMEM((heads, 8, 2 * nres), F32),
             pltpu.VMEM((nseq // 2, chan, 2 * nres), F32),
-            dma, dma, dma9, dma9, dma9, dma9,
+            dma, dma, dma, dma, dma, dma,
         ],
         compiler_params=pltpu.CompilerParams(vmem_limit_bytes=38 * 2 ** 20, collective_id=0, has_side_effects=True),
     )(*args)
@@ -455,7 +459,7 @@
     )(m1, g2, o2, wo)
 
 
-def tri_attend(pc, early, zin, wb_ref, wqkvg_ref, wo_ref, maskcol, zln, brow, ball, bias, proj, gate, flat, wot, lbuf, mbuf, pbuf, rbuf, obuf, zrel, tsend, zrecv,
+def tri_attend(pc, early, zin, wb_ref, wqkvg_ref, wo_ref, maskcol, zln, brow, ball, bias, proj, gate, flat, wot, lbuf, mbuf, pbuf, rbuf, obuf, tsend, zrecv,
                ssem_b, rsem_b, ssem_t, rsem_t):
     me = pc.me
     rows, nres, chan = zin.shape
@@ -560,9 +564,8 @@
         def regroup(j):
             tsend[h, j] = flat[ds8(j * pitch + h * hrow, hrow), :].astype(BF)
         loop(nres, regroup, 8)
-        pc.scatter(tblk(h), tslot(h), zrel.at[h], ssem_t.at[h], rsem_t.at[h])
+        pc.scatter(tblk(h), tslot(h), ssem_t.at[h], rsem_t.at[h])
     for h in range(2):
-        pc.scatter_relay(tslot(h), zrel.at[h], ssem_t.at[h], rsem_t.at[h])
         if early and h == 0:
             make_bias(zin, *early)
         zrecv[:, ds8(me * rows + h * hrow, hrow), :] = tsend[h, pl.ds(me * rows, rows)]
@@ -573,7 +576,7 @@
 def pair_kernel(n, sizes, mask_ref, x_ref, z_ref, rm_ref, wproj_ref, wopm_ref, wb1_ref, wqkvg1_ref, wo1_ref, wb2_ref, wqkvg2_ref, wo2_ref,
                 zo_ref,
                 ac, at, w32, wt, cbuf, asend, csend, call, apack, arel, aall, upd, osc, z1, zln, brow, ball1, ball2, bias, proj, gate, flat, wot,
-                lbuf, mbuf, pbuf, rbuf, obuf, maskcol, tsend1, tsend2, zrel1, zrel2, zmid, zfin,
+                lbuf, mbuf, pbuf, rbuf, obuf, maskcol, tsend1, tsend2, zmid, zfin,
                 ssem_a, rsem_a, ssem_c, rsem_c, ssem_b1, rsem_b1, ssem_t1, rsem_t1, ssem_b2, rsem_b2, ssem_t2, rsem_t2):
     pc = Place(n)
     me = pc.me
@@ -631,7 +634,7 @@
     def aslot(dev):
         return apack.at[dev]
 
-    pc.scatter(lambda dev: asend.at[dev], aslot, arel, ssem_a, rsem_a)
+    pc.scatter(lambda dev: asend.at[dev], aslot, ssem_a, rsem_a, arel)
 
     own(1)
     apack[me] = asend[me]
@@ -695,10 +698,10 @@
         z1[i] = (z_ref[i].astype(F32) + u.T).astype(BF)
     loop(rows, residual, 8)
 
-    for early, zin, wb, wq, wo, ball, ts, zrel, zout, sems in (
-            ((wb2_ref, ball2, ssem_b2, rsem_b2), z1, wb1_ref, wqkvg1_ref, wo1_ref, ball1, tsend1, zrel1, zmid, (ssem_b1, rsem_b1, ssem_t1, rsem_t1)),
-            (None, zmid, wb2_ref, wqkvg2_ref, wo2_ref, ball2, tsend2, zrel2, zfin, (ssem_b2, rsem_b2, ssem_t2, rsem_t2))):
-        tri_attend(pc, early, zin, wb, wq, wo, maskcol, zln, brow, ball, bias, proj, gate, flat, wot, lbuf, mbuf, pbuf, rbuf, obuf, zrel, ts, zout, *sems)
+    for early, zin, wb, wq, wo, ball, ts, zout, sems in (
+            ((wb2_ref, ball2, ssem_b2, rsem_b2), z1, wb1_ref, wqkvg1_ref, wo1_ref, ball1, tsend1, zmid, (ssem_b1, rsem_b1, ssem_t1, rsem_t1)),
+            (None, zmid, wb2_ref, wqkvg2_ref, wo2_ref, ball2, tsend2, zfin, (ssem_b2, rsem_b2, ssem_t2, rsem_t2))):
+        tri_attend(pc, early, zin, wb, wq, wo, maskcol, zln, brow, ball, bias, proj, gate, flat, wot, lbuf, mbuf, pbuf, rbuf, obuf, ts, zout, *sems)
     zo_ref[:] = zfin[:]
     pc.drain()
 
@@ -718,7 +721,6 @@
     sq = pltpu.VMEM((nres, nres), F32)
     vb = pltpu.VMEM((heads, n * rows, nres), BF)
     vt = pltpu.VMEM((2, nres, rows // 2, chan), BF)
-    vr = pltpu.VMEM((2, 2, rows, rows // 2, chan), BF)
     dma29 = pltpu.SemaphoreType.DMA((2, 9))
     apk = rows * ne * nseq // nres
     row8 = pltpu.VMEM((heads, 8, 2 * nres), F32)
@@ -751,7 +753,7 @@
             pltpu.VMEM((nres * pitch, chan), F32),
             pltpu.VMEM((chan, chan), BF),
             pltpu.VMEM((heads, nres, 2 * nres), F32), row8, pltpu.VMEM((heads, nres, 2 * nres), BF), row8,
-            fz, sq, vt, vt, vr, vr, vz, vz,
+            fz, sq, vt, vt, vz, vz,
             dma9, dma9, dmac, dmac, dma, dma, dma29, dma29, dma, dma, dma29, dma29,
         ],
         compiler_params=pltpu.CompilerParams(vmem_limit_bytes=40 * 2 ** 20, collective_id=1, has_side_effects=True),

time: 119 us -> 115 us (0.966)
  Pallas kernels: 117 us -> 113 us
    pallas_call x1, Pallas kernels: 42.9 us -> 40.1 us  [msa_call(): pl.pallas_call(functools.partial(msa_kernel, n, len(args)), name='msa', o...]
    pallas_call x1, Pallas kernels: 72.5 us -> 71.3 us  [pair_call(): pl.pallas_call(functools.partial(pair_kernel, n, sizes), name='pair', out...]
where the time goes in v6:
time: 115 us
  Pallas kernels  113 us (98%)
    pallas_call x1, Pallas kernels, pair_call(): pl.pallas_call(functools.partial(pair_kernel, n, sizes), name='pair', out...  71.3 us
    pallas_call x1, Pallas kernels, msa_call(): pl.pallas_call(functools.partial(msa_kernel, n, len(args)), name='msa', o...  40.1 us

profile of v6, /device:TPU:81, one launch (start us, length us, event | category | flops | bytes accessed | tf_op | source)
XLA Modules:
  0.0 115.1 jit_solution(16114047921645084810)
XLA Ops:
  0.6 0.0 copy-start.7
  0.6 40.1 %msa.1 = (bf16[96,64,128]{2,1,0:T(8,128)(2,1)S(1)}, f32[48,64,256]{2,1,0:T(8,128)S(1)}, f32[64,128]{1,0:T(8,128)S(1)}) custom-call(bf16[16,128,128]{2,1,0:T(8,128)(2,1)} %z_ref.1, bf16[8,128]{1,0:T(8,128)(2,1)} %bitcast.48, s32[768,128]{1,0:T(8,128)} %mask_ref.1, bf16[96,64,128]{2,1,0:T(8,128)(2,1)} %bitcast.42, bf16[256,64]{1,0:T(8,128)(2,1)} %bitcast.43, ...), custom_call_target="tpu_custom_call" | custom-call | tf_op jit(solution)/shard_map/msa/pallas_call | solution.py:389
  40.7 0.0 copy-done.7
  40.8 0.0 copy-start
  40.8 0.0 copy-start.1
  40.8 0.0 copy-start.2
  40.8 0.0 copy-start.3
  40.8 0.0 copy-start.4
  40.8 0.0 copy-start.5
  40.8 0.0 copy-start.6
  40.8 0.0 copy-start.8
  40.8 0.0 copy-start.9
  40.9 0.0 copy-start.10
  40.9 0.0 copy-start.11
  40.9 2.0 %gate.1 = (bf16[96,64,128]{2,1,0:T(8,128)(2,1)}, bf16[48,64,256]{2,1,0:T(8,128)(2,1)S(1)}) custom-call(bf16[96,64,128]{2,1,0:T(8,128)(2,1)S(1)} %get-tuple-element.7.m1_ref, f32[48,64,256]{2,1,0:T(8,128)S(1)} %get-tuple-element.8.g2_ref, f32[64,128]{1,0:T(8,128)S(1)} %get-tuple-element.9.o2_ref, bf16[64,64]{1,0:T(8,128)(2,1)S(1)} %bitcast.37), custom_call_target="tpu_custom_call" | custom-call | tf_op jit(solution)/shard_map/gate/pallas_call | solution.py:451
  42.9 0.0 copy-done
  42.9 0.0 copy-done.1
  42.9 0.0 copy-done.2
  42.9 0.0 copy-done.3
  43.0 0.0 copy-done.4
  43.0 0.0 copy-done.5
  43.0 0.0 copy-done.6
  43.0 0.0 copy-done.8
  43.0 0.0 copy-done.9
  43.0 0.0 copy-done.10
  43.0 0.0 copy-done.11
  43.0 71.3 %pair.1 = bf16[16,128,128]{2,1,0:T(8,128)(2,1)S(1)} custom-call(s32[768,128]{1,0:T(8,128)S(1)} %copy-done.1, bf16[48,64,256]{2,1,0:T(8,128)(2,1)S(1)} %get-tuple-element.11.x_ref, bf16[16,128,128]{2,1,0:T(8,128)(2,1)S(1)} %copy-done, s32[1,128]{1,0:T(1,128)S(1)} %bitcast.41, bf16[64,64]{1,0:T(8,128)(2,1)S(1)} %bitcast.38, bf16[1024,128]{1,0:T(8,128)(2,1)S(1)} %bitcast.32, ...), custom_call_target="tpu_custom_call" | custom-call | tf_op jit(solution)/shard_map/pair/pallas_call | solution.py:728
  114.3 0.8 copy.22
Async XLA Ops:
  0.6 40.1 %copy-start.7 = (bf16[8,8,64]{2,1,0:T(8,128)(2,1)S(1)}, bf16[8,8,64]{2,1,0:T(8,128)(2,1)}, u32[]{:S(2)}) copy-start(bf16[8,8,64]{2,1,0:T(8,128)(2,1)} %param.29) | copy-start | bytes 24580
  40.8 2.2 %copy-start = (bf16[16,128,128]{2,1,0:T(8,128)(2,1)S(1)}, bf16[16,128,128]{2,1,0:T(8,128)(2,1)}, u32[]{:S(2)}) copy-start(bf16[16,128,128]{2,1,0:T(8,128)(2,1)} %z_ref.1) | copy-start | bytes 1572868
  40.8 2.2 %copy-start.1 = (s32[768,128]{1,0:T(8,128)S(1)}, s32[768,128]{1,0:T(8,128)}, u32[]{:S(2)}) copy-start(s32[768,128]{1,0:T(8,128)} %mask_ref.1) | copy-start | bytes 1179652
  40.8 2.2 %copy-start.2 = (bf16[32,32,128]{2,1,0:T(8,128)(2,1)S(1)}, bf16[32,32,128]{2,1,0:T(8,128)(2,1)}, u32[]{:S(2)}) copy-start(bf16[32,32,128]{2,1,0:T(8,128)(2,1)} %param.31) | copy-start | bytes 786436
  40.8 2.2 %copy-start.3 = (bf16[128,4,4,32]{0,3,2,1:T(8,128)(2,1)S(1)}, bf16[128,4,4,32]{0,3,2,1:T(8,128)(2,1)}, u32[]{:S(2)}) copy-start(bf16[128,4,4,32]{0,3,2,1:T(8,128)(2,1)} %param.33) | copy-start | bytes 393220
  40.8 2.2 %copy-start.4 = (bf16[128,4,4,32]{0,3,2,1:T(8,128)(2,1)S(1)}, bf16[128,4,4,32]{0,3,2,1:T(8,128)(2,1)}, u32[]{:S(2)}) copy-start(bf16[128,4,4,32]{0,3,2,1:T(8,128)(2,1)} %param.36) | copy-start | bytes 393220
  40.8 2.2 %copy-start.5 = (bf16[4,32,128]{2,1,0:T(8,128)(2,1)S(1)}, bf16[4,32,128]{2,1,0:T(8,128)(2,1)}, u32[]{:S(2)}) copy-start(bf16[4,32,128]{2,1,0:T(8,128)(2,1)} %param.34) | copy-start | bytes 98308
  40.8 2.2 %copy-start.6 = (bf16[4,32,128]{2,1,0:T(8,128)(2,1)S(1)}, bf16[4,32,128]{2,1,0:T(8,128)(2,1)}, u32[]{:S(2)}) copy-start(bf16[4,32,128]{2,1,0:T(8,128)(2,1)} %param.37) | copy-start | bytes 98308
  40.8 2.2 %copy-start.8 = (bf16[64,2,32]{0,2,1:T(8,128)(2,1)S(1)}, bf16[64,2,32]{0,2,1:T(8,128)(2,1)}, u32[]{:S(2)}) copy-start(bf16[64,2,32]{0,2,1:T(8,128)(2,1)} %param.30) | copy-start | bytes 24580
  40.8 2.1 %copy-start.9 = (bf16[128,4]{0,1:T(4,128)(2,1)S(1)}, bf16[128,4]{0,1:T(4,128)(2,1)}, u32[]{:S(2)}) copy-start(bf16[128,4]{0,1:T(4,128)(2,1)} %param.32) | copy-start | bytes 3076
  40.9 2.1 %copy-start.10 = (bf16[128,4]{0,1:T(4,128)(2,1)S(1)}, bf16[128,4]{0,1:T(4,128)(2,1)}, u32[]{:S(2)}) copy-start(bf16[128,4]{0,1:T(4,128)(2,1)} %param.35) | copy-start | bytes 3076
  40.9 2.1 %copy-start.11 = (s32[128]{0:T(128)S(1)}, s32[128]{0:T(128)}, u32[]{:S(2)}) copy-start(s32[128]{0:T(128)} %param.22) | copy-start | bytes 1540

commit v7 on v6

--- a/solution.py
+++ b/solution.py
@@ -281,7 +281,7 @@
             if u > 0:
                 pv(t, u - 1)
         pv(t, units - 1)
-    loop(npair, row_pair, 2)
+    loop(npair, row_pair, 4)
 
     def finish(t):
         s0 = t * 2
@@ -324,7 +324,7 @@
         tot = tot + qpart[d]
     tmp[:] = rnd(dot(wq2_ref[:], (tot / count).astype(BF)))
     qd = [tmp[pl.ds(d, heads, stride=hd), :] for d in range(hd)]
-    unroll = 8
+    unroll = 16
 
     def logit(t, mx):
         for u in range(unroll):
@@ -711,7 +711,7 @@
     nseq = 2 * x.shape[0]
     ne = wproj.shape[0] // 2
     heads = wb1.shape[0]
-    sizes = (8, 8, 8, 4, 4)
+    sizes = (8, 8, 4, 4, 4, 4)
     dma = pltpu.SemaphoreType.DMA((n,))
     dma9 = pltpu.SemaphoreType.DMA((9,))
     dmac = pltpu.SemaphoreType.DMA((len(sizes), 9))

time: 115 us -> 115 us (level)
  no operation moved by 1% of the time
where the time goes in v7:
time: 115 us
  Pallas kernels  113 us (98%)
    pallas_call x1, Pallas kernels, pair_call(): pl.pallas_call(functools.partial(pair_kernel, n, sizes), name='pair', out...  71.4 us
    pallas_call x1, Pallas kernels, msa_call(): pl.pallas_call(functools.partial(msa_kernel, n, len(args)), name='msa', o...  39.4 us

profile of v7, /device:TPU:81, one launch (start us, length us, event | category | flops | bytes accessed | tf_op | source)
XLA Modules:
  0.0 114.5 jit_solution(10770600948524271499)
XLA Ops:
  0.6 0.0 copy-start.7
  0.6 39.4 %msa.1 = (bf16[96,64,128]{2,1,0:T(8,128)(2,1)S(1)}, f32[48,64,256]{2,1,0:T(8,128)S(1)}, f32[64,128]{1,0:T(8,128)S(1)}) custom-call(bf16[16,128,128]{2,1,0:T(8,128)(2,1)} %z_ref.1, bf16[8,128]{1,0:T(8,128)(2,1)} %bitcast.48, s32[768,128]{1,0:T(8,128)} %mask_ref.1, bf16[96,64,128]{2,1,0:T(8,128)(2,1)} %bitcast.42, bf16[256,64]{1,0:T(8,128)(2,1)} %bitcast.43, ...), custom_call_target="tpu_custom_call" | custom-call | tf_op jit(solution)/shard_map/msa/pallas_call | solution.py:389
  40.0 0.0 copy-done.7
  40.0 0.0 copy-start
  40.1 0.0 copy-start.1
  40.1 0.0 copy-start.2
  40.1 0.0 copy-start.3
  40.1 0.0 copy-start.4
  40.1 0.0 copy-start.5
  40.1 0.0 copy-start.6
  40.1 0.0 copy-start.8
  40.1 0.0 copy-start.9
  40.2 0.0 copy-start.10
  40.2 0.0 copy-start.11
  40.2 2.0 %gate.1 = (bf16[96,64,128]{2,1,0:T(8,128)(2,1)}, bf16[48,64,256]{2,1,0:T(8,128)(2,1)S(1)}) custom-call(bf16[96,64,128]{2,1,0:T(8,128)(2,1)S(1)} %get-tuple-element.7.m1_ref, f32[48,64,256]{2,1,0:T(8,128)S(1)} %get-tuple-element.8.g2_ref, f32[64,128]{1,0:T(8,128)S(1)} %get-tuple-element.9.o2_ref, bf16[64,64]{1,0:T(8,128)(2,1)S(1)} %bitcast.37), custom_call_target="tpu_custom_call" | custom-call | tf_op jit(solution)/shard_map/gate/pallas_call | solution.py:451
  42.2 0.0 copy-done
  42.2 0.0 copy-done.1
  42.2 0.0 copy-done.2
  42.2 0.0 copy-done.3
  42.3 0.0 copy-done.4
  42.3 0.0 copy-done.5
  42.3 0.0 copy-done.6
  42.3 0.0 copy-done.8
  42.3 0.0 copy-done.9
  42.3 0.0 copy-done.10
  42.3 0.0 copy-done.11
  42.3 71.4 %pair.1 = bf16[16,128,128]{2,1,0:T(8,128)(2,1)S(1)} custom-call(s32[768,128]{1,0:T(8,128)S(1)} %copy-done.1, bf16[48,64,256]{2,1,0:T(8,128)(2,1)S(1)} %get-tuple-element.11.x_ref, bf16[16,128,128]{2,1,0:T(8,128)(2,1)S(1)} %copy-done, s32[1,128]{1,0:T(1,128)S(1)} %bitcast.41, bf16[64,64]{1,0:T(8,128)(2,1)S(1)} %bitcast.38, bf16[1024,128]{1,0:T(8,128)(2,1)S(1)} %bitcast.32, ...), custom_call_target="tpu_custom_call" | custom-call | tf_op jit(solution)/shard_map/pair/pallas_call | solution.py:728
  113.7 0.8 copy.22
Async XLA Ops:
  0.6 39.4 %copy-start.7 = (bf16[8,8,64]{2,1,0:T(8,128)(2,1)S(1)}, bf16[8,8,64]{2,1,0:T(8,128)(2,1)}, u32[]{:S(2)}) copy-start(bf16[8,8,64]{2,1,0:T(8,128)(2,1)} %param.29) | copy-start | bytes 24580
  40.0 2.2 %copy-start = (bf16[16,128,128]{2,1,0:T(8,128)(2,1)S(1)}, bf16[16,128,128]{2,1,0:T(8,128)(2,1)}, u32[]{:S(2)}) copy-start(bf16[16,128,128]{2,1,0:T(8,128)(2,1)} %z_ref.1) | copy-start | bytes 1572868
  40.1 2.2 %copy-start.1 = (s32[768,128]{1,0:T(8,128)S(1)}, s32[768,128]{1,0:T(8,128)}, u32[]{:S(2)}) copy-start(s32[768,128]{1,0:T(8,128)} %mask_ref.1) | copy-start | bytes 1179652
  40.1 2.2 %copy-start.2 = (bf16[32,32,128]{2,1,0:T(8,128)(2,1)S(1)}, bf16[32,32,128]{2,1,0:T(8,128)(2,1)}, u32[]{:S(2)}) copy-start(bf16[32,32,128]{2,1,0:T(8,128)(2,1)} %param.31) | copy-start | bytes 786436
  40.1 2.2 %copy-start.3 = (bf16[128,4,4,32]{0,3,2,1:T(8,128)(2,1)S(1)}, bf16[128,4,4,32]{0,3,2,1:T(8,128)(2,1)}, u32[]{:S(2)}) copy-start(bf16[128,4,4,32]{0,3,2,1:T(8,128)(2,1)} %param.33) | copy-start | bytes 393220
  40.1 2.2 %copy-start.4 = (bf16[128,4,4,32]{0,3,2,1:T(8,128)(2,1)S(1)}, bf16[128,4,4,32]{0,3,2,1:T(8,128)(2,1)}, u32[]{:S(2)}) copy-start(bf16[128,4,4,32]{0,3,2,1:T(8,128)(2,1)} %param.36) | copy-start | bytes 393220
  40.1 2.2 %copy-start.5 = (bf16[4,32,128]{2,1,0:T(8,128)(2,1)S(1)}, bf16[4,32,128]{2,1,0:T(8,128)(2,1)}, u32[]{:S(2)}) copy-start(bf16[4,32,128]{2,1,0:T(8,128)(2,1)} %param.34) | copy-start | bytes 98308
  40.1 2.2 %copy-start.6 = (bf16[4,32,128]{2,1,0:T(8,128)(2,1)S(1)}, bf16[4,32,128]{2,1,0:T(8,128)(2,1)}, u32[]{:S(2)}) copy-start(bf16[4,32,128]{2,1,0:T(8,128)(2,1)} %param.37) | copy-start | bytes 98308
  40.1 2.2 %copy-start.8 = (bf16[64,2,32]{0,2,1:T(8,128)(2,1)S(1)}, bf16[64,2,32]{0,2,1:T(8,128)(2,1)}, u32[]{:S(2)}) copy-start(bf16[64,2,32]{0,2,1:T(8,128)(2,1)} %param.30) | copy-start | bytes 24580
  40.1 2.2 %copy-start.9 = (bf16[128,4]{0,1:T(4,128)(2,1)S(1)}, bf16[128,4]{0,1:T(4,128)(2,1)}, u32[]{:S(2)}) copy-start(bf16[128,4]{0,1:T(4,128)(2,1)} %param.32) | copy-start | bytes 3076
  40.2 2.1 %copy-start.10 = (bf16[128,4]{0,1:T(4,128)(2,1)S(1)}, bf16[128,4]{0,1:T(4,128)(2,1)}, u32[]{:S(2)}) copy-start(bf16[128,4]{0,1:T(4,128)(2,1)} %param.35) | copy-start | bytes 3076
  40.2 2.1 %copy-start.11 = (s32[128]{0:T(128)S(1)}, s32[128]{0:T(128)}, u32[]{:S(2)}) copy-start(s32[128]{0:T(128)} %param.22) | copy-start | bytes 1540
